TPU v7x, 256 devices: a 4x2x16 block of a 4x16x16 slice. The times are simulated.
256 devices in a mesh: groups: 2 (over y), shard: 128 (over z, x, core).
Axes of the slice: x: 4, y: 2, z: 16, core: 2. Of those that a mesh axis runs over, the one named last changes fastest.
The devices are a block of a 4x16x16 slice.
Arguments:
- query_tokens: bfloat16 [8192, 32, 128], P(('groups', 'shard')), parts along dimension 0, may hold values from -0.1875 to 0.1875
- candidates: int32 [8192, 24], P(('groups', 'shard')), parts along dimension 0, may hold values from 0 to 4095, as said below
- cand_count: int32 [8192], P(('groups', 'shard')), parts along dimension 0, may hold values from 3 to 24, as said below
- placement_map: int32 [8192], P('groups'), parts along dimension 0, may hold values from 0 to 4095, as said below
- passage_base: bfloat16 [8192, 128, 128], P(('groups', 'shard')), parts along dimension 0, may hold values from -6 to 6
- residual_codes: int32 [8192, 128, 128], P(('groups', 'shard')), parts along dimension 0, may hold values from 0 to 3
- passage_lengths: int32 [8192], P(('groups', 'shard')), parts along dimension 0, may hold values from 32 to 128
- bucket_weights: float32 [8], P('groups'), parts along dimension 0, may hold values from -3 to 3
Outputs:
- scores: float32 [8192, 24], P(('groups', 'shard')), parts along dimension 0
There are 2 independent parts, one for each index of `groups`. A program takes and returns all parts, laid end to end along the dimension named above; each array names one. Nothing has to cross between parts.
Inputs may be any that keep to these rules, and one draw needn't show every extreme that they name: In row q the first cand_count[q] entries are distinct passage ids; the devices that store them (device placement_map[id] // 32 of the shard axis) are at most 3, and one device stores at most 8 of them. Of the 32 queries of one device, one storing device (the same for all devices) holds candidates of exactly 3, and every other storing device holds candidates of at most 1. Entries at or beyond cand_count[q] are arbitrary ids. `cand_count`: entries of candidates at or beyond this count are not scored. A permutation: passage id p is row placement_map[p] of the passage store.
All inputs are finite; a program needn't handle non-finite values.
Results may differ from a plain program's by a relative error of at most 0.0003.
Values may be sent and summed in bfloat16 or wider, within the bound.
No kernel may reach another device: no remote copies, remote signals or barrier semaphores. Data moves between devices by JAX's collectives and lax.ppermute only.
A program may use at most 64 MiB of HBM per device.

v0:
```python
import jax
import jax.numpy as jnp
from jax import lax
from jax.sharding import PartitionSpec as P

OWNERS_Q = 3
CPQ = 8


epsilon = 1e-06
negative = -1e30


def decode(bases, code_ids, levels):
    residual = jnp.zeros(bases.shape, jnp.float32)
    for bucket in range(4):
        residual = residual + jnp.where(code_ids == bucket, levels[bucket], 0.0)
    summed = bases.astype(jnp.float32) + residual
    inverse_norm = lax.rsqrt(jnp.sum(summed * summed, axis=-1, keepdims=True) + epsilon)
    return (summed * inverse_norm).astype(jnp.bfloat16)


def score_block(query_rows, token_rows, lengths):
    similarity_scores = jnp.einsum(
        "mqd,mkpd->mqkp", query_rows, token_rows, preferred_element_type=jnp.float32
    )
    inside = (
        jnp.arange(token_rows.shape[2], dtype=jnp.int32)[None, None, None, :]
        < lengths[:, None, :, None]
    )
    maxima = jnp.max(jnp.where(inside, similarity_scores, negative), axis=3)
    return jnp.sum(maxima, axis=1)


def score_slots(query_rows, wanted, decoded, lengths):
    item_count = query_rows.shape[0]
    group_size = 16
    padding = -item_count % group_size
    wanted = jnp.maximum(wanted, 0)
    blocks = (item_count + padding) // group_size

    def one_block(bundle):
        query_part, row_part = bundle
        return score_block(query_part, decoded[row_part], lengths[row_part])

    result = lax.map(
        one_block,
        (
            query_rows.reshape(blocks, group_size, query_rows.shape[1], query_rows.shape[2]),
            wanted.reshape(blocks, group_size, wanted.shape[1]),
        ),
    )
    return result.reshape(blocks * group_size, wanted.shape[1])


def pack(present, holder, capacity, query_tokens):
    present_int = present.astype(jnp.int32)
    slot_of = jnp.cumsum(present_int, axis=0) - present_int
    selection_mask = present.T[:, None, :] & (
        slot_of.T[:, None, :] == jnp.arange(capacity, dtype=jnp.int32)[None, :, None]
    )
    outgoing = jnp.einsum(
        "ksq,qtd->kstd",
        selection_mask.astype(jnp.bfloat16),
        query_tokens,
        preferred_element_type=jnp.float32,
    ).astype(jnp.bfloat16)
    target = (
        jnp.sum(
            selection_mask[:, :, :, None].astype(jnp.int32)
            * (jnp.transpose(holder, (1, 0, 2))[:, None, :, :] + 1),
            axis=2,
        )
        - 1
    )
    return (outgoing, target, slot_of)


def local(
    query_tokens,
    candidates,
    cand_count,
    placement_map,
    passage_base,
    residual_codes,
    passage_lengths,
    bucket_weights,
):
    device_count = lax.axis_size("shard")
    query_count, slot_count = candidates.shape
    store_rows = passage_base.shape[0]
    hot_cap = query_count * OWNERS_Q // device_count + 3
    decoded = decode(passage_base, residual_codes, bucket_weights)
    usable = jnp.arange(slot_count, dtype=jnp.int32)[None, :] < cand_count[:, None]
    stored = placement_map[candidates]
    holders = stored // store_rows
    local_row = stored % store_rows
    shared = usable[:, :, None] & usable[:, None, :] & (holders[:, :, None] == holders[:, None, :])
    preceding_total = (
        jnp.arange(slot_count, dtype=jnp.int32)[None, :]
        < jnp.arange(slot_count, dtype=jnp.int32)[:, None]
    )
    within = jnp.sum((shared & preceding_total[None, :, :]).astype(jnp.int32), axis=2)
    owner_ids = jnp.arange(device_count, dtype=jnp.int32)
    matches = usable[:, :, None] & (holders[:, :, None] == owner_ids[None, None, :])
    present = jnp.any(matches, axis=1)
    rank_ids = jnp.arange(CPQ, dtype=jnp.int32)
    holder = (
        jnp.sum(
            jnp.where(
                matches[:, :, :, None]
                & (within[:, :, None, None] == rank_ids[None, None, None, :]),
                local_row[:, :, None, None] + 1,
                0,
            ),
            axis=1,
        )
        - 1
    )
    outgoing, target, slot_of = pack(present, holder, hot_cap, query_tokens)
    queries_in = lax.all_to_all(outgoing, "shard", split_axis=0, concat_axis=0, tiled=True)
    rows_in = lax.all_to_all(
        target.astype(jnp.bfloat16), "shard", split_axis=0, concat_axis=0, tiled=True
    )
    senders = rows_in.shape[0]
    slots_in = rows_in.shape[1]
    flat_queries = queries_in.reshape(senders * slots_in, queries_in.shape[2], queries_in.shape[3])
    row_list_flat = rows_in.astype(jnp.int32).reshape(senders * slots_in, rows_in.shape[2])
    visited = score_slots(flat_queries, row_list_flat, decoded, passage_lengths).reshape(
        senders, slots_in, rows_in.shape[2]
    )
    returned = lax.all_to_all(visited, "shard", split_axis=0, concat_axis=0, tiled=True)
    flattened = returned.reshape(-1)
    pick_slot = jnp.take_along_axis(slot_of, jnp.clip(holders, 0, device_count - 1), axis=1)
    position = holders * (hot_cap * CPQ) + pick_slot * CPQ + within
    result = jnp.take(flattened, position, mode="clip")
    return jnp.where(usable, result, 0.0)


def solution(mesh):
    return jax.shard_map(
        local,
        mesh=mesh,
        in_specs=(
            P(("groups", "shard"), None, None),
            P(("groups", "shard"), None),
            P(("groups", "shard")),
            P("groups"),
            P(("groups", "shard"), None, None),
            P(("groups", "shard"), None, None),
            P(("groups", "shard")),
            P("groups"),
        ),
        out_specs=P(("groups", "shard"), None),
        check_vma=False,
    )
```

profile of v0, /device:TPU:33, one launch (start us, length us, event | category | flops | bytes accessed | tf_op | source)
XLA Modules:
  0.0 453.0 jit_solution(4618229472252225203)
XLA Ops:
  1.8 4.5 gather_fusion.2
  10.3 31.0 %all-to-all-start = ((bf16[128,3,8]{2,1,0:T(4,128)(2,1)}), bf16[128,3,8]{2,1,0:T(4,128)(2,1)S(1)}, u32[]{:S(2)}, u32[]{:S(2)}) async-start(bf16[128,3,8]{2,1,0:T(4,128)(2,1)} %copy.83), calls=%async_computation | async-start | bytes 262144 | tf_op jit(solution)/shard_map/all_to_all | solution.py:122
  46.1 11.1 %all-to-all-done = bf16[128,3,8]{2,1,0:T(4,128)(2,1)S(1)} async-done(((bf16[128,3,8]{2,1,0:T(4,128)(2,1)}), bf16[128,3,8]{2,1,0:T(4,128)(2,1)S(1)}, u32[]{:S(2)}, u32[]{:S(2)}) %all-to-all-start) | async-done | bytes 6176 | tf_op jit(solution)/shard_map/all_to_all | solution.py:122
  57.1 8.4 %all-to-all-start.1 = ((bf16[128,3,32,128]{3,2,1,0:T(8,128)(2,1)}), bf16[128,3,32,128]{3,2,1,0:T(8,128)(2,1)}, u32[]{:S(2)}, u32[]{:S(2)}) async-start(bf16[128,3,32,128]{3,2,1,0:T(8,128)(2,1)} %copy.85), calls=%async_computation.1 | async-start | bytes 6291456 | tf_op jit(solution)/shard_map/all_to_all | solution.py:121
  65.9 5.0 %gather_fusion.4 = s32[768]{0:T(1024)S(1)} fusion(s32[32,128]{1,0:T(8,128)S(1)} %convert_subtract_fusion, s32[768]{0:T(1024)S(1)} %reshape.292), kind=kCustom, calls=%fused_computation.4 | custom fusion | bytes 12288 | tf_op jit(solution)/shard_map/jit(take_along_axis)/gather | solution.py:134
  71.9 4.8 %multiply_reduce_fusion = f32[32,128]{1,0:T(8,128)S(1)} fusion(f32[]{:T(128)} %bitcast.16, s32[32,128,128]{2,1,0:T(8,128)S(1)} %copy-done.2, f32[]{:T(128)} %bitcast.15, f32[]{:T(128)} %bitcast.14, f32[]{:T(128)} %bitcast.13, bf16[32,128,128]{2,1,0:T(8,128)(2,1)} %param.14), kind=kLoop, calls=%fused_computation.16 | loop fusion | flops 7860224 | bytes 3162128 | tf_op jit(solution)/shard_map/reduce_sum | solution.py:19
  76.7 4.5 %multiply_convert_fusion = bf16[32,128,128]{2,1,0:T(8,128)(2,1)S(1)} fusion(f32[32,128]{1,0:T(8,128)S(1)} %add_rsqrt_fusion, f32[]{:T(128)} %bitcast.16, s32[32,128,128]{2,1,0:T(8,128)S(1)} %copy-done.2, f32[]{:T(128)} %bitcast.15, f32[]{:T(128)} %bitcast.14, f32[]{:T(128)} %bitcast.13, bf16[32,128,128]{2,1,0:T(8,128)(2,1)} %param.14), kind=kLoop, calls=%fused_computation.15 | loop fusion | flops 7864320 | bytes 4210704 | tf_op jit(solution)/shard_map/convert_element_type | solution.py:20
  81.6 123.9 %all-to-all-done.1 = bf16[128,3,32,128]{3,2,1,0:T(8,128)(2,1)} async-done(((bf16[128,3,32,128]{3,2,1,0:T(8,128)(2,1)}), bf16[128,3,32,128]{3,2,1,0:T(8,128)(2,1)}, u32[]{:S(2)}, u32[]{:S(2)}) %all-to-all-start.1) | async-done | bytes 3145760 | tf_op jit(solution)/shard_map/all_to_all | solution.py:121
  205.5 208.4 %while.10 = (s32[]{:T(128)}, f32[24,16,8]{1,2,0:T(8,128)S(1)}, s32[24,16,8]{1,2,0:T(8,128)S(1)}, s32[32]{0:T(128)S(1)}, bf16[24,16,32,128]{3,2,1,0:T(8,128)(2,1)...) while((s32[]{:T(128)}, f32[24,16,8]{1,2,0:T(8,128)S(1)}, s32[24,16,8]{1,2,0:T(8,128)S(1)}, ...), condition=%wide.region_9.10_spmd, body=%wide.region_6.9_spmd.sunk | while | flops 135283968 | bytes 12800621 | solution.py:46
  210.1 3.9 select_reduce_fusion.3
  218.8 3.9 select_reduce_fusion.3
  227.5 3.9 select_reduce_fusion.3
  236.2 3.9 select_reduce_fusion.3
  244.8 3.9 select_reduce_fusion.3
  253.5 3.9 select_reduce_fusion.3
  262.2 3.9 select_reduce_fusion.3
  270.9 3.9 select_reduce_fusion.3
  279.6 3.9 select_reduce_fusion.3
  288.3 3.9 select_reduce_fusion.3
  296.9 3.9 select_reduce_fusion.3
  305.6 3.9 select_reduce_fusion.3
  314.3 3.9 select_reduce_fusion.3
  323.0 3.9 select_reduce_fusion.3
  331.7 3.9 select_reduce_fusion.3
  340.4 3.9 select_reduce_fusion.3
  349.0 3.9 select_reduce_fusion.3
  357.7 3.9 select_reduce_fusion.3
  366.4 3.9 select_reduce_fusion.3
  392.4 3.9 select_reduce_fusion.3
  414.8 12.9 %all-to-all-start.2 = ((f32[128,3,8]{2,1,0:T(4,128)}), f32[128,3,8]{2,1,0:T(4,128)S(1)}, u32[]{:S(2)}, u32[]{:S(2)}) async-start(f32[128,3,8]{2,1,0:T(4,128)} %reshape_reshape.7), calls=%async_computation.2 | async-start | bytes 524288 | tf_op jit(solution)/shard_map/all_to_all | solution.py:132
  427.7 19.8 %all-to-all-done.2 = f32[128,3,8]{2,1,0:T(4,128)S(1)} async-done(((f32[128,3,8]{2,1,0:T(4,128)}), f32[128,3,8]{2,1,0:T(4,128)S(1)}, u32[]{:S(2)}, u32[]{:S(2)}) %all-to-all-start.2) | async-done | bytes 12320 | tf_op jit(solution)/shard_map/all_to_all | solution.py:132
  447.7 4.5 gather_fusion.3
  (328 shorter events, 143.5 us)
Async XLA Ops:
  0.0 1.7 copy-start
  1.7 39.6 %copy-start.3 = (bf16[32,32,128]{2,1,0:T(8,128)(2,1)S(1)}, bf16[32,32,128]{2,1,0:T(8,128)(2,1)}, u32[]{:S(2)}) copy-start(bf16[32,32,128]{2,1,0:T(8,128)(2,1)} %param.10) | copy-start | bytes 786436
  10.3 46.8 %all-to-all-start = ((bf16[128,3,8]{2,1,0:T(4,128)(2,1)}), bf16[128,3,8]{2,1,0:T(4,128)(2,1)S(1)}, u32[]{:S(2)}, u32[]{:S(2)}) async-start(bf16[128,3,8]{2,1,0:T(4,128)(2,1)} %copy.83), calls=%async_computation | async-start | bytes 262144 | tf_op jit(solution)/shard_map/all_to_all | solution.py:122
  57.1 148.4 %all-to-all-start.1 = ((bf16[128,3,32,128]{3,2,1,0:T(8,128)(2,1)}), bf16[128,3,32,128]{3,2,1,0:T(8,128)(2,1)}, u32[]{:S(2)}, u32[]{:S(2)}) async-start(bf16[128,3,32,128]{3,2,1,0:T(8,128)(2,1)} %copy.85), calls=%async_computation.1 | async-start | bytes 6291456 | tf_op jit(solution)/shard_map/all_to_all | solution.py:121
  65.9 5.3 %copy-start.4 = (f32[4]{0:T(128)S(1)}, f32[4]{0:T(128)}, u32[]{:S(2)}) copy-start(f32[4]{0:T(128)} %param.17) | copy-start | bytes 52
  65.9 6.0 %copy-start.2 = (s32[32,128,128]{2,1,0:T(8,128)S(1)}, s32[32,128,128]{2,1,0:T(8,128)}, u32[]{:S(2)}) copy-start(s32[32,128,128]{2,1,0:T(8,128)} %param.15) | copy-start | bytes 6291460
  76.7 128.8 %copy-start.1 = (s32[32]{0:T(128)S(1)}, s32[32]{0:T(128)}, u32[]{:S(2)}) copy-start(s32[32]{0:T(128)} %param.16) | copy-start | bytes 388
  414.8 32.7 %all-to-all-start.2 = ((f32[128,3,8]{2,1,0:T(4,128)}), f32[128,3,8]{2,1,0:T(4,128)S(1)}, u32[]{:S(2)}, u32[]{:S(2)}) async-start(f32[128,3,8]{2,1,0:T(4,128)} %reshape_reshape.7), calls=%async_computation.2 | async-start | bytes 524288 | tf_op jit(solution)/shard_map/all_to_all | solution.py:132
  447.7 4.6 %copy-start.5 = (s32[32]{0:T(128)S(1)}, s32[32]{0:T(128)}, u32[]{:S(2)}) copy-start(s32[32]{0:T(128)} %param.12) | copy-start | bytes 388
where the time goes:
time: 454 us; the launch traced here: 453 us
  waiting for transfers between devices  155 us (34%)
  local copies, waits for them, and re-layouts  132 us (29%)
  matrix products  94.4 us (21%)
  starting transfers between devices  52.3 us (12%)
  other arithmetic  17.9 us (4%)
    all_to_all x1, waiting for transfers between devices, local(): lax.all_to_all(outgoing, 'shard', split_axis=0, concat_axis=0, tiled=True)  124 us
    gather x72, local copies, waits for them, and re-layouts, one_block(): return score_block(query_part, decoded[row_part], lengths[row_part])  104 us
    dot_general x24, matrix products, score_block(): jnp.einsum('mqd,mkpd->mqkp', query_rows, token_rows, preferred_element_ty...  93.4 us
    all_to_all x1, starting transfers between devices, local(): lax.all_to_all(target.astype(jnp.bfloat16), 'shard', split_axis=0, concat...  31 us
    all_to_all x1, waiting for transfers between devices, local(): lax.all_to_all(visited, 'shard', split_axis=0, concat_axis=0, tiled=True)  19.8 us
    all_to_all x1, starting transfers between devices, local(): lax.all_to_all(visited, 'shard', split_axis=0, concat_axis=0, tiled=True)  12.9 us
    all_to_all x1, waiting for transfers between devices, local(): lax.all_to_all(target.astype(jnp.bfloat16), 'shard', split_axis=0, concat...  11.1 us
  transfers between devices with their start and end apart: 3, of which 3 were waited for; matrix products, arithmetic and copies ran while one was open for 5% of the time, Pallas kernels for 0%

commit v1 on v0

v1 whole, which is shorter than its diff:
```python
import functools

import jax
import jax.numpy as jnp
from jax import lax
from jax.experimental import pallas as pl
from jax.experimental.pallas import tpu as pltpu
from jax.sharding import PartitionSpec as P

EPSILON = 1e-06
PLANE = 8
F32 = jnp.float32
BF16 = jnp.bfloat16


def vmem(*_):
    return pl.BlockSpec(memory_space=pltpu.VMEM)


def smem(*_):
    return pl.BlockSpec(memory_space=pltpu.SMEM)


def cost(flops, moved):
    return pl.CostEstimate(flops=flops, transcendentals=0, bytes_accessed=moved)


def columns(parts, width):
    lane = lax.broadcasted_iota(jnp.int32, (parts[0].shape[0], width), 1)
    out = jnp.zeros((parts[0].shape[0], width), F32)
    for index, part in enumerate(parts):
        out = jnp.where(lane == index, part, out)
    return out


def prepare_kernel(
    store_rows, device_count,
    cand_ref, count_ref, map_ref, query_ref,
    out_ref, holder_ref, row_ref, busiest_ref,
    pick_vmem, pick_smem, sem,
):
    queries, slots = cand_ref.shape
    table_rows, lanes = map_ref.shape
    table = map_ref[...]
    holder_table = table // store_rows
    row_table = table - holder_table * store_rows
    both = jnp.concatenate([holder_table, row_table], axis=1).astype(F32).astype(BF16)
    ids = cand_ref[...]
    high = ids // lanes
    low = ids - high * lanes
    table_iota = lax.broadcasted_iota(jnp.int32, (queries, table_rows), 1)
    lane_iota = lax.broadcasted_iota(jnp.int32, (queries, lanes), 1)
    device_iota = lax.broadcasted_iota(jnp.int32, (queries, device_count), 1)
    marks = [
        jnp.where(table_iota == high[:, c : c + 1], 1.0, 0.0) for c in range(slots)
    ]
    rows = jnp.dot(
        jnp.concatenate(marks, axis=0).astype(BF16), both, preferred_element_type=F32
    )
    present = jnp.zeros((queries, device_count), F32)
    holders, local_rows = [], []
    for c in range(slots):
        block = rows[c * queries : (c + 1) * queries]
        here = lane_iota == low[:, c : c + 1]
        holder = jnp.sum(jnp.where(here, block[:, :lanes], 0.0), axis=1, keepdims=True)
        row = jnp.sum(jnp.where(here, block[:, lanes:], 0.0), axis=1, keepdims=True)
        holder = jnp.where(count_ref[...] > c, holder, -1.0)
        present = jnp.where(device_iota == holder.astype(jnp.int32), 1.0, present)
        holders.append(holder)
        local_rows.append(row)
    holder_ref[...] = columns(holders, slots)
    row_ref[...] = columns(local_rows, slots)
    query_iota = lax.broadcasted_iota(jnp.int32, (queries, device_count), 0).astype(F32)
    pick = jnp.max(present * query_iota, axis=0, keepdims=True)
    pick_vmem[...] = jnp.broadcast_to(pick.astype(jnp.int32), pick_vmem.shape)
    copy = pltpu.make_async_copy(pick_vmem, pick_smem, sem)
    copy.start()
    shared = jnp.sum(present, axis=0, keepdims=True)
    device = lax.broadcasted_iota(jnp.int32, (1, device_count), 1).astype(F32)
    busiest_ref[0] = jnp.max(jnp.where(shared > 1.5, device, 0.0)).astype(jnp.int32)
    copy.wait()

    def pack(step, carry):
        for inner in range(8):
            device = step * 8 + inner
            out_ref[device] = query_ref[pick_smem[0, device]]
        return carry

    lax.fori_loop(0, device_count // 8, pack, 0)


def prepare(candidates, cand_count, placement_map, query_tokens, store_rows, device_count):
    queries, slots = candidates.shape
    _, tokens, dim = query_tokens.shape
    return pl.pallas_call(
        functools.partial(prepare_kernel, store_rows, device_count),
        name="prepare",
        out_shape=(
            jax.ShapeDtypeStruct((device_count, tokens, dim), BF16),
            jax.ShapeDtypeStruct((queries, slots), F32),
            jax.ShapeDtypeStruct((queries, slots), F32),
            jax.ShapeDtypeStruct((1,), jnp.int32),
        ),
        in_specs=[vmem(), vmem(), vmem(), vmem()],
        out_specs=(vmem(), vmem(), vmem(), smem()),
        scratch_shapes=[
            pltpu.VMEM((8, device_count), jnp.int32),
            pltpu.SMEM((8, device_count), jnp.int32),
            pltpu.SemaphoreType.DMA(()),
        ],
    )(
        candidates,
        cand_count.reshape(queries, 1),
        placement_map.reshape(-1, 128),
        query_tokens,
    )


def decode_kernel(length_ref, level_ref, base_ref, code_ref, out_ref):
    step = pl.program_id(0)
    block, length, dim = base_ref.shape
    token = lax.broadcasted_iota(jnp.int32, (length, dim), 0)
    for index in range(block):
        code = code_ref[index]
        residual = jnp.where(
            code < 2,
            jnp.where(code == 0, level_ref[0], level_ref[1]),
            jnp.where(code == 2, level_ref[2], level_ref[3]),
        )
        summed = base_ref[index].astype(F32) + residual
        inverse = lax.rsqrt(jnp.sum(summed * summed, axis=1, keepdims=True) + EPSILON)
        tokens = summed * inverse
        tokens = jnp.where(token < length_ref[step * block + index], tokens, tokens[0:1])
        out_ref[index] = tokens.astype(BF16)


def decode(passage_base, residual_codes, passage_lengths, bucket_weights):
    rows, length, dim = passage_base.shape
    block = 8
    spec = pl.BlockSpec((block, length, dim), lambda i: (i, 0, 0))
    return pl.pallas_call(
        decode_kernel,
        name="decode",
        grid=(rows // block,),
        out_shape=jax.ShapeDtypeStruct(passage_base.shape, BF16),
        in_specs=[smem(), smem(), spec, spec],
        out_specs=spec,
        cost_estimate=cost(rows * length * dim * 20, rows * length * dim * 8),
    )(passage_lengths, bucket_weights, passage_base, residual_codes)


def score_kernel(query_ref, store_ref, out_ref, best_ref):
    group, tokens, dim = query_ref.shape
    rows, length, _ = store_ref.shape
    wide = group * tokens
    query = query_ref[...].reshape(wide, dim)

    def one(row):
        similar = lax.dot_general(
            store_ref[row], query, (((1,), (1,)), ((), ())), preferred_element_type=F32
        )
        best_ref[row] = jnp.max(similar.reshape(length // 8, 8, wide), axis=0)

    def some(step, carry):
        for inner in range(4):
            one(step * 4 + inner)
        return carry

    lax.fori_loop(0, rows // 4, some, 0)
    best = jnp.max(best_ref[...], axis=1)
    member = lax.broadcasted_iota(jnp.int32, (group, wide), 1) // tokens
    mine = lax.broadcasted_iota(jnp.int32, (group, wide), 0)
    picks = jnp.where(member == mine, 1.0, 0.0)
    out_ref[...] = lax.dot_general(
        picks, best, (((1,), (1,)), ((), ())),
        preferred_element_type=F32, precision=lax.Precision.HIGHEST,
    )


def score(queries, store):
    count, tokens, dim = queries.shape
    rows, length, _ = store.shape
    group = 8
    return pl.pallas_call(
        score_kernel,
        name="score",
        grid=(count // group,),
        out_shape=jax.ShapeDtypeStruct((count, rows), F32),
        in_specs=[
            pl.BlockSpec((group, tokens, dim), lambda i: (i, 0, 0)),
            pl.BlockSpec((rows, length, dim), lambda i: (0, 0, 0)),
        ],
        out_specs=pl.BlockSpec((group, rows), lambda i: (i, 0)),
        scratch_shapes=[pltpu.VMEM((rows, 8, group * tokens), F32)],
        cost_estimate=cost(
            2 * count * tokens * rows * length * dim,
            2 * (count * tokens + rows * length) * dim,
        ),
    )(queries, store)


def finish_kernel(busiest_ref, holder_ref, row_ref, back_ref, hot_ref, out_ref):
    queries, slots = holder_ref.shape
    device_count, rows = back_ref.shape
    back = back_ref[...]
    first = back.astype(BF16)
    rest = back - first.astype(F32)
    second = rest.astype(BF16)
    third = (rest - second.astype(F32)).astype(BF16)
    device_iota = lax.broadcasted_iota(jnp.int32, (queries, device_count), 1)
    row_iota = lax.broadcasted_iota(jnp.int32, (queries, rows), 1)
    holder_all = holder_ref[...].astype(jnp.int32)
    row_all = row_ref[...].astype(jnp.int32)
    marks = [
        jnp.where(device_iota == holder_all[:, c : c + 1], 1.0, 0.0)
        for c in range(slots)
    ]
    mark = jnp.concatenate(marks, axis=0).astype(BF16)
    away = (
        jnp.dot(mark, first, preferred_element_type=F32)
        + jnp.dot(mark, second, preferred_element_type=F32)
    ) + jnp.dot(mark, third, preferred_element_type=F32)
    hot = hot_ref[...]
    picked = []
    for c in range(slots):
        holder = holder_all[:, c : c + 1]
        found = jnp.where(
            holder == busiest_ref[0], hot, away[c * queries : (c + 1) * queries]
        )
        value = jnp.sum(
            jnp.where(row_iota == row_all[:, c : c + 1], found, 0.0),
            axis=1, keepdims=True,
        )
        picked.append(jnp.where(holder >= 0, value, 0.0))
    out_ref[...] = columns(picked, slots)


def finish(busiest, holder, row, back, hot):
    return pl.pallas_call(
        finish_kernel,
        name="finish",
        out_shape=jax.ShapeDtypeStruct(holder.shape, F32),
        in_specs=[smem(), vmem(), vmem(), vmem(), vmem()],
        out_specs=vmem(),
    )(busiest, holder, row, back, hot)


def spread(store, busiest, device_count):
    planes = device_count // PLANE
    me = lax.axis_index("shard")
    plane, seat = me // PLANE, me % PLANE
    source_plane, source_seat = busiest // PLANE, busiest % PLANE
    rows, length, dim = store.shape
    part = rows // PLANE
    groups = [[p * PLANE + s for s in range(PLANE)] for p in range(planes)]
    parts = lax.all_to_all(
        store, "shard", 0, 0, tiled=True, axis_index_groups=groups
    ).reshape(PLANE, part * length, dim)
    piece = lax.dynamic_index_in_dim(parts, source_seat, 0, keepdims=False)

    def from_plane(start):
        def run(value):
            have, hop = [start], planes // 2
            while hop:
                pairs = [
                    (p * PLANE + s, ((p + hop) % planes) * PLANE + s)
                    for p in have for s in range(PLANE)
                ]
                moved = lax.ppermute(value, "shard", pairs)
                fresh = (plane - start) % (2 * hop) == hop
                value = jnp.where(fresh, moved, value)
                have = have + [(p + hop) % planes for p in have]
                hop //= 2
            return value

        return run

    piece = lax.switch(source_plane, [from_plane(p) for p in range(planes)], piece)
    pieces = [piece]
    for turn in range(1, PLANE):
        pieces.append(
            lax.ppermute(
                piece, "shard",
                [
                    (p * PLANE + s, p * PLANE + (s + turn) % PLANE)
                    for p in range(planes) for s in range(PLANE)
                ],
            )
        )
    turned = jnp.stack(pieces)
    order = (seat - jnp.arange(PLANE, dtype=jnp.int32)) % PLANE
    return turned[order].reshape(rows, length, dim)


def local(
    query_tokens, candidates, cand_count, placement_map,
    passage_base, residual_codes, passage_lengths, bucket_weights,
):
    device_count = lax.axis_size("shard")
    store_rows = passage_base.shape[0]
    outgoing, holder, row, busiest = prepare(
        candidates, cand_count, placement_map, query_tokens, store_rows, device_count
    )
    arrived = lax.all_to_all(outgoing, "shard", 0, 0, tiled=True)
    store = decode(passage_base, residual_codes, passage_lengths, bucket_weights)
    hot_store = spread(store, busiest[0], device_count)
    visited = score(arrived, store)
    back = lax.all_to_all(visited, "shard", 0, 0, tiled=True)
    hot = score(query_tokens, hot_store)
    return finish(busiest, holder, row, back, hot)


def solution(mesh):
    whole = P(("groups", "shard"))
    return jax.shard_map(
        local,
        mesh=mesh,
        in_specs=(whole, whole, whole, P("groups"), whole, whole, whole, P("groups")),
        out_specs=whole,
        check_vma=False,
    )
```

time: 454 us -> 258 us (0.57)
  local copies, waits for them, and re-layouts: 132 us -> 7.08 us
  matrix products: 94.4 us -> 0 us
  waiting for transfers between devices: 155 us -> 74.2 us
  Pallas kernels: 0 us -> 61.6 us
  starting transfers between devices: 52.3 us -> 113 us
  other arithmetic: 17.9 us -> 0.74 us
    all_to_all x3, waiting for transfers between devices: 155 us -> 10.5 us  [the longest x1 6.76 us: spread(): lax.all_to_all(store, 'shard', 0, 0, tiled=True, axis_index_groups=groups)]
    gather x83 -> x1, local copies, waits for them, and re-layouts: 118 us -> 1.68 us  [spread(): return turned[order].reshape(rows, length, dim)]
    dot_general x25 -> x0, matrix products: 94.4 us -> none  [the longest x24 93.4 us: score_block(): jnp.einsum('mqd,mkpd->mqkp', query_rows, token_rows, preferred_element_ty...]
    ppermute x0 -> x11, waiting for transfers between devices: none -> 63.7 us  [the longest x4 59.4 us: run(): moved = lax.ppermute(value, 'shard', pairs)]
    pallas_call x0 -> x5, Pallas kernels: none -> 61.6 us  [the longest x2 45.6 us: score(): pl.pallas_call(score_kernel, name='score', grid=(count // group,), out_sh...]
    ppermute x0 -> x11, starting transfers between devices: none -> 59.2 us  [the longest x7 55.8 us: spread(): lax.ppermute(piece, 'shard', [(p * PLANE + s, p * PLANE + (s + turn) % PL...]
    reduce_sum x28 -> x0, other arithmetic: 9.33 us -> none  [the longest x1 4.76 us: decode(): jnp.sum(summed * summed, axis=-1, keepdims=True) + epsilon]
    select_n x50 -> x0, local copies, waits for them, and re-layouts: 4.72 us -> none  [the longest x48 3.98 us: one_block(): return score_block(query_part, decoded[row_part], lengths[row_part])]
  transfers between devices with their start and end apart: 3 -> 14, of which waited for: 3 -> 4; matrix products, arithmetic and copies ran while one was open for 5% -> 2% of each run, Pallas kernels for 0% -> 7%
where the time goes in v1:
time: 258 us; the launch traced here: 260 us
  starting transfers between devices  113 us (44%)
  waiting for transfers between devices  74.2 us (29%)
  Pallas kernels  61.6 us (24%)
  local copies, waits for them, and re-layouts  7.08 us (3%)
  between operations  2.76 us (1%)
    ppermute x4, waiting for transfers between devices, run(): moved = lax.ppermute(value, 'shard', pairs)  59.4 us
    ppermute x7, starting transfers between devices, spread(): lax.ppermute(piece, 'shard', [(p * PLANE + s, p * PLANE + (s + turn) % PL...  55.8 us
    pallas_call x2, Pallas kernels, score(): pl.pallas_call(score_kernel, name='score', grid=(count // group,), out_sh...  45.6 us
    all_to_all x1, starting transfers between devices, spread(): lax.all_to_all(store, 'shard', 0, 0, tiled=True, axis_index_groups=groups)  24 us
    all_to_all x1, starting transfers between devices, local(): back = lax.all_to_all(visited, 'shard', 0, 0, tiled=True)  19.6 us
    all_to_all x1, starting transfers between devices, local(): arrived = lax.all_to_all(outgoing, 'shard', 0, 0, tiled=True)  10.5 us
    pallas_call x1, Pallas kernels, prepare(): pl.pallas_call(functools.partial(prepare_kernel, store_rows, device_count...  6.93 us
    all_to_all x1, waiting for transfers between devices, spread(): lax.all_to_all(store, 'shard', 0, 0, tiled=True, axis_index_groups=groups)  6.76 us
  transfers between devices with their start and end apart: 14, of which 4 were waited for; matrix products, arithmetic and copies ran while one was open for 2% of the time, Pallas kernels for 7%

profile of v1, /device:TPU:33, one launch (start us, length us, event | category | flops | bytes accessed | tf_op | source)
XLA Modules:
  0.0 259.9 jit_solution(4079308198902317658)
XLA Ops:
  0.0 4.3 %decode.1.store_ref = bf16[32,128,128]{2,1,0:T(8,128)(2,1)} custom-call(s32[32]{0:T(128)} %length_ref.1, f32[4]{0:T(128)} %level_ref.1, bf16[32,128,128]{2,1,0:T(8,128)(2,1)} %base_ref.1, s32[32,128,128]{2,1,0:T(8,128)} %code_ref.1), custom_call_target="tpu_custom_call" | custom-call | flops 10485760 | bytes 4194304 | tf_op jit(solution)/shard_map/decode/pallas_call | solution.py:141
  4.3 24.0 %all-to-all-start.2 = ((bf16[32,128,128]{2,1,0:T(8,128)(2,1)}), bf16[32,128,128]{2,1,0:T(8,128)(2,1)S(1)}, u32[]{:S(2)}, u32[]{:S(2)}) async-start(bf16[32,128,128]{2,1,0:T(8,128)(2,1)} %decode.1.store_ref), calls=%async_computation.2 | async-start | bytes 2097152 | tf_op jit(solution)/shard_map/all_to_all | solution.py:256
  28.4 0.7 copy.12.cand_ref
  29.0 0.7 copy.13.count_ref
  29.7 6.9 %prepare.1 = (bf16[128,32,128]{2,1,0:T(8,128)(2,1)}, f32[32,24]{1,0:T(8,128)}, f32[32,24]{1,0:T(8,128)}, s32[1]{0:T(128)}) custom-call(s32[32,24]{1,0:T(8,128)} %copy.12.cand_ref, s32[32,1]{1,0:T(8,128)} %copy.13.count_ref, s32[32,128]{1,0:T(8,128)} %bitcast.155, bf16[32,32,128]{2,1,0:T(8,128)(2,1)} %query_ref.3), custom_call_target="tpu_custom_call" | custom-call | tf_op jit(solution)/shard_map/prepare/pallas_call | solution.py:95
  36.7 6.8 %all-to-all-done.2 = bf16[32,128,128]{2,1,0:T(8,128)(2,1)S(1)} async-done(((bf16[32,128,128]{2,1,0:T(8,128)(2,1)}), bf16[32,128,128]{2,1,0:T(8,128)(2,1)S(1)}, u32[]{:S(2)}, u32[]{:S(2)}) %all-to-all-start.2) | async-done | bytes 1048608 | tf_op jit(solution)/shard_map/all_to_all | solution.py:256
  43.4 10.5 %all-to-all-start = ((bf16[128,32,128]{2,1,0:T(8,128)(2,1)}), bf16[128,32,128]{2,1,0:T(8,128)(2,1)S(1)}, u32[]{:S(2)}, u32[]{:S(2)}) async-start(bf16[128,32,128]{2,1,0:T(8,128)(2,1)} %get-tuple-element.688), calls=%async_computation | async-start | bytes 2097152 | tf_op jit(solution)/shard_map/all_to_all | solution.py:304
  56.5 64.6 %conditional.1 = (bf16[512,128]{1,0:T(8,128)(2,1)}, bf16[1,512,128]{2,1,0:T(8,128)(2,1)S(1)}) conditional(s32[]{:T(128)} %clamp.3, (s32[]{:T(128)}, s32[]{:T(128)}, pred[]{:T(512)}, s32[]{:T(128)}, bf16[32,128,128]{2,1,0:T(8,128)(2,1)S(1)}, /*index=5*/s32[]{:T(128)}) %tuple.85, (s32[]{:T(128)}, s32[]{:T(128)}, ...), branch_computations={%region_0.1_spmd, %region_1.2_spmd, %region_2.3_spmd, %region_3.4_... | conditional | flops 262195 | bytes 4194995 | solution.py:278
  56.6 0.7 collective-permute-start.44
  57.4 0.7 collective-permute-start.45
  58.1 0.7 collective-permute-start.46
  58.8 1.3 collective-permute-start.47
  60.2 59.4 %collective-permute-done.47 = bf16[512,128]{1,0:T(8,128)(2,1)S(1)} collective-permute-done((bf16[512,128]{1,0:T(8,128)(2,1)S(1)}, bf16[512,128]{1,0:T(8,128)(2,1)S(1)}, u32[]{:S(2)}, u32[]{:S(2)}) %collective-permute-start.47) | collective-permute-done | bytes 131104 | tf_op jit(solution)/shard_map/cond/branch_11_fun/ppermute | solution.py:269
  119.5 0.7 broadcast_select_fusion.47
  120.2 0.9 copy.39
  121.1 3.8 %collective-permute-start.64 = (bf16[512,128]{1,0:T(8,128)(2,1)}, bf16[512,128]{1,0:T(8,128)(2,1)S(1)}, u32[]{:S(2)}, u32[]{:S(2)}) collective-permute-start(bf16[512,128]{1,0:T(8,128)(2,1)} %get-tuple-element.690), channel_id=1, source_target_pairs={{0,1},{1,2},{2,3},{3,4},{4,5},{5,6},{6,7},{7,0},{8,9},{9,10},{10,1... | collective-permute-start | bytes 393224 | tf_op jit(solution)/shard_map/ppermute | solution.py:282
  124.9 1.2 collective-permute-start.65
  126.1 1.8 collective-permute-start.66
  127.9 0.4 collective-permute-start.67
  128.3 14.6 %collective-permute-start.68 = (bf16[512,128]{1,0:T(8,128)(2,1)}, bf16[512,128]{1,0:T(8,128)(2,1)S(1)}, u32[]{:S(2)}, u32[]{:S(2)}) collective-permute-start(bf16[512,128]{1,0:T(8,128)(2,1)} %get-tuple-element.690), channel_id=1, source_target_pairs={{0,5},{1,6},{2,7},{3,0},{4,1},{5,2},{6,3},{7,4},{8,13},{9,14},{10,... | collective-permute-start | bytes 393224 | tf_op jit(solution)/shard_map/ppermute | solution.py:282
  142.9 17.1 %collective-permute-start.69 = (bf16[512,128]{1,0:T(8,128)(2,1)}, bf16[512,128]{1,0:T(8,128)(2,1)S(1)}, u32[]{:S(2)}, u32[]{:S(2)}) collective-permute-start(bf16[512,128]{1,0:T(8,128)(2,1)} %get-tuple-element.690), channel_id=1, source_target_pairs={{0,6},{1,7},{2,0},{3,1},{4,2},{5,3},{6,4},{7,5},{8,14},{9,15},{10,... | collective-permute-start | bytes 393224 | tf_op jit(solution)/shard_map/ppermute | solution.py:282
  160.0 17.0 %collective-permute-start.70 = (bf16[512,128]{1,0:T(8,128)(2,1)}, bf16[512,128]{1,0:T(8,128)(2,1)S(1)}, u32[]{:S(2)}, u32[]{:S(2)}) collective-permute-start(bf16[512,128]{1,0:T(8,128)(2,1)} %get-tuple-element.690), channel_id=1, source_target_pairs={{0,7},{1,0},{2,1},{3,2},{4,3},{5,4},{6,5},{7,6},{8,15},{9,8},{10,9... | collective-permute-start | bytes 393224 | tf_op jit(solution)/shard_map/ppermute | solution.py:282
  177.2 4.3 %collective-permute-done.70 = bf16[512,128]{1,0:T(8,128)(2,1)S(1)} collective-permute-done((bf16[512,128]{1,0:T(8,128)(2,1)}, bf16[512,128]{1,0:T(8,128)(2,1)S(1)}, u32[]{:S(2)}, u32[]{:S(2)}) %collective-permute-start.70) | collective-permute-done | bytes 131104 | tf_op jit(solution)/shard_map/ppermute | solution.py:282
  181.5 1.7 gather_fusion
  183.2 1.0 copy-done
  184.2 35.4 %score.2 = f32[128,32]{1,0:T(8,128)} custom-call(bf16[128,32,128]{2,1,0:T(8,128)(2,1)} %copy-done, bf16[32,128,128]{2,1,0:T(8,128)(2,1)} %decode.1.store_ref), custom_call_target="tpu_custom_call" | custom-call | flops 4294967296 | bytes 2097152 | tf_op jit(solution)/shard_map/score/pallas_call | solution.py:184
  219.6 19.6 %all-to-all-start.1 = ((f32[128,1,32]{2,1,0:T(1,128)}), f32[128,1,32]{2,1,0:T(1,128)S(1)}, u32[]{:S(2)}, u32[]{:S(2)}) async-start(f32[128,1,32]{2,1,0:T(1,128)} %bitcast.154), calls=%async_computation.1 | async-start | bytes 131072 | tf_op jit(solution)/shard_map/all_to_all | solution.py:308
  239.2 10.3 %score.3.hot_ref = f32[32,32]{1,0:T(8,128)} custom-call(bf16[32,32,128]{2,1,0:T(8,128)(2,1)} %query_ref.3, bf16[32,128,128]{2,1,0:T(8,128)(2,1)} %bitcast.152), custom_call_target="tpu_custom_call" | custom-call | flops 1073741824 | bytes 1310720 | tf_op jit(solution)/shard_map/score/pallas_call | solution.py:184
  249.4 3.7 %all-to-all-done.1 = f32[128,1,32]{2,1,0:T(1,128)S(1)} async-done(((f32[128,1,32]{2,1,0:T(1,128)}), f32[128,1,32]{2,1,0:T(1,128)S(1)}, u32[]{:S(2)}, u32[]{:S(2)}) %all-to-all-start.1) | async-done | bytes 16416 | tf_op jit(solution)/shard_map/all_to_all | solution.py:308
  253.2 0.6 copy-done.1
  253.8 4.7 %finish.1 = f32[32,24]{1,0:T(8,128)} custom-call(s32[1]{0:T(128)} %get-tuple-element.685.busiest_ref, f32[32,24]{1,0:T(8,128)} %get-tuple-element.686.holder_ref, f32[32,24]{1,0:T(8,128)} %get-tuple-element.687.row_ref, f32[128,32]{1,0:T(8,128)} %bitcast.153, f32[32,32]{1,0:T(8,128)} %score.3.hot_ref), custom_call_target="tpu_custom_call" | custom-call | tf_op jit(solution)/shard_map/finish/pallas_call | solution.py:239
  258.5 1.4 copy.15
  (30 shorter events, 0.3 us)
Async XLA Ops:
  4.3 24.0 %copy-start.2 = (s32[32,24]{0,1:T(8,128)S(1)}, s32[32,24]{0,1:T(8,128)}, u32[]{:S(2)}) copy-start(s32[32,24]{0,1:T(8,128)} %param.25) | copy-start | bytes 9220
  4.3 24.7 %copy-start.3 = (s32[32]{0:T(128)S(1)}, s32[32]{0:T(128)}, u32[]{:S(2)}) copy-start(s32[32]{0:T(128)} %param.26) | copy-start | bytes 388
  4.3 39.1 %all-to-all-start.2 = ((bf16[32,128,128]{2,1,0:T(8,128)(2,1)}), bf16[32,128,128]{2,1,0:T(8,128)(2,1)S(1)}, u32[]{:S(2)}, u32[]{:S(2)}) async-start(bf16[32,128,128]{2,1,0:T(8,128)(2,1)} %decode.1.store_ref), calls=%async_computation.2 | async-start | bytes 2097152 | tf_op jit(solution)/shard_map/all_to_all | solution.py:256
  43.4 139.8 %all-to-all-start = ((bf16[128,32,128]{2,1,0:T(8,128)(2,1)}), bf16[128,32,128]{2,1,0:T(8,128)(2,1)S(1)}, u32[]{:S(2)}, u32[]{:S(2)}) async-start(bf16[128,32,128]{2,1,0:T(8,128)(2,1)} %get-tuple-element.688), calls=%async_computation | async-start | bytes 2097152 | tf_op jit(solution)/shard_map/all_to_all | solution.py:304
  56.6 0.7 collective-permute-start.44
  57.4 0.7 collective-permute-start.45
  58.1 0.7 collective-permute-start.46
  58.8 60.7 %collective-permute-start.47 = (bf16[512,128]{1,0:T(8,128)(2,1)S(1)}, bf16[512,128]{1,0:T(8,128)(2,1)S(1)}, u32[]{:S(2)}, u32[]{:S(2)}) collective-permute-start(bf16[512,128]{1,0:T(8,128)(2,1)S(1)} %broadcast_select_fusion.46), channel_id=1, source_target_pairs={{88,96},{89,97},{90,98},{91,99},{92,100},{93,101},{94,102},{95,103... | collective-permute-start | bytes 393224 | tf_op jit(solution)/shard_map/cond/branch_11_fun/ppermute | solution.py:269
  121.1 21.8 %collective-permute-start.64 = (bf16[512,128]{1,0:T(8,128)(2,1)}, bf16[512,128]{1,0:T(8,128)(2,1)S(1)}, u32[]{:S(2)}, u32[]{:S(2)}) collective-permute-start(bf16[512,128]{1,0:T(8,128)(2,1)} %get-tuple-element.690), channel_id=1, source_target_pairs={{0,1},{1,2},{2,3},{3,4},{4,5},{5,6},{6,7},{7,0},{8,9},{9,10},{10,1... | collective-permute-start | bytes 393224 | tf_op jit(solution)/shard_map/ppermute | solution.py:282
  124.9 35.1 %collective-permute-start.65 = (bf16[512,128]{1,0:T(8,128)(2,1)}, bf16[512,128]{1,0:T(8,128)(2,1)S(1)}, u32[]{:S(2)}, u32[]{:S(2)}) collective-permute-start(bf16[512,128]{1,0:T(8,128)(2,1)} %get-tuple-element.690), channel_id=1, source_target_pairs={{0,2},{1,3},{2,4},{3,5},{4,6},{5,7},{6,0},{7,1},{8,10},{9,11},{10,... | collective-permute-start | bytes 393224 | tf_op jit(solution)/shard_map/ppermute | solution.py:282
  126.1 50.9 %collective-permute-start.66 = (bf16[512,128]{1,0:T(8,128)(2,1)}, bf16[512,128]{1,0:T(8,128)(2,1)S(1)}, u32[]{:S(2)}, u32[]{:S(2)}) collective-permute-start(bf16[512,128]{1,0:T(8,128)(2,1)} %get-tuple-element.690), channel_id=1, source_target_pairs={{0,3},{1,4},{2,5},{3,6},{4,7},{5,0},{6,1},{7,2},{8,11},{9,12},{10,... | collective-permute-start | bytes 393224 | tf_op jit(solution)/shard_map/ppermute | solution.py:282
  127.9 49.2 %collective-permute-start.67 = (bf16[512,128]{1,0:T(8,128)(2,1)}, bf16[512,128]{1,0:T(8,128)(2,1)S(1)}, u32[]{:S(2)}, u32[]{:S(2)}) collective-permute-start(bf16[512,128]{1,0:T(8,128)(2,1)} %get-tuple-element.690), channel_id=1, source_target_pairs={{0,4},{1,5},{2,6},{3,7},{4,0},{5,1},{6,2},{7,3},{8,12},{9,13},{10,... | collective-permute-start | bytes 393224 | tf_op jit(solution)/shard_map/ppermute | solution.py:282
  128.3 48.8 %collective-permute-start.68 = (bf16[512,128]{1,0:T(8,128)(2,1)}, bf16[512,128]{1,0:T(8,128)(2,1)S(1)}, u32[]{:S(2)}, u32[]{:S(2)}) collective-permute-start(bf16[512,128]{1,0:T(8,128)(2,1)} %get-tuple-element.690), channel_id=1, source_target_pairs={{0,5},{1,6},{2,7},{3,0},{4,1},{5,2},{6,3},{7,4},{8,13},{9,14},{10,... | collective-permute-start | bytes 393224 | tf_op jit(solution)/shard_map/ppermute | solution.py:282
  142.9 34.3 %collective-permute-start.69 = (bf16[512,128]{1,0:T(8,128)(2,1)}, bf16[512,128]{1,0:T(8,128)(2,1)S(1)}, u32[]{:S(2)}, u32[]{:S(2)}) collective-permute-start(bf16[512,128]{1,0:T(8,128)(2,1)} %get-tuple-element.690), channel_id=1, source_target_pairs={{0,6},{1,7},{2,0},{3,1},{4,2},{5,3},{6,4},{7,5},{8,14},{9,15},{10,... | collective-permute-start | bytes 393224 | tf_op jit(solution)/shard_map/ppermute | solution.py:282
  160.0 21.5 %collective-permute-start.70 = (bf16[512,128]{1,0:T(8,128)(2,1)}, bf16[512,128]{1,0:T(8,128)(2,1)S(1)}, u32[]{:S(2)}, u32[]{:S(2)}) collective-permute-start(bf16[512,128]{1,0:T(8,128)(2,1)} %get-tuple-element.690), channel_id=1, source_target_pairs={{0,7},{1,0},{2,1},{3,2},{4,3},{5,4},{6,5},{7,6},{8,15},{9,8},{10,9... | collective-permute-start | bytes 393224 | tf_op jit(solution)/shard_map/ppermute | solution.py:282
  183.2 1.0 copy-start
  219.6 33.6 %all-to-all-start.1 = ((f32[128,1,32]{2,1,0:T(1,128)}), f32[128,1,32]{2,1,0:T(1,128)S(1)}, u32[]{:S(2)}, u32[]{:S(2)}) async-start(f32[128,1,32]{2,1,0:T(1,128)} %bitcast.154), calls=%async_computation.1 | async-start | bytes 131072 | tf_op jit(solution)/shard_map/all_to_all | solution.py:308
  253.2 0.6 copy-start.1

commit v2 on v1

v2 whole, which is shorter than its diff:
```python
import functools

import jax
import jax.numpy as jnp
from jax import lax
from jax.experimental import pallas as pl
from jax.experimental.pallas import tpu as pltpu
from jax.sharding import PartitionSpec as P

EPSILON = 1e-06
PLANE = 8
F32 = jnp.float32
BF16 = jnp.bfloat16


def vmem(*_):
    return pl.BlockSpec(memory_space=pltpu.VMEM)


def smem(*_):
    return pl.BlockSpec(memory_space=pltpu.SMEM)


def cost(flops, moved):
    return pl.CostEstimate(flops=flops, transcendentals=0, bytes_accessed=moved)


def columns(parts, width):
    lane = lax.broadcasted_iota(jnp.int32, (parts[0].shape[0], width), 1)
    out = jnp.zeros((parts[0].shape[0], width), F32)
    for index, part in enumerate(parts):
        out = jnp.where(lane == index, part, out)
    return out


def prepare_kernel(
    store_rows, device_count,
    cand_ref, count_ref, map_ref, query_ref,
    out_ref, holder_ref, row_ref, note_ref,
    pick_vmem, pick_smem, sem,
):
    queries, slots = cand_ref.shape
    table_rows, lanes = map_ref.shape
    table = map_ref[...]
    holder_table = table // store_rows
    row_table = table - holder_table * store_rows
    both = jnp.concatenate([holder_table, row_table], axis=1).astype(F32).astype(BF16)
    ids = cand_ref[...]
    high = ids // lanes
    low = ids - high * lanes
    table_iota = lax.broadcasted_iota(jnp.int32, (queries, table_rows), 1)
    lane_iota = lax.broadcasted_iota(jnp.int32, (queries, lanes), 1)
    device_iota = lax.broadcasted_iota(jnp.int32, (queries, device_count), 1)
    marks = [
        jnp.where(table_iota == high[:, c : c + 1], 1.0, 0.0) for c in range(slots)
    ]
    rows = jnp.dot(
        jnp.concatenate(marks, axis=0).astype(BF16), both, preferred_element_type=F32
    )
    present = jnp.zeros((queries, device_count), F32)
    holders, local_rows = [], []
    for c in range(slots):
        block = rows[c * queries : (c + 1) * queries]
        here = lane_iota == low[:, c : c + 1]
        holder = jnp.sum(jnp.where(here, block[:, :lanes], 0.0), axis=1, keepdims=True)
        row = jnp.sum(jnp.where(here, block[:, lanes:], 0.0), axis=1, keepdims=True)
        holder = jnp.where(count_ref[...] > c, holder, -1.0)
        present = jnp.where(device_iota == holder.astype(jnp.int32), 1.0, present)
        holders.append(holder)
        local_rows.append(row)
    holder_ref[...] = columns(holders, slots)
    row_ref[...] = columns(local_rows, slots)
    query_iota = lax.broadcasted_iota(jnp.int32, (queries, device_count), 0).astype(F32)
    pick = jnp.max(present * query_iota, axis=0, keepdims=True)
    pick_vmem[...] = jnp.broadcast_to(pick.astype(jnp.int32), pick_vmem.shape)
    copy = pltpu.make_async_copy(pick_vmem, pick_smem, sem)
    copy.start()
    shared = jnp.sum(present, axis=0, keepdims=True)
    device = lax.broadcasted_iota(jnp.int32, (1, device_count), 1).astype(F32)
    busiest = jnp.max(jnp.where(shared > 1.5, device, 0.0)).astype(jnp.int32)
    theirs = jnp.where(device_iota == busiest, present, 0.0)
    last = jnp.max(theirs * query_iota).astype(jnp.int32)
    total = jnp.sum(theirs * query_iota).astype(jnp.int32)
    first = (queries - 1) - jnp.max(theirs * ((queries - 1) - query_iota)).astype(jnp.int32)
    middle = jnp.clip(total - first - last, 0, queries - 1)
    note_ref[0] = busiest
    note_ref[1] = first
    note_ref[2] = middle
    tokens = query_ref.shape[1]
    extra = 2 * tokens // PLANE
    spare = []
    for seat in range(PLANE):
        query = first if seat < PLANE // 2 else middle
        start = (seat % (PLANE // 2)) * extra
        spare.append(query_ref[query, start : start + extra, :])
    copy.wait()

    def pack(step, carry):
        for seat in range(PLANE):
            device = step * PLANE + seat
            out_ref[device, 0:tokens, :] = query_ref[pick_smem[0, device]]
            out_ref[device, tokens : tokens + extra, :] = spare[seat]
        return carry

    lax.fori_loop(0, device_count // PLANE, pack, 0)


def prepare(candidates, cand_count, placement_map, query_tokens, store_rows, device_count):
    queries, slots = candidates.shape
    _, tokens, dim = query_tokens.shape
    return pl.pallas_call(
        functools.partial(prepare_kernel, store_rows, device_count),
        name="prepare",
        out_shape=(
            jax.ShapeDtypeStruct((device_count, tokens + 2 * tokens // PLANE, dim), BF16),
            jax.ShapeDtypeStruct((queries, slots), F32),
            jax.ShapeDtypeStruct((queries, slots), F32),
            jax.ShapeDtypeStruct((4,), jnp.int32),
        ),
        in_specs=[vmem(), vmem(), vmem(), vmem()],
        out_specs=(vmem(), vmem(), vmem(), smem()),
        scratch_shapes=[
            pltpu.VMEM((8, device_count), jnp.int32),
            pltpu.SMEM((8, device_count), jnp.int32),
            pltpu.SemaphoreType.DMA(()),
        ],
        cost_estimate=cost(10**9, 2 * 10**6),
    )(
        candidates,
        cand_count.reshape(queries, 1),
        placement_map.reshape(-1, 128),
        query_tokens,
    )


def decode_kernel(seat_ref, length_ref, level_ref, base_ref, code_ref, out_ref):
    part, length, dim = base_ref.shape
    block = lax.rem(seat_ref[0] + pl.program_id(0), PLANE)
    token = lax.broadcasted_iota(jnp.int32, (length, dim), 0)
    for index in range(part):
        code = code_ref[index]
        residual = jnp.where(
            code < 2,
            jnp.where(code == 0, level_ref[0], level_ref[1]),
            jnp.where(code == 2, level_ref[2], level_ref[3]),
        )
        summed = base_ref[index].astype(F32) + residual
        inverse = lax.rsqrt(jnp.sum(summed * summed, axis=1, keepdims=True) + EPSILON)
        tokens = summed * inverse
        tokens = jnp.where(token < length_ref[block * part + index], tokens, tokens[0:1])
        out_ref[0, index] = tokens.astype(BF16)


def decode(seat, passage_base, residual_codes, passage_lengths, bucket_weights):
    rows, length, dim = passage_base.shape
    part = rows // PLANE
    spec = pl.BlockSpec(
        (part, length, dim), lambda i, seat_ref: (lax.rem(seat_ref[0] + i, PLANE), 0, 0)
    )
    return pl.pallas_call(
        decode_kernel,
        name="decode",
        out_shape=jax.ShapeDtypeStruct((PLANE, part, length, dim), BF16),
        grid_spec=pltpu.PrefetchScalarGridSpec(
            num_scalar_prefetch=1,
            grid=(PLANE,),
            in_specs=[smem(), smem(), spec, spec],
            out_specs=pl.BlockSpec((1, part, length, dim), lambda i, _: (i, 0, 0, 0)),
        ),
        cost_estimate=cost(rows * length * dim * 20, rows * length * dim * 8),
    )(seat, passage_lengths, bucket_weights, passage_base, residual_codes)


def score_kernel(seat_ref, arrived_ref, store_ref, *refs):
    hot_refs, (out_ref, best_ref) = refs[:PLANE], refs[PLANE:]
    slots, height, dim = arrived_ref.shape
    _, part, length, _ = store_ref.shape
    rows = PLANE * part
    tokens = height * PLANE // (PLANE + 2)
    extra = height - tokens
    group = slots * extra // tokens
    wide = group * tokens
    seat = seat_ref[0]

    def against(query, block, turned, sign):
        for k in range(PLANE):
            home = lax.rem(seat + sign * k + PLANE, PLANE) * part
            for j in range(part):
                similar = lax.dot_general(
                    block(k, j), query, (((1,), (1,)), ((), ())),
                    preferred_element_type=F32,
                )
                best_ref[home + j] = jnp.max(similar.reshape(length // 8, 8, wide), axis=0)
        best = jnp.max(best_ref[...], axis=1)
        count = wide // turned
        member = lax.broadcasted_iota(jnp.int32, (count, wide), 1) // turned
        mine = lax.broadcasted_iota(jnp.int32, (count, wide), 0)
        picks = jnp.where(member == mine, 1.0, 0.0)
        return lax.dot_general(
            picks, best, (((1,), (1,)), ((), ())),
            preferred_element_type=F32, precision=lax.Precision.HIGHEST,
        )

    def some(step, carry):
        start = pl.multiple_of(step * group, group)
        query = arrived_ref[pl.ds(start, group), 0:tokens, :].reshape(wide, dim)
        out_ref[pl.ds(start, group), 0:rows] = against(
            query, lambda k, j: store_ref[k, j], tokens, 1
        )
        return carry

    lax.fori_loop(0, slots // group, some, 0)
    query = arrived_ref[:, tokens:height, :].reshape(wide, dim)
    out_ref[:, rows : 2 * rows] = against(
        query, lambda k, j: hot_refs[k][j], extra, -1
    )


def score(seat, arrived, store, hot_parts):
    count, height, dim = arrived.shape
    _, part, length, _ = store.shape
    rows = PLANE * part
    slots = 32
    hot_spec = pl.BlockSpec((part, length, dim), lambda i: (0, 0, 0))
    return pl.pallas_call(
        score_kernel,
        name="score",
        grid=(count // slots,),
        out_shape=jax.ShapeDtypeStruct((count, 2 * rows), F32),
        in_specs=[
            smem(),
            pl.BlockSpec((slots, height, dim), lambda i: (i, 0, 0)),
            pl.BlockSpec((PLANE, part, length, dim), lambda i: (0, 0, 0, 0)),
        ] + [hot_spec] * PLANE,
        out_specs=pl.BlockSpec((slots, 2 * rows), lambda i: (i, 0)),
        scratch_shapes=[pltpu.VMEM((rows, 8, 256), F32)],
        cost_estimate=cost(
            2 * count * height * rows * length * dim,
            2 * (count * height + 2 * rows * length) * dim,
        ),
    )(seat, arrived, store, *hot_parts)


def finish_kernel(note_ref, holder_ref, row_ref, back_ref, out_ref):
    queries, slots = holder_ref.shape
    device_count, wide = back_ref.shape
    rows = wide // 2
    busiest = note_ref[0]
    back = back_ref[...]
    near = back[:, :rows]
    first = near.astype(BF16)
    rest = near - first.astype(F32)
    second = rest.astype(BF16)
    third = (rest - second.astype(F32)).astype(BF16)
    device_iota = lax.broadcasted_iota(jnp.int32, (queries, device_count), 1)
    row_iota = lax.broadcasted_iota(jnp.int32, (queries, rows), 1)
    query_iota = lax.broadcasted_iota(jnp.int32, (queries, rows), 0)
    holder_all = holder_ref[...].astype(jnp.int32)
    row_all = row_ref[...].astype(jnp.int32)
    marks = [
        jnp.where(device_iota == holder_all[:, c : c + 1], 1.0, 0.0)
        for c in range(slots)
    ]
    mark = jnp.concatenate(marks, axis=0).astype(BF16)
    away = (
        jnp.dot(mark, first, preferred_element_type=F32)
        + jnp.dot(mark, second, preferred_element_type=F32)
    ) + jnp.dot(mark, third, preferred_element_type=F32)
    plane = pl.multiple_of(busiest // PLANE * PLANE, PLANE)
    parts = back_ref[pl.ds(plane, PLANE), :][:, rows:]
    half = PLANE // 2
    early = jnp.sum(parts[:half], axis=0, keepdims=True)
    later = jnp.sum(parts[half:], axis=0, keepdims=True)
    picked = []
    for c in range(slots):
        holder = holder_all[:, c : c + 1]
        found = away[c * queries : (c + 1) * queries]
        found = jnp.where(
            holder == busiest,
            jnp.where(
                query_iota == note_ref[1], early,
                jnp.where(query_iota == note_ref[2], later, found),
            ),
            found,
        )
        value = jnp.sum(
            jnp.where(row_iota == row_all[:, c : c + 1], found, 0.0),
            axis=1, keepdims=True,
        )
        picked.append(jnp.where(holder >= 0, value, 0.0))
    out_ref[...] = columns(picked, slots)


def finish(note, holder, row, back):
    return pl.pallas_call(
        finish_kernel,
        name="finish",
        out_shape=jax.ShapeDtypeStruct(holder.shape, F32),
        in_specs=[smem(), vmem(), vmem(), vmem()],
        out_specs=vmem(),
    )(note, holder, row, back)


def turn(value, hop, planes):
    pairs = [
        (p * PLANE + s, p * PLANE + (s + hop) % PLANE)
        for p in range(planes) for s in range(PLANE)
    ]
    return lax.ppermute(value, "shard", pairs)


def local(
    query_tokens, candidates, cand_count, placement_map,
    passage_base, residual_codes, passage_lengths, bucket_weights,
):
    device_count = lax.axis_size("shard")
    planes = device_count // PLANE
    seat = lax.rem(lax.axis_index("shard"), PLANE).astype(jnp.int32).reshape(1)
    store_rows = passage_base.shape[0]
    store = decode(seat, passage_base, residual_codes, passage_lengths, bucket_weights)
    parts = [store[0]] + [turn(store[k], k, planes) for k in range(1, PLANE)]
    outgoing, holder, row, note = prepare(
        candidates, cand_count, placement_map, query_tokens, store_rows, device_count
    )
    arrived = lax.all_to_all(outgoing, "shard", 0, 0, tiled=True)
    wanted = lax.rem(seat[0] - lax.rem(note[0], PLANE) + PLANE, PLANE)
    piece = parts[0]
    for k in range(1, PLANE):
        piece = jnp.where(wanted == k, parts[k], piece)
    hot_parts = [piece] + [turn(piece, k, planes) for k in range(1, PLANE)]
    visited = score(seat, arrived, store, hot_parts)
    back = lax.all_to_all(visited, "shard", 0, 0, tiled=True)
    return finish(note, holder, row, back)


def solution(mesh):
    whole = P(("groups", "shard"))
    return jax.shard_map(
        local,
        mesh=mesh,
        in_specs=(whole, whole, whole, P("groups"), whole, whole, whole, P("groups")),
        out_specs=whole,
        check_vma=False,
    )
```

time: 258 us -> 159 us (0.62); the launches traced: 260 us -> 158 us
  starting transfers between devices: 113 us -> 54.3 us
  waiting for transfers between devices: 74.2 us -> 29.5 us
  blocking collectives: 0 us -> 26.4 us
  Pallas kernels: 61.6 us -> 40.1 us
    all_to_all x2 -> x0, starting transfers between devices: 43.6 us -> none  [the longest x1 24 us: spread(): lax.all_to_all(store, 'shard', 0, 0, tiled=True, axis_index_groups=groups)]
    ppermute x11 -> x14, waiting for transfers between devices: 63.7 us -> 21.2 us  [turn(): return lax.ppermute(value, 'shard', pairs)]
    ppermute x11 -> x14, starting transfers between devices: 59.2 us -> 23.3 us  [turn(): return lax.ppermute(value, 'shard', pairs)]
    all_to_all x0 -> x1, blocking collectives: none -> 26.4 us  [local(): back = lax.all_to_all(visited, 'shard', 0, 0, tiled=True)]
    pallas_call x3 -> x2, Pallas kernels: 50 us -> 27.9 us  [the longest x1 21.5 us: score(): pl.pallas_call(score_kernel, name='score', grid=(count // slots,), out_sh...]
    all_to_all x1, starting transfers between devices: 10.5 us -> 31 us  [local(): arrived = lax.all_to_all(outgoing, 'shard', 0, 0, tiled=True)]
    all_to_all x2 -> x0, waiting for transfers between devices: 10.5 us -> none  [the longest x1 6.76 us: spread(): lax.all_to_all(store, 'shard', 0, 0, tiled=True, axis_index_groups=groups)]
    all_to_all x1, waiting for transfers between devices: 0.01 us -> 8.31 us  [local(): arrived = lax.all_to_all(outgoing, 'shard', 0, 0, tiled=True)]
  transfers between devices with their start and end apart: 14 -> 15, of which waited for: 4 -> 10; matrix products, arithmetic and copies ran while one was open for 2% -> 1% of each run, Pallas kernels for 7% -> 4%
where the time goes in v2:
time: 159 us; the launch traced here: 158 us
  starting transfers between devices  54.3 us (34%)
  Pallas kernels  40.1 us (25%)
  waiting for transfers between devices  29.5 us (19%)
  blocking collectives  26.4 us (17%)
  local copies, waits for them, and re-layouts  6.51 us (4%)
    all_to_all x1, starting transfers between devices, local(): arrived = lax.all_to_all(outgoing, 'shard', 0, 0, tiled=True)  31 us
    all_to_all x1, blocking collectives, local(): back = lax.all_to_all(visited, 'shard', 0, 0, tiled=True)  26.4 us
    ppermute x14, starting transfers between devices, turn(): return lax.ppermute(value, 'shard', pairs)  23.3 us
    pallas_call x1, Pallas kernels, score(): pl.pallas_call(score_kernel, name='score', grid=(count // slots,), out_sh...  21.5 us
    ppermute x14, waiting for transfers between devices, turn(): return lax.ppermute(value, 'shard', pairs)  21.2 us
    all_to_all x1, waiting for transfers between devices, local(): arrived = lax.all_to_all(outgoing, 'shard', 0, 0, tiled=True)  8.31 us
    pallas_call x1, Pallas kernels, prepare(): pl.pallas_call(functools.partial(prepare_kernel, store_rows, device_count...  6.98 us
    pallas_call x1, Pallas kernels, decode(): pl.pallas_call(decode_kernel, name='decode', out_shape=jax.ShapeDtypeStru...  6.31 us
  transfers between devices with their start and end apart: 15, of which 10 were waited for; matrix products, arithmetic and copies ran while one was open for 1% of the time, Pallas kernels for 4%

profile of v2, /device:TPU:33, one launch (start us, length us, event | category | flops | bytes accessed | tf_op | source)
XLA Modules:
  0.0 158.0 jit_solution(7622194193543048100)
XLA Ops:
  0.0 1.4 copy.12.cand_ref
  1.4 1.3 copy.13.count_ref
  2.7 7.0 %prepare.1 = (bf16[128,40,128]{2,1,0:T(8,128)(2,1)}, f32[32,24]{1,0:T(8,128)}, f32[32,24]{1,0:T(8,128)}, s32[4]{0:T(128)}) custom-call(s32[32,24]{1,0:T(8,128)} %copy.12.cand_ref, s32[32,1]{1,0:T(8,128)} %copy.13.count_ref, s32[32,128]{1,0:T(8,128)} %bitcast.45, bf16[32,32,128]{2,1,0:T(8,128)(2,1)} %query_ref.1), custom_call_target="tpu_custom_call" | custom-call | flops 1000000000 | bytes 2000000 | tf_op jit(solution)/shard_map/prepare/pallas_call | solution.py:111
  9.7 31.0 %all-to-all-start = ((bf16[128,40,128]{2,1,0:T(8,128)(2,1)}), bf16[128,40,128]{2,1,0:T(8,128)(2,1)S(1)}, u32[]{:S(2)}, u32[]{:S(2)}) async-start(bf16[128,40,128]{2,1,0:T(8,128)(2,1)} %get-tuple-element.12), calls=%async_computation | async-start | bytes 2621440 | tf_op jit(solution)/shard_map/all_to_all | solution.py:325
  40.7 6.3 %decode.1.store_ref = bf16[8,4,128,128]{3,2,1,0:T(8,128)(2,1)} custom-call(s32[1]{0:T(128)} %bitcast.2.seat_ref, s32[32]{0:T(128)} %length_ref.1, f32[4]{0:T(128)} %level_ref.1, bf16[32,128,128]{2,1,0:T(8,128)(2,1)} %base_ref.1, s32[32,128,128]{2,1,0:T(8,128)} %code_ref.1), custom_call_target="tpu_custom_call" | custom-call | flops 10485760 | bytes 4194304 | tf_op jit(solution)/shard_map/decode/pallas_call | solution.py:160
  47.0 1.3 slice_bitcast_fusion.1
  48.4 2.6 %collective-permute-start = (bf16[4,128,128]{2,1,0:T(8,128)(2,1)S(1)}, bf16[4,128,128]{2,1,0:T(8,128)(2,1)S(1)}, u32[]{:S(2)}, u32[]{:S(2)}) collective-permute-start(bf16[4,128,128]{2,1,0:T(8,128)(2,1)S(1)} %get-tuple-element.19), channel_id=1, source_target_pairs={{0,7},{1,0},{2,1},{3,2},{4,3},{5,4},{6,5},{7,6},{8,15},{9,8},{10,9... | collective-permute-start | bytes 393224 | tf_op jit(solution)/shard_map/ppermute | solution.py:309
  51.0 0.4 collective-permute-start.1
  51.4 1.0 collective-permute-start.2
  52.4 2.4 %collective-permute-start.3 = (bf16[4,128,128]{2,1,0:T(8,128)(2,1)S(1)}, bf16[4,128,128]{2,1,0:T(8,128)(2,1)S(1)}, u32[]{:S(2)}, u32[]{:S(2)}) collective-permute-start(bf16[4,128,128]{2,1,0:T(8,128)(2,1)S(1)} %get-tuple-element.16), channel_id=1, source_target_pairs={{0,4},{1,5},{2,6},{3,7},{4,0},{5,1},{6,2},{7,3},{8,12},{9,13},{10,... | collective-permute-start | bytes 393224 | tf_op jit(solution)/shard_map/ppermute | solution.py:309
  54.8 0.7 collective-permute-start.4
  55.5 1.2 collective-permute-start.5
  56.7 3.7 %collective-permute-start.6 = (bf16[4,128,128]{2,1,0:T(8,128)(2,1)S(1)}, bf16[4,128,128]{2,1,0:T(8,128)(2,1)S(1)}, u32[]{:S(2)}, u32[]{:S(2)}) collective-permute-start(bf16[4,128,128]{2,1,0:T(8,128)(2,1)S(1)} %get-tuple-element.13), channel_id=1, source_target_pairs={{0,1},{1,2},{2,3},{3,4},{4,5},{5,6},{6,7},{7,0},{8,9},{9,10},{10,1... | collective-permute-start | bytes 393224 | tf_op jit(solution)/shard_map/ppermute | solution.py:309
  60.6 5.7 %collective-permute-done.2 = bf16[4,128,128]{2,1,0:T(8,128)(2,1)S(1)} collective-permute-done((bf16[4,128,128]{2,1,0:T(8,128)(2,1)S(1)}, bf16[4,128,128]{2,1,0:T(8,128)(2,1)S(1)}, u32[]{:S(2)}, u32[]{:S(2)}) %collective-permute-start.2) | collective-permute-done | bytes 131104 | tf_op jit(solution)/shard_map/ppermute | solution.py:309
  66.3 0.6 collective-permute-done.4
  67.1 1.9 %collective-permute-done.6 = bf16[4,128,128]{2,1,0:T(8,128)(2,1)S(1)} collective-permute-done((bf16[4,128,128]{2,1,0:T(8,128)(2,1)S(1)}, bf16[4,128,128]{2,1,0:T(8,128)(2,1)S(1)}, u32[]{:S(2)}, u32[]{:S(2)}) %collective-permute-start.6) | collective-permute-done | bytes 131104 | tf_op jit(solution)/shard_map/ppermute | solution.py:309
  69.0 1.0 fusion.6.refs_0_
  70.0 2.5 %collective-permute-start.7 = (bf16[4,128,128]{2,1,0:T(8,128)(2,1)S(1)}, bf16[4,128,128]{2,1,0:T(8,128)(2,1)S(1)}, u32[]{:S(2)}, u32[]{:S(2)}) collective-permute-start(bf16[4,128,128]{2,1,0:T(8,128)(2,1)S(1)} %fusion.6.refs_0_), channel_id=1, source_target_pairs={{0,1},{1,2},{2,3},{3,4},{4,5},{5,6},{6,7},{7,0},{8,9},{9,10},{10,1... | collective-permute-start | bytes 393224 | tf_op jit(solution)/shard_map/ppermute | solution.py:309
  72.5 1.2 collective-permute-start.8
  73.7 4.5 %collective-permute-start.9 = (bf16[4,128,128]{2,1,0:T(8,128)(2,1)S(1)}, bf16[4,128,128]{2,1,0:T(8,128)(2,1)S(1)}, u32[]{:S(2)}, u32[]{:S(2)}) collective-permute-start(bf16[4,128,128]{2,1,0:T(8,128)(2,1)S(1)} %fusion.6.refs_0_), channel_id=1, source_target_pairs={{0,3},{1,4},{2,5},{3,6},{4,7},{5,0},{6,1},{7,2},{8,11},{9,12},{10,... | collective-permute-start | bytes 393224 | tf_op jit(solution)/shard_map/ppermute | solution.py:309
  78.2 2.2 %collective-permute-start.11 = (bf16[4,128,128]{2,1,0:T(8,128)(2,1)S(1)}, bf16[4,128,128]{2,1,0:T(8,128)(2,1)S(1)}, u32[]{:S(2)}, u32[]{:S(2)}) collective-permute-start(bf16[4,128,128]{2,1,0:T(8,128)(2,1)S(1)} %fusion.6.refs_0_), channel_id=1, source_target_pairs={{0,5},{1,6},{2,7},{3,0},{4,1},{5,2},{6,3},{7,4},{8,13},{9,14},{10,... | collective-permute-start | bytes 393224 | tf_op jit(solution)/shard_map/ppermute | solution.py:309
  80.4 0.9 collective-permute-start.12
  81.3 3.6 %collective-permute-done.8.refs_2_ = bf16[4,128,128]{2,1,0:T(8,128)(2,1)S(1)} collective-permute-done((bf16[4,128,128]{2,1,0:T(8,128)(2,1)S(1)}, bf16[4,128,128]{2,1,0:T(8,128)(2,1)S(1)}, u32[]{:S(2)}, u32[]{:S(2)}) %collective-permute-start.8) | collective-permute-done | bytes 131104 | tf_op jit(solution)/shard_map/ppermute | solution.py:309
  84.9 0.5 collective-permute-done.9.refs_3_
  85.4 7.8 %collective-permute-done.10.refs_4_ = bf16[4,128,128]{2,1,0:T(8,128)(2,1)S(1)} collective-permute-done((bf16[4,128,128]{2,1,0:T(8,128)(2,1)S(1)}, bf16[4,128,128]{2,1,0:T(8,128)(2,1)S(1)}, u32[]{:S(2)}, u32[]{:S(2)}) %collective-permute-start.10) | collective-permute-done | bytes 131104 | tf_op jit(solution)/shard_map/ppermute | solution.py:309
  93.3 0.7 collective-permute-done.11.refs_5_
  94.0 8.3 %all-to-all-done.arrived_ref = bf16[128,40,128]{2,1,0:T(8,128)(2,1)S(1)} async-done(((bf16[128,40,128]{2,1,0:T(8,128)(2,1)}), bf16[128,40,128]{2,1,0:T(8,128)(2,1)S(1)}, u32[]{:S(2)}, u32[]{:S(2)}) %all-to-all-start) | async-done | bytes 1310752 | tf_op jit(solution)/shard_map/all_to_all | solution.py:325
  102.4 1.1 copy-done
  103.4 21.5 %score.1 = f32[128,64]{1,0:T(8,128)} custom-call(s32[1]{0:T(128)} %bitcast.2.seat_ref, bf16[128,40,128]{2,1,0:T(8,128)(2,1)} %copy-done, bf16[8,4,128,128]{3,2,1,0:T(8,128)(2,1)} %decode.1.store_ref, bf16[4,128,128]{2,1,0:T(8,128)(2,1)} %copy-done.1, bf16[4,128,128]{2,1,0:T(8,128)(2,1)} %copy-done.3, bf16[4,128,128]{2,1,0:T(8,128)(2,1)} %copy-done.4, ...), custom_call_target="tpu_custom_call" | custom-call | flops 5368709120 | bytes 3407872 | tf_op jit(solution)/shard_map/score/pallas_call | solution.py:225
  125.0 26.4 %all_to_all.16 = f32[128,1,64]{2,1,0:T(1,128)} all-to-all(f32[128,1,64]{2,1,0:T(1,128)} %bitcast.40), channel_id=1, replica_groups=mesh['groups'=2,'shard'=128] {'shard'}, dimensions={0} | all-to-all | bytes 65536 | tf_op jit(solution)/shard_map/all_to_all | solution.py:332
  151.3 5.2 %finish.1 = f32[32,24]{1,0:T(8,128)} custom-call(s32[4]{0:T(128)} %get-tuple-element.9.note_ref, f32[32,24]{1,0:T(8,128)} %get-tuple-element.10.holder_ref, f32[32,24]{1,0:T(8,128)} %get-tuple-element.11.row_ref, f32[128,64]{1,0:T(8,128)} %bitcast.39), custom_call_target="tpu_custom_call" | custom-call | tf_op jit(solution)/shard_map/finish/pallas_call | solution.py:295
  156.6 1.4 copy.15
  (28 shorter events, 0.3 us)
Async XLA Ops:
  9.7 92.6 %all-to-all-start = ((bf16[128,40,128]{2,1,0:T(8,128)(2,1)}), bf16[128,40,128]{2,1,0:T(8,128)(2,1)S(1)}, u32[]{:S(2)}, u32[]{:S(2)}) async-start(bf16[128,40,128]{2,1,0:T(8,128)(2,1)} %get-tuple-element.12), calls=%async_computation | async-start | bytes 2621440 | tf_op jit(solution)/shard_map/all_to_all | solution.py:325
  47.0 13.4 %copy-start.2 = (s32[4]{0:T(128)S(1)}, s32[4]{0:T(128)}, u32[]{:S(2)}) copy-start(s32[4]{0:T(128)} %get-tuple-element.9.note_ref) | copy-start | bytes 52
  48.4 7.1 %collective-permute-start = (bf16[4,128,128]{2,1,0:T(8,128)(2,1)S(1)}, bf16[4,128,128]{2,1,0:T(8,128)(2,1)S(1)}, u32[]{:S(2)}, u32[]{:S(2)}) collective-permute-start(bf16[4,128,128]{2,1,0:T(8,128)(2,1)S(1)} %get-tuple-element.19), channel_id=1, source_target_pairs={{0,7},{1,0},{2,1},{3,2},{4,3},{5,4},{6,5},{7,6},{8,15},{9,8},{10,9... | collective-permute-start | bytes 393224 | tf_op jit(solution)/shard_map/ppermute | solution.py:309
  51.0 5.7 %collective-permute-start.1 = (bf16[4,128,128]{2,1,0:T(8,128)(2,1)S(1)}, bf16[4,128,128]{2,1,0:T(8,128)(2,1)S(1)}, u32[]{:S(2)}, u32[]{:S(2)}) collective-permute-start(bf16[4,128,128]{2,1,0:T(8,128)(2,1)S(1)} %get-tuple-element.18), channel_id=1, source_target_pairs={{0,6},{1,7},{2,0},{3,1},{4,2},{5,3},{6,4},{7,5},{8,14},{9,15},{10,... | collective-permute-start | bytes 393224 | tf_op jit(solution)/shard_map/ppermute | solution.py:309
  51.4 14.9 %collective-permute-start.2 = (bf16[4,128,128]{2,1,0:T(8,128)(2,1)S(1)}, bf16[4,128,128]{2,1,0:T(8,128)(2,1)S(1)}, u32[]{:S(2)}, u32[]{:S(2)}) collective-permute-start(bf16[4,128,128]{2,1,0:T(8,128)(2,1)S(1)} %get-tuple-element.17), channel_id=1, source_target_pairs={{0,5},{1,6},{2,7},{3,0},{4,1},{5,2},{6,3},{7,4},{8,13},{9,14},{10,... | collective-permute-start | bytes 393224 | tf_op jit(solution)/shard_map/ppermute | solution.py:309
  52.4 13.9 %collective-permute-start.3 = (bf16[4,128,128]{2,1,0:T(8,128)(2,1)S(1)}, bf16[4,128,128]{2,1,0:T(8,128)(2,1)S(1)}, u32[]{:S(2)}, u32[]{:S(2)}) collective-permute-start(bf16[4,128,128]{2,1,0:T(8,128)(2,1)S(1)} %get-tuple-element.16), channel_id=1, source_target_pairs={{0,4},{1,5},{2,6},{3,7},{4,0},{5,1},{6,2},{7,3},{8,12},{9,13},{10,... | collective-permute-start | bytes 393224 | tf_op jit(solution)/shard_map/ppermute | solution.py:309
  54.8 12.1 %collective-permute-start.4 = (bf16[4,128,128]{2,1,0:T(8,128)(2,1)S(1)}, bf16[4,128,128]{2,1,0:T(8,128)(2,1)S(1)}, u32[]{:S(2)}, u32[]{:S(2)}) collective-permute-start(bf16[4,128,128]{2,1,0:T(8,128)(2,1)S(1)} %get-tuple-element.15), channel_id=1, source_target_pairs={{0,3},{1,4},{2,5},{3,6},{4,7},{5,0},{6,1},{7,2},{8,11},{9,12},{10,... | collective-permute-start | bytes 393224 | tf_op jit(solution)/shard_map/ppermute | solution.py:309
  55.5 11.6 %collective-permute-start.5 = (bf16[4,128,128]{2,1,0:T(8,128)(2,1)S(1)}, bf16[4,128,128]{2,1,0:T(8,128)(2,1)S(1)}, u32[]{:S(2)}, u32[]{:S(2)}) collective-permute-start(bf16[4,128,128]{2,1,0:T(8,128)(2,1)S(1)} %get-tuple-element.14), channel_id=1, source_target_pairs={{0,2},{1,3},{2,4},{3,5},{4,6},{5,7},{6,0},{7,1},{8,10},{9,11},{10,... | collective-permute-start | bytes 393224 | tf_op jit(solution)/shard_map/ppermute | solution.py:309
  56.7 12.3 %collective-permute-start.6 = (bf16[4,128,128]{2,1,0:T(8,128)(2,1)S(1)}, bf16[4,128,128]{2,1,0:T(8,128)(2,1)S(1)}, u32[]{:S(2)}, u32[]{:S(2)}) collective-permute-start(bf16[4,128,128]{2,1,0:T(8,128)(2,1)S(1)} %get-tuple-element.13), channel_id=1, source_target_pairs={{0,1},{1,2},{2,3},{3,4},{4,5},{5,6},{6,7},{7,0},{8,9},{9,10},{10,1... | collective-permute-start | bytes 393224 | tf_op jit(solution)/shard_map/ppermute | solution.py:309
  70.0 32.3 %copy-start.1 = (bf16[4,128,128]{2,1,0:T(8,128)(2,1)}, bf16[4,128,128]{2,1,0:T(8,128)(2,1)S(1)}, u32[]{:S(2)}) copy-start(bf16[4,128,128]{2,1,0:T(8,128)(2,1)S(1)} %fusion.6.refs_0_) | copy-start | bytes 393220
  70.0 10.4 %collective-permute-start.7 = (bf16[4,128,128]{2,1,0:T(8,128)(2,1)S(1)}, bf16[4,128,128]{2,1,0:T(8,128)(2,1)S(1)}, u32[]{:S(2)}, u32[]{:S(2)}) collective-permute-start(bf16[4,128,128]{2,1,0:T(8,128)(2,1)S(1)} %fusion.6.refs_0_), channel_id=1, source_target_pairs={{0,1},{1,2},{2,3},{3,4},{4,5},{5,6},{6,7},{7,0},{8,9},{9,10},{10,1... | collective-permute-start | bytes 393224 | tf_op jit(solution)/shard_map/ppermute | solution.py:309
  72.5 12.4 %collective-permute-start.8 = (bf16[4,128,128]{2,1,0:T(8,128)(2,1)S(1)}, bf16[4,128,128]{2,1,0:T(8,128)(2,1)S(1)}, u32[]{:S(2)}, u32[]{:S(2)}) collective-permute-start(bf16[4,128,128]{2,1,0:T(8,128)(2,1)S(1)} %fusion.6.refs_0_), channel_id=1, source_target_pairs={{0,2},{1,3},{2,4},{3,5},{4,6},{5,7},{6,0},{7,1},{8,10},{9,11},{10,... | collective-permute-start | bytes 393224 | tf_op jit(solution)/shard_map/ppermute | solution.py:309
  73.7 11.7 %collective-permute-start.9 = (bf16[4,128,128]{2,1,0:T(8,128)(2,1)S(1)}, bf16[4,128,128]{2,1,0:T(8,128)(2,1)S(1)}, u32[]{:S(2)}, u32[]{:S(2)}) collective-permute-start(bf16[4,128,128]{2,1,0:T(8,128)(2,1)S(1)} %fusion.6.refs_0_), channel_id=1, source_target_pairs={{0,3},{1,4},{2,5},{3,6},{4,7},{5,0},{6,1},{7,2},{8,11},{9,12},{10,... | collective-permute-start | bytes 393224 | tf_op jit(solution)/shard_map/ppermute | solution.py:309
  78.2 15.1 %collective-permute-start.10 = (bf16[4,128,128]{2,1,0:T(8,128)(2,1)S(1)}, bf16[4,128,128]{2,1,0:T(8,128)(2,1)S(1)}, u32[]{:S(2)}, u32[]{:S(2)}) collective-permute-start(bf16[4,128,128]{2,1,0:T(8,128)(2,1)S(1)} %fusion.6.refs_0_), channel_id=1, source_target_pairs={{0,4},{1,5},{2,6},{3,7},{4,0},{5,1},{6,2},{7,3},{8,12},{9,13},{10,... | collective-permute-start | bytes 393224 | tf_op jit(solution)/shard_map/ppermute | solution.py:309
  78.2 15.8 %collective-permute-start.11 = (bf16[4,128,128]{2,1,0:T(8,128)(2,1)S(1)}, bf16[4,128,128]{2,1,0:T(8,128)(2,1)S(1)}, u32[]{:S(2)}, u32[]{:S(2)}) collective-permute-start(bf16[4,128,128]{2,1,0:T(8,128)(2,1)S(1)} %fusion.6.refs_0_), channel_id=1, source_target_pairs={{0,5},{1,6},{2,7},{3,0},{4,1},{5,2},{6,3},{7,4},{8,13},{9,14},{10,... | collective-permute-start | bytes 393224 | tf_op jit(solution)/shard_map/ppermute | solution.py:309
  80.4 21.9 %copy-start.3 = (bf16[4,128,128]{2,1,0:T(8,128)(2,1)}, bf16[4,128,128]{2,1,0:T(8,128)(2,1)S(1)}, u32[]{:S(2)}) copy-start(bf16[4,128,128]{2,1,0:T(8,128)(2,1)S(1)} %collective-permute-done.7.refs_1_) | copy-start | bytes 393220
  80.4 13.5 %collective-permute-start.12 = (bf16[4,128,128]{2,1,0:T(8,128)(2,1)S(1)}, bf16[4,128,128]{2,1,0:T(8,128)(2,1)S(1)}, u32[]{:S(2)}, u32[]{:S(2)}) collective-permute-start(bf16[4,128,128]{2,1,0:T(8,128)(2,1)S(1)} %fusion.6.refs_0_), channel_id=1, source_target_pairs={{0,6},{1,7},{2,0},{3,1},{4,2},{5,3},{6,4},{7,5},{8,14},{9,15},{10,... | collective-permute-start | bytes 393224 | tf_op jit(solution)/shard_map/ppermute | solution.py:309
  84.9 17.4 %copy-start.4 = (bf16[4,128,128]{2,1,0:T(8,128)(2,1)}, bf16[4,128,128]{2,1,0:T(8,128)(2,1)S(1)}, u32[]{:S(2)}) copy-start(bf16[4,128,128]{2,1,0:T(8,128)(2,1)S(1)} %collective-permute-done.8.refs_2_) | copy-start | bytes 393220
  84.9 9.1 %collective-permute-start.13 = (bf16[4,128,128]{2,1,0:T(8,128)(2,1)S(1)}, bf16[4,128,128]{2,1,0:T(8,128)(2,1)S(1)}, u32[]{:S(2)}, u32[]{:S(2)}) collective-permute-start(bf16[4,128,128]{2,1,0:T(8,128)(2,1)S(1)} %fusion.6.refs_0_), channel_id=1, source_target_pairs={{0,7},{1,0},{2,1},{3,2},{4,3},{5,4},{6,5},{7,6},{8,15},{9,8},{10,9... | collective-permute-start | bytes 393224 | tf_op jit(solution)/shard_map/ppermute | solution.py:309
  85.4 16.9 %copy-start.5 = (bf16[4,128,128]{2,1,0:T(8,128)(2,1)}, bf16[4,128,128]{2,1,0:T(8,128)(2,1)S(1)}, u32[]{:S(2)}) copy-start(bf16[4,128,128]{2,1,0:T(8,128)(2,1)S(1)} %collective-permute-done.9.refs_3_) | copy-start | bytes 393220
  93.2 9.1 %copy-start.6 = (bf16[4,128,128]{2,1,0:T(8,128)(2,1)}, bf16[4,128,128]{2,1,0:T(8,128)(2,1)S(1)}, u32[]{:S(2)}) copy-start(bf16[4,128,128]{2,1,0:T(8,128)(2,1)S(1)} %collective-permute-done.10.refs_4_) | copy-start | bytes 393220
  94.0 8.4 %copy-start.7 = (bf16[4,128,128]{2,1,0:T(8,128)(2,1)}, bf16[4,128,128]{2,1,0:T(8,128)(2,1)S(1)}, u32[]{:S(2)}) copy-start(bf16[4,128,128]{2,1,0:T(8,128)(2,1)S(1)} %collective-permute-done.11.refs_5_) | copy-start | bytes 393220
  94.0 8.4 %copy-start.8 = (bf16[4,128,128]{2,1,0:T(8,128)(2,1)}, bf16[4,128,128]{2,1,0:T(8,128)(2,1)S(1)}, u32[]{:S(2)}) copy-start(bf16[4,128,128]{2,1,0:T(8,128)(2,1)S(1)} %collective-permute-done.12.refs_6_) | copy-start | bytes 393220
  94.0 8.4 %copy-start.9 = (bf16[4,128,128]{2,1,0:T(8,128)(2,1)}, bf16[4,128,128]{2,1,0:T(8,128)(2,1)S(1)}, u32[]{:S(2)}) copy-start(bf16[4,128,128]{2,1,0:T(8,128)(2,1)S(1)} %collective-permute-done.13.refs_7_) | copy-start | bytes 393220
  102.3 1.1 copy-start

commit v3 on v2

v3 whole, which is shorter than its diff:
```python
import functools

import jax
import jax.numpy as jnp
from jax import lax
from jax.experimental import pallas as pl
from jax.experimental.pallas import tpu as pltpu
from jax.sharding import PartitionSpec as P

EPSILON = 1e-06
PLANE = 8
F32 = jnp.float32
BF16 = jnp.bfloat16


def vmem(*_):
    return pl.BlockSpec(memory_space=pltpu.VMEM)


def near(value):
    return pltpu.with_memory_space_constraint(value, pltpu.VMEM)


def smem(*_):
    return pl.BlockSpec(memory_space=pltpu.SMEM)


def cost(flops, moved):
    return pl.CostEstimate(flops=flops, transcendentals=0, bytes_accessed=moved)


def log2(value):
    assert value & (value - 1) == 0
    return value.bit_length() - 1


def prepare_kernel(
    store_rows, device_count,
    cand_ref, count_ref, map_ref, query_ref,
    out_ref, holder_ref, row_ref, turned_ref, note_ref,
    present_ref, pick_vmem, pick_smem, sem,
):
    slots, queries = cand_ref.shape
    table_rows, lanes = map_ref.shape
    groups = lanes // queries
    per = slots // groups
    part_bits = log2(store_rows // PLANE)
    table = map_ref[...]
    holder_table = lax.shift_right_logical(table, log2(store_rows))
    row_table = table & (store_rows - 1)
    both = jnp.concatenate([holder_table, row_table], axis=1).astype(F32)
    both = jnp.transpose(both).astype(BF16)
    ids = cand_ref[...]
    ids = jnp.concatenate([ids[g * per : (g + 1) * per] for g in range(groups)], axis=1)
    count = jnp.concatenate([count_ref[...]] * groups, axis=1)
    high = lax.shift_right_logical(ids, log2(lanes))
    low = ids & (lanes - 1)
    lane = lax.broadcasted_iota(jnp.int32, (1, lanes), 1)
    first_slot = lax.shift_right_logical(lane, log2(queries)) * per
    table_iota = lax.broadcasted_iota(jnp.int32, (table_rows, lanes), 0)
    low_iota = lax.broadcasted_iota(jnp.int32, (lanes, lanes), 0)
    device_iota = lax.broadcasted_iota(jnp.int32, (device_count, lanes), 0)
    present = jnp.zeros((device_count, lanes), F32)
    for s in range(per):
        mark = jnp.where(table_iota == high[s : s + 1], 1.0, 0.0).astype(BF16)
        got = jnp.dot(both, mark, preferred_element_type=F32)
        here = low_iota == low[s : s + 1]
        holder = jnp.sum(jnp.where(here, got[:lanes], 0.0), axis=0, keepdims=True)
        row = jnp.sum(jnp.where(here, got[lanes:], 0.0), axis=0, keepdims=True)
        row = row.astype(jnp.int32)
        holder = jnp.where(first_slot + s < count, holder.astype(jnp.int32), -1)
        present = jnp.where(device_iota == holder, 1.0, present)
        block = (lax.shift_right_logical(row, part_bits) - holder) & (PLANE - 1)
        holder_ref[s : s + 1] = holder
        row_ref[s : s + 1] = row
        turned_ref[s : s + 1] = (block << part_bits) + (row & ((1 << part_bits) - 1))
    shift = queries
    while shift < lanes:
        present = jnp.maximum(present, pltpu.roll(present, shift, 1))
        shift *= 2
    present = jnp.where(lane < queries, present, 0.0)
    present_ref[...] = present
    kind = lax.broadcasted_iota(jnp.int32, (16, lanes), 0)
    lane_all = lax.broadcasted_iota(jnp.int32, (16, lanes), 1)
    weigh = jnp.where(kind == 0, lane_all, jnp.where(kind == 1, 1, 0))
    sums = lax.dot_general(
        weigh.astype(F32).astype(BF16), present.astype(BF16),
        (((1,), (1,)), ((), ())), preferred_element_type=F32,
    )
    device = lax.broadcasted_iota(jnp.int32, (1, device_count), 1)
    busiest = jnp.max(jnp.where(sums[1:2] > 1.5, device.astype(F32), 0.0)).astype(jnp.int32)
    theirs = present_ref[pl.ds(busiest, 1), :]
    lane_f = lane.astype(F32)
    last = jnp.max(theirs * lane_f).astype(jnp.int32)
    first = queries - 1 - jnp.max(theirs * (queries - 1 - lane_f)).astype(jnp.int32)
    middle = jnp.sum(theirs * lane_f).astype(jnp.int32) - first - last
    middle = jnp.clip(middle, 0, queries - 1)
    pick = jnp.where(device == busiest, last, sums[0:1].astype(jnp.int32))
    pick_vmem[...] = jnp.clip(pick, 0, queries - 1)
    copy = pltpu.make_async_copy(pick_vmem, pick_smem, sem)
    copy.start()
    note_ref[0] = busiest
    note_ref[1] = first
    note_ref[2] = middle
    note_ref[3] = last
    tokens = query_ref.shape[1]
    extra = 2 * tokens // PLANE
    spare = []
    for seat in range(PLANE):
        query = first if seat < PLANE // 2 else middle
        start = (seat % (PLANE // 2)) * extra
        spare.append(query_ref[query, start : start + extra, :])
    copy.wait()

    def pack(step, carry):
        for seat in range(PLANE):
            device = step * PLANE + seat
            out_ref[device, 0:tokens, :] = query_ref[pick_smem[0, device]]
            out_ref[device, tokens : tokens + extra, :] = spare[seat]
        return carry

    lax.fori_loop(0, device_count // PLANE, pack, 0)


def prepare(candidates, cand_count, placement_map, query_tokens, store_rows, device_count):
    queries, slots = candidates.shape
    _, tokens, dim = query_tokens.shape
    wide = jax.ShapeDtypeStruct((slots * queries // dim, dim), jnp.int32)
    return pl.pallas_call(
        functools.partial(prepare_kernel, store_rows, device_count),
        name="prepare",
        out_shape=(
            jax.ShapeDtypeStruct((device_count, tokens + 2 * tokens // PLANE, dim), BF16),
            wide, wide, wide,
            jax.ShapeDtypeStruct((4,), jnp.int32),
        ),
        in_specs=[vmem(), vmem(), vmem(), vmem()],
        out_specs=(vmem(), vmem(), vmem(), vmem(), smem()),
        scratch_shapes=[
            pltpu.VMEM((device_count, dim), F32),
            pltpu.VMEM((1, device_count), jnp.int32),
            pltpu.SMEM((1, device_count), jnp.int32),
            pltpu.SemaphoreType.DMA(()),
        ],
        cost_estimate=cost(10**9, 2 * 10**6),
    )(
        jnp.transpose(candidates),
        cand_count.reshape(1, queries),
        placement_map.reshape(-1, dim),
        query_tokens,
    )


def decode_kernel(seat_ref, length_ref, level_ref, base_ref, code_ref, out_ref):
    part, length, dim = base_ref.shape
    block = lax.rem(seat_ref[0] + pl.program_id(0), PLANE)
    token = lax.broadcasted_iota(jnp.int32, (length, dim), 0)
    for index in range(part):
        code = code_ref[index]
        residual = jnp.where(
            code < 2,
            jnp.where(code == 0, level_ref[0], level_ref[1]),
            jnp.where(code == 2, level_ref[2], level_ref[3]),
        )
        summed = base_ref[index].astype(F32) + residual
        inverse = lax.rsqrt(jnp.sum(summed * summed, axis=1, keepdims=True) + EPSILON)
        tokens = summed * inverse
        tokens = jnp.where(token < length_ref[block * part + index], tokens, tokens[0:1])
        out_ref[0, index] = tokens.astype(BF16)


def decode(seat, passage_base, residual_codes, passage_lengths, bucket_weights):
    rows, length, dim = passage_base.shape
    part = rows // PLANE
    spec = pl.BlockSpec(
        (part, length, dim), lambda i, seat_ref: (lax.rem(seat_ref[0] + i, PLANE), 0, 0)
    )
    return pl.pallas_call(
        decode_kernel,
        name="decode",
        out_shape=jax.ShapeDtypeStruct((PLANE, part, length, dim), BF16),
        grid_spec=pltpu.PrefetchScalarGridSpec(
            num_scalar_prefetch=1,
            grid=(PLANE,),
            in_specs=[smem(), smem(), spec, spec],
            out_specs=pl.BlockSpec((1, part, length, dim), lambda i, _: (i, 0, 0, 0)),
        ),
        cost_estimate=cost(rows * length * dim * 20, rows * length * dim * 8),
    )(seat, passage_lengths, bucket_weights, passage_base, residual_codes)


def score_kernel(arrived_ref, store_ref, *refs):
    hot_refs, (out_ref,) = refs[:PLANE], refs[PLANE:]
    count, height, dim = arrived_ref.shape
    _, part, length, _ = store_ref.shape
    rows = PLANE * part
    tokens = height * PLANE // (PLANE + 2)
    extra = height - tokens
    group = 256 // tokens
    slots = 256 // extra
    wide = 256

    def against(query, block, span):
        best = []
        for row in range(rows):
            similar = lax.dot_general(
                block(row // part, row % part), query, (((1,), (1,)), ((), ())),
                preferred_element_type=F32,
            )
            best.append(jnp.max(similar, axis=0, keepdims=True))
        best = jnp.concatenate(best, axis=0)
        first = best.astype(BF16)
        rest = best - first.astype(F32)
        second = rest.astype(BF16)
        third = (rest - second.astype(F32)).astype(BF16)
        member = lax.broadcasted_iota(jnp.int32, (wide // span, wide), 1) // span
        mine = lax.broadcasted_iota(jnp.int32, (wide // span, wide), 0)
        picks = jnp.where(member == mine, 1.0, 0.0).astype(BF16)
        total = [
            lax.dot_general(
                picks, piece, (((1,), (1,)), ((), ())), preferred_element_type=F32
            )
            for piece in (first, second, third)
        ]
        return (total[0] + total[1]) + total[2]

    def some(step, carry):
        start = pl.multiple_of(step * slots, slots)
        for inner in range(slots // group):
            here = pl.ds(start + inner * group, group)
            query = arrived_ref[here, 0:tokens, :].reshape(wide, dim)
            out_ref[here, 0:rows] = against(query, lambda k, j: store_ref[k, j], tokens)
        here = pl.ds(start, slots)
        query = arrived_ref[here, tokens:height, :].reshape(wide, dim)
        out_ref[here, rows : 2 * rows] = against(query, lambda k, j: hot_refs[k][j], extra)
        return carry

    lax.fori_loop(0, count // slots, some, 0)


def score(arrived, store, hot_parts):
    count, height, dim = arrived.shape
    _, part, length, _ = store.shape
    rows = PLANE * part
    return pl.pallas_call(
        score_kernel,
        name="score",
        compiler_params=pltpu.CompilerParams(vmem_limit_bytes=16 * 2**20),
        out_shape=pltpu.VMEM((count, 2 * rows), F32),
        in_specs=[vmem()] * (2 + PLANE),
        out_specs=vmem(),
        cost_estimate=cost(
            2 * count * height * rows * length * dim,
            2 * (count * height + 2 * rows * length) * dim,
        ),
    )(near(arrived), store, *[near(part) for part in hot_parts])


def finish_kernel(note_ref, holder_ref, row_ref, turned_ref, back_ref, out_ref):
    slots, queries = out_ref.shape
    per, lanes = holder_ref.shape
    device_count, double = back_ref.shape
    rows = double // 2
    part = rows // PLANE
    busiest = note_ref[0]
    back = jnp.transpose(back_ref[...])
    near, far = back[:rows], back[rows:]
    first = near.astype(BF16)
    rest = near - first.astype(F32)
    second = rest.astype(BF16)
    third = (rest - second.astype(F32)).astype(BF16)
    pieces = jnp.concatenate([first, second, third], axis=0)
    device_iota = lax.broadcasted_iota(jnp.int32, (device_count, lanes), 0)
    row_iota = lax.broadcasted_iota(jnp.int32, (rows, lanes), 0)
    lane = lax.broadcasted_iota(jnp.int32, (1, lanes), 1)
    query = lane & (queries - 1)
    device_lane = lax.broadcasted_iota(jnp.int32, (rows, device_count), 1)
    plane = busiest - lax.rem(busiest, PLANE)
    sums = []
    for half in range(2):
        total = jnp.zeros((rows, 1), F32)
        for seat in range(half * PLANE // 2, (half + 1) * PLANE // 2):
            mine = jnp.sum(
                jnp.where(device_lane == plane + seat, far, 0.0), axis=1, keepdims=True
            )
            if seat:
                cut = rows - seat * part
                mine = jnp.concatenate([mine[cut:], mine[:cut]], axis=0)
            total = total + mine
        sums.append(total)
    values = []
    for s in range(per):
        holder = holder_ref[s : s + 1]
        mark = jnp.where(device_iota == holder, 1.0, 0.0).astype(BF16)
        three = jnp.dot(pieces, mark, preferred_element_type=F32)
        away = (three[:rows] + three[rows : 2 * rows]) + three[2 * rows :]
        hot = (holder == busiest) & ((query == note_ref[1]) | (query == note_ref[2]))
        extra = jnp.where(query == note_ref[1], sums[0], sums[1])
        found = jnp.where(hot, extra, away)
        row = jnp.where(hot, row_ref[s : s + 1], turned_ref[s : s + 1])
        value = jnp.sum(jnp.where(row_iota == row, found, 0.0), axis=0, keepdims=True)
        values.append(jnp.where(holder >= 0, value, 0.0))
    values = jnp.concatenate(values, axis=0)
    for g in range(slots // per):
        out_ref[g * per : (g + 1) * per, :] = values[:, g * queries : (g + 1) * queries]


def finish(note, holder, row, turned, back, slots, queries):
    return pl.pallas_call(
        finish_kernel,
        name="finish",
        out_shape=jax.ShapeDtypeStruct((slots, queries), F32),
        in_specs=[smem(), vmem(), vmem(), vmem(), vmem()],
        out_specs=vmem(),
    )(note, holder, row, turned, near(back))


def turn(value, hop, planes):
    pairs = [
        (p * PLANE + s, p * PLANE + (s + hop) % PLANE)
        for p in range(planes) for s in range(PLANE)
    ]
    return lax.ppermute(value, "shard", pairs)


def local(
    query_tokens, candidates, cand_count, placement_map,
    passage_base, residual_codes, passage_lengths, bucket_weights,
):
    device_count = lax.axis_size("shard")
    planes = device_count // PLANE
    seat = lax.rem(lax.axis_index("shard"), PLANE).astype(jnp.int32).reshape(1)
    store_rows = passage_base.shape[0]
    store = decode(seat, passage_base, residual_codes, passage_lengths, bucket_weights)
    parts = [store[0]] + [turn(store[k], k, planes) for k in range(1, PLANE)]
    outgoing, holder, row, turned, note = prepare(
        candidates, cand_count, placement_map, query_tokens, store_rows, device_count
    )
    arrived = lax.all_to_all(outgoing, "shard", 0, 0, tiled=True)
    wanted = lax.rem(seat[0] - lax.rem(note[0], PLANE) + PLANE, PLANE)
    piece = parts[0]
    for k in range(1, PLANE):
        piece = jnp.where(wanted == k, parts[k], piece)
    hot_parts = [piece] + [turn(piece, -k, planes) for k in range(1, PLANE)]
    visited = score(arrived, store, hot_parts)
    back = lax.all_to_all(visited, "shard", 0, 0, tiled=True)
    queries, slots = candidates.shape
    return jnp.transpose(finish(note, holder, row, turned, back, slots, queries))


def solution(mesh):
    whole = P(("groups", "shard"))
    return jax.shard_map(
        local,
        mesh=mesh,
        in_specs=(whole, whole, whole, P("groups"), whole, whole, whole, P("groups")),
        out_specs=whole,
        check_vma=False,
    )
```

time: 159 us -> 140 us (0.88)
  Pallas kernels: 40.1 us -> 27.2 us
  local copies, waits for them, and re-layouts: 6.51 us -> 1.4 us
    pallas_call x1, Pallas kernels: 21.5 us -> 15.3 us  [score(): pl.pallas_call(score_kernel, name='score', compiler_params=pltpu.Compiler...]
    pallas_call x1, Pallas kernels: 5.23 us -> 1.81 us  [finish(): pl.pallas_call(finish_kernel, name='finish', out_shape=jax.ShapeDtypeStru...]
    pallas_call x1, Pallas kernels: 6.98 us -> 3.79 us  [prepare(): pl.pallas_call(functools.partial(prepare_kernel, store_rows, device_count...]
    unnamed x21 -> x4, local copies, waits for them, and re-layouts: 2.47 us -> 0.01 us
  transfers between devices with their start and end apart: 15 -> 15, of which waited for: 10 -> 9; matrix products, arithmetic and copies ran while one was open for 1% -> 1% of each run, Pallas kernels for 4% -> 5%
where the time goes in v3:
time: 140 us
  starting transfers between devices  55.2 us (39%)
  waiting for transfers between devices  29.5 us (21%)
  Pallas kernels  27.2 us (19%)
  blocking collectives  26.3 us (19%)
    all_to_all x1, starting transfers between devices, local(): arrived = lax.all_to_all(outgoing, 'shard', 0, 0, tiled=True)  31 us
    all_to_all x1, blocking collectives, local(): back = lax.all_to_all(visited, 'shard', 0, 0, tiled=True)  26.3 us
    ppermute x14, starting transfers between devices, turn(): return lax.ppermute(value, 'shard', pairs)  24.2 us
    ppermute x14, waiting for transfers between devices, turn(): return lax.ppermute(value, 'shard', pairs)  20.3 us
    pallas_call x1, Pallas kernels, score(): pl.pallas_call(score_kernel, name='score', compiler_params=pltpu.Compiler...  15.3 us
    all_to_all x1, waiting for transfers between devices, local(): arrived = lax.all_to_all(outgoing, 'shard', 0, 0, tiled=True)  9.23 us
    pallas_call x1, Pallas kernels, decode(): pl.pallas_call(decode_kernel, name='decode', out_shape=jax.ShapeDtypeStru...  6.3 us
    pallas_call x1, Pallas kernels, prepare(): pl.pallas_call(functools.partial(prepare_kernel, store_rows, device_count...  3.79 us
  transfers between devices with their start and end apart: 15, of which 9 were waited for; matrix products, arithmetic and copies ran while one was open for 1% of the time, Pallas kernels for 5%

profile of v3, /device:TPU:33, one launch (start us, length us, event | category | flops | bytes accessed | tf_op | source)
XLA Modules:
  0.0 139.7 jit_solution(907680413764838699)
XLA Ops:
  0.0 3.8 %prepare.1 = (bf16[128,40,128]{2,1,0:T(8,128)(2,1)}, s32[6,128]{1,0:T(8,128)}, s32[6,128]{1,0:T(8,128)}, s32[6,128]{1,0:T(8,128)}, s32[4]{0:T(128)}) custom-call(s32[24,32]{1,0:T(8,128)} %bitcast.47, s32[1,32]{1,0:T(1,128)} %bitcast.48, s32[32,128]{1,0:T(8,128)} %bitcast.46, bf16[32,32,128]{2,1,0:T(8,128)(2,1)} %query_ref.1), custom_call_target="tpu_custom_call" | custom-call | flops 1000000000 | bytes 2000000 | tf_op jit(solution)/shard_map/prepare/pallas_call | solution.py:129
  3.8 31.0 %all-to-all-start = ((bf16[128,40,128]{2,1,0:T(8,128)(2,1)}), bf16[128,40,128]{2,1,0:T(8,128)(2,1)S(1)}, u32[]{:S(2)}, u32[]{:S(2)}) async-start(bf16[128,40,128]{2,1,0:T(8,128)(2,1)} %get-tuple-element.14), calls=%async_computation | async-start | bytes 2621440 | tf_op jit(solution)/shard_map/all_to_all | solution.py:339
  34.8 6.3 %decode.1.store_ref = bf16[8,4,128,128]{3,2,1,0:T(8,128)(2,1)} custom-call(s32[1]{0:T(128)} %bitcast.3.seat_ref, s32[32]{0:T(128)} %length_ref.1, f32[4]{0:T(128)} %level_ref.1, bf16[32,128,128]{2,1,0:T(8,128)(2,1)} %base_ref.1, s32[32,128,128]{2,1,0:T(8,128)} %code_ref.1), custom_call_target="tpu_custom_call" | custom-call | flops 10485760 | bytes 4194304 | tf_op jit(solution)/shard_map/decode/pallas_call | solution.py:178
  41.1 1.4 slice_bitcast_fusion.1
  42.5 2.6 %collective-permute-start = (bf16[4,128,128]{2,1,0:T(8,128)(2,1)S(1)}, bf16[4,128,128]{2,1,0:T(8,128)(2,1)S(1)}, u32[]{:S(2)}, u32[]{:S(2)}) collective-permute-start(bf16[4,128,128]{2,1,0:T(8,128)(2,1)S(1)} %get-tuple-element.21), channel_id=1, source_target_pairs={{0,7},{1,0},{2,1},{3,2},{4,3},{5,4},{6,5},{7,6},{8,15},{9,8},{10,9... | collective-permute-start | bytes 393224 | tf_op jit(solution)/shard_map/ppermute | solution.py:323
  45.1 0.4 collective-permute-start.1
  45.5 1.0 collective-permute-start.2
  46.5 2.4 %collective-permute-start.3 = (bf16[4,128,128]{2,1,0:T(8,128)(2,1)S(1)}, bf16[4,128,128]{2,1,0:T(8,128)(2,1)S(1)}, u32[]{:S(2)}, u32[]{:S(2)}) collective-permute-start(bf16[4,128,128]{2,1,0:T(8,128)(2,1)S(1)} %get-tuple-element.18), channel_id=1, source_target_pairs={{0,4},{1,5},{2,6},{3,7},{4,0},{5,1},{6,2},{7,3},{8,12},{9,13},{10,... | collective-permute-start | bytes 393224 | tf_op jit(solution)/shard_map/ppermute | solution.py:323
  48.9 0.7 collective-permute-start.4
  49.6 0.0 collective-permute-done
  49.6 1.2 collective-permute-start.5
  50.8 0.0 collective-permute-done.1
  50.8 3.8 %collective-permute-start.6 = (bf16[4,128,128]{2,1,0:T(8,128)(2,1)S(1)}, bf16[4,128,128]{2,1,0:T(8,128)(2,1)}, u32[]{:S(2)}, u32[]{:S(2)}) collective-permute-start(bf16[4,128,128]{2,1,0:T(8,128)(2,1)S(1)} %get-tuple-element.15), channel_id=1, source_target_pairs={{0,1},{1,2},{2,3},{3,4},{4,5},{5,6},{6,7},{7,0},{8,9},{9,10},{10,1... | collective-permute-start | bytes 393224 | tf_op jit(solution)/shard_map/ppermute | solution.py:323
  54.7 5.7 %collective-permute-done.2 = bf16[4,128,128]{2,1,0:T(8,128)(2,1)S(1)} collective-permute-done((bf16[4,128,128]{2,1,0:T(8,128)(2,1)S(1)}, bf16[4,128,128]{2,1,0:T(8,128)(2,1)S(1)}, u32[]{:S(2)}, u32[]{:S(2)}) %collective-permute-start.2) | collective-permute-done | bytes 131104 | tf_op jit(solution)/shard_map/ppermute | solution.py:323
  60.4 0.6 collective-permute-done.4
  61.0 0.3 collective-permute-done.5
  61.3 1.8 %collective-permute-done.6 = bf16[4,128,128]{2,1,0:T(8,128)(2,1)} collective-permute-done((bf16[4,128,128]{2,1,0:T(8,128)(2,1)S(1)}, bf16[4,128,128]{2,1,0:T(8,128)(2,1)}, u32[]{:S(2)}, u32[]{:S(2)}) %collective-permute-start.6) | collective-permute-done | bytes 131104 | tf_op jit(solution)/shard_map/ppermute | solution.py:323
  63.1 0.1 fusion.6.refs_0_
  63.2 4.0 %collective-permute-start.7 = (bf16[4,128,128]{2,1,0:T(8,128)(2,1)S(1)}, bf16[4,128,128]{2,1,0:T(8,128)(2,1)S(1)}, u32[]{:S(2)}, u32[]{:S(2)}) collective-permute-start(bf16[4,128,128]{2,1,0:T(8,128)(2,1)S(1)} %fusion.6.refs_0_), channel_id=1, source_target_pairs={{0,7},{1,0},{2,1},{3,2},{4,3},{5,4},{6,5},{7,6},{8,15},{9,8},{10,9... | collective-permute-start | bytes 393224 | tf_op jit(solution)/shard_map/ppermute | solution.py:323
  67.2 3.8 %collective-permute-start.8 = (bf16[4,128,128]{2,1,0:T(8,128)(2,1)S(1)}, bf16[4,128,128]{2,1,0:T(8,128)(2,1)S(1)}, u32[]{:S(2)}, u32[]{:S(2)}) collective-permute-start(bf16[4,128,128]{2,1,0:T(8,128)(2,1)S(1)} %fusion.6.refs_0_), channel_id=1, source_target_pairs={{0,6},{1,7},{2,0},{3,1},{4,2},{5,3},{6,4},{7,5},{8,14},{9,15},{10,... | collective-permute-start | bytes 393224 | tf_op jit(solution)/shard_map/ppermute | solution.py:323
  71.0 0.2 collective-permute-start.9
  71.1 3.4 %collective-permute-start.11 = (bf16[4,128,128]{2,1,0:T(8,128)(2,1)S(1)}, bf16[4,128,128]{2,1,0:T(8,128)(2,1)S(1)}, u32[]{:S(2)}, u32[]{:S(2)}) collective-permute-start(bf16[4,128,128]{2,1,0:T(8,128)(2,1)S(1)} %fusion.6.refs_0_), channel_id=1, source_target_pairs={{0,3},{1,4},{2,5},{3,6},{4,7},{5,0},{6,1},{7,2},{8,11},{9,12},{10,... | collective-permute-start | bytes 393224 | tf_op jit(solution)/shard_map/ppermute | solution.py:323
  74.5 0.6 collective-permute-start.12
  75.1 1.3 collective-permute-done.8.refs_2_
  76.3 0.2 collective-permute-start.13
  76.6 7.9 %collective-permute-done.9.refs_3_ = bf16[4,128,128]{2,1,0:T(8,128)(2,1)S(1)} collective-permute-done((bf16[4,128,128]{2,1,0:T(8,128)(2,1)S(1)}, bf16[4,128,128]{2,1,0:T(8,128)(2,1)S(1)}, u32[]{:S(2)}, u32[]{:S(2)}) %collective-permute-start.9) | collective-permute-done | bytes 131104 | tf_op jit(solution)/shard_map/ppermute | solution.py:323
  84.5 2.3 %collective-permute-done.11.refs_5_ = bf16[4,128,128]{2,1,0:T(8,128)(2,1)S(1)} collective-permute-done((bf16[4,128,128]{2,1,0:T(8,128)(2,1)S(1)}, bf16[4,128,128]{2,1,0:T(8,128)(2,1)S(1)}, u32[]{:S(2)}, u32[]{:S(2)}) %collective-permute-start.11) | collective-permute-done | bytes 131104 | tf_op jit(solution)/shard_map/ppermute | solution.py:323
  86.8 0.3 collective-permute-done.12.refs_6_
  87.2 9.2 %all-to-all-done.arrived_ref = bf16[128,40,128]{2,1,0:T(8,128)(2,1)S(1)} async-done(((bf16[128,40,128]{2,1,0:T(8,128)(2,1)}), bf16[128,40,128]{2,1,0:T(8,128)(2,1)S(1)}, u32[]{:S(2)}, u32[]{:S(2)}) %all-to-all-start) | async-done | bytes 1310752 | tf_op jit(solution)/shard_map/all_to_all | solution.py:339
  96.4 15.3 %score.1 = f32[128,64]{1,0:T(8,128)S(1)} custom-call(bf16[128,40,128]{2,1,0:T(8,128)(2,1)S(1)} %all-to-all-done.arrived_ref, bf16[8,4,128,128]{3,2,1,0:T(8,128)(2,1)S(1)} %copy-done, bf16[4,128,128]{2,1,0:T(8,128)(2,1)S(1)} %fusion.6.refs_0_, bf16[4,128,128]{2,1,0:T(8,128)(2,1)S(1)} %collective-permute-done.7.refs_1_, ...), custom_call_target="tpu_custom_call" | custom-call | flops 5368709120 | bytes 3407872 | tf_op jit(solution)/shard_map/score/pallas_call | solution.py:245
  111.7 26.3 %all_to_all.16 = f32[128,1,64]{2,1,0:T(1,128)S(1)} all-to-all(f32[128,1,64]{2,1,0:T(1,128)S(1)} %bitcast.42), channel_id=1, replica_groups=mesh['groups'=2,'shard'=128] {'shard'}, dimensions={0} | all-to-all | bytes 65536 | tf_op jit(solution)/shard_map/all_to_all | solution.py:346
  137.9 1.8 %finish.1 = f32[24,32]{1,0:T(8,128)} custom-call(s32[4]{0:T(128)} %get-tuple-element.10.note_ref, s32[6,128]{1,0:T(8,128)} %get-tuple-element.11.holder_ref, s32[6,128]{1,0:T(8,128)} %get-tuple-element.12.row_ref, s32[6,128]{1,0:T(8,128)} %get-tuple-element.13.turned_ref, f32[128,64]{1,0:T(8,128)S(1)} %bitcast.41), custom_call_target="tpu_custom_call" | custom-call | tf_op jit(solution)/shard_map/finish/pallas_call | solution.py:309
  (9 shorter events, 0.0 us)
Async XLA Ops:
  3.8 92.6 %all-to-all-start = ((bf16[128,40,128]{2,1,0:T(8,128)(2,1)}), bf16[128,40,128]{2,1,0:T(8,128)(2,1)S(1)}, u32[]{:S(2)}, u32[]{:S(2)}) async-start(bf16[128,40,128]{2,1,0:T(8,128)(2,1)} %get-tuple-element.14), calls=%async_computation | async-start | bytes 2621440 | tf_op jit(solution)/shard_map/all_to_all | solution.py:339
  41.1 13.5 %copy-start.1 = (s32[4]{0:T(128)S(1)}, s32[4]{0:T(128)}, u32[]{:S(2)}) copy-start(s32[4]{0:T(128)} %get-tuple-element.10.note_ref) | copy-start | bytes 52
  41.1 22.0 %copy-start = (bf16[8,4,128,128]{3,2,1,0:T(8,128)(2,1)S(1)}, bf16[8,4,128,128]{3,2,1,0:T(8,128)(2,1)}, u32[]{:S(2)}) copy-start(bf16[8,4,128,128]{3,2,1,0:T(8,128)(2,1)} %decode.1.store_ref) | copy-start | bytes 3145732
  42.5 7.1 %collective-permute-start = (bf16[4,128,128]{2,1,0:T(8,128)(2,1)S(1)}, bf16[4,128,128]{2,1,0:T(8,128)(2,1)S(1)}, u32[]{:S(2)}, u32[]{:S(2)}) collective-permute-start(bf16[4,128,128]{2,1,0:T(8,128)(2,1)S(1)} %get-tuple-element.21), channel_id=1, source_target_pairs={{0,7},{1,0},{2,1},{3,2},{4,3},{5,4},{6,5},{7,6},{8,15},{9,8},{10,9... | collective-permute-start | bytes 393224 | tf_op jit(solution)/shard_map/ppermute | solution.py:323
  45.1 5.7 %collective-permute-start.1 = (bf16[4,128,128]{2,1,0:T(8,128)(2,1)S(1)}, bf16[4,128,128]{2,1,0:T(8,128)(2,1)S(1)}, u32[]{:S(2)}, u32[]{:S(2)}) collective-permute-start(bf16[4,128,128]{2,1,0:T(8,128)(2,1)S(1)} %get-tuple-element.20), channel_id=1, source_target_pairs={{0,6},{1,7},{2,0},{3,1},{4,2},{5,3},{6,4},{7,5},{8,14},{9,15},{10,... | collective-permute-start | bytes 393224 | tf_op jit(solution)/shard_map/ppermute | solution.py:323
  45.5 14.9 %collective-permute-start.2 = (bf16[4,128,128]{2,1,0:T(8,128)(2,1)S(1)}, bf16[4,128,128]{2,1,0:T(8,128)(2,1)S(1)}, u32[]{:S(2)}, u32[]{:S(2)}) collective-permute-start(bf16[4,128,128]{2,1,0:T(8,128)(2,1)S(1)} %get-tuple-element.19), channel_id=1, source_target_pairs={{0,5},{1,6},{2,7},{3,0},{4,1},{5,2},{6,3},{7,4},{8,13},{9,14},{10,... | collective-permute-start | bytes 393224 | tf_op jit(solution)/shard_map/ppermute | solution.py:323
  46.5 13.9 %collective-permute-start.3 = (bf16[4,128,128]{2,1,0:T(8,128)(2,1)S(1)}, bf16[4,128,128]{2,1,0:T(8,128)(2,1)S(1)}, u32[]{:S(2)}, u32[]{:S(2)}) collective-permute-start(bf16[4,128,128]{2,1,0:T(8,128)(2,1)S(1)} %get-tuple-element.18), channel_id=1, source_target_pairs={{0,4},{1,5},{2,6},{3,7},{4,0},{5,1},{6,2},{7,3},{8,12},{9,13},{10,... | collective-permute-start | bytes 393224 | tf_op jit(solution)/shard_map/ppermute | solution.py:323
  48.9 12.1 %collective-permute-start.4 = (bf16[4,128,128]{2,1,0:T(8,128)(2,1)S(1)}, bf16[4,128,128]{2,1,0:T(8,128)(2,1)}, u32[]{:S(2)}, u32[]{:S(2)}) collective-permute-start(bf16[4,128,128]{2,1,0:T(8,128)(2,1)S(1)} %get-tuple-element.17), channel_id=1, source_target_pairs={{0,3},{1,4},{2,5},{3,6},{4,7},{5,0},{6,1},{7,2},{8,11},{9,12},{10,... | collective-permute-start | bytes 393224 | tf_op jit(solution)/shard_map/ppermute | solution.py:323
  49.6 11.7 %collective-permute-start.5 = (bf16[4,128,128]{2,1,0:T(8,128)(2,1)S(1)}, bf16[4,128,128]{2,1,0:T(8,128)(2,1)}, u32[]{:S(2)}, u32[]{:S(2)}) collective-permute-start(bf16[4,128,128]{2,1,0:T(8,128)(2,1)S(1)} %get-tuple-element.16), channel_id=1, source_target_pairs={{0,2},{1,3},{2,4},{3,5},{4,6},{5,7},{6,0},{7,1},{8,10},{9,11},{10,... | collective-permute-start | bytes 393224 | tf_op jit(solution)/shard_map/ppermute | solution.py:323
  50.8 12.3 %collective-permute-start.6 = (bf16[4,128,128]{2,1,0:T(8,128)(2,1)S(1)}, bf16[4,128,128]{2,1,0:T(8,128)(2,1)}, u32[]{:S(2)}, u32[]{:S(2)}) collective-permute-start(bf16[4,128,128]{2,1,0:T(8,128)(2,1)S(1)} %get-tuple-element.15), channel_id=1, source_target_pairs={{0,1},{1,2},{2,3},{3,4},{4,5},{5,6},{6,7},{7,0},{8,9},{9,10},{10,1... | collective-permute-start | bytes 393224 | tf_op jit(solution)/shard_map/ppermute | solution.py:323
  63.2 11.3 %collective-permute-start.7 = (bf16[4,128,128]{2,1,0:T(8,128)(2,1)S(1)}, bf16[4,128,128]{2,1,0:T(8,128)(2,1)S(1)}, u32[]{:S(2)}, u32[]{:S(2)}) collective-permute-start(bf16[4,128,128]{2,1,0:T(8,128)(2,1)S(1)} %fusion.6.refs_0_), channel_id=1, source_target_pairs={{0,7},{1,0},{2,1},{3,2},{4,3},{5,4},{6,5},{7,6},{8,15},{9,8},{10,9... | collective-permute-start | bytes 393224 | tf_op jit(solution)/shard_map/ppermute | solution.py:323
  67.2 9.2 %collective-permute-start.8 = (bf16[4,128,128]{2,1,0:T(8,128)(2,1)S(1)}, bf16[4,128,128]{2,1,0:T(8,128)(2,1)S(1)}, u32[]{:S(2)}, u32[]{:S(2)}) collective-permute-start(bf16[4,128,128]{2,1,0:T(8,128)(2,1)S(1)} %fusion.6.refs_0_), channel_id=1, source_target_pairs={{0,6},{1,7},{2,0},{3,1},{4,2},{5,3},{6,4},{7,5},{8,14},{9,15},{10,... | collective-permute-start | bytes 393224 | tf_op jit(solution)/shard_map/ppermute | solution.py:323
  71.0 13.5 %collective-permute-start.9 = (bf16[4,128,128]{2,1,0:T(8,128)(2,1)S(1)}, bf16[4,128,128]{2,1,0:T(8,128)(2,1)S(1)}, u32[]{:S(2)}, u32[]{:S(2)}) collective-permute-start(bf16[4,128,128]{2,1,0:T(8,128)(2,1)S(1)} %fusion.6.refs_0_), channel_id=1, source_target_pairs={{0,5},{1,6},{2,7},{3,0},{4,1},{5,2},{6,3},{7,4},{8,13},{9,14},{10,... | collective-permute-start | bytes 393224 | tf_op jit(solution)/shard_map/ppermute | solution.py:323
  71.1 13.4 %collective-permute-start.10 = (bf16[4,128,128]{2,1,0:T(8,128)(2,1)S(1)}, bf16[4,128,128]{2,1,0:T(8,128)(2,1)S(1)}, u32[]{:S(2)}, u32[]{:S(2)}) collective-permute-start(bf16[4,128,128]{2,1,0:T(8,128)(2,1)S(1)} %fusion.6.refs_0_), channel_id=1, source_target_pairs={{0,4},{1,5},{2,6},{3,7},{4,0},{5,1},{6,2},{7,3},{8,12},{9,13},{10,... | collective-permute-start | bytes 393224 | tf_op jit(solution)/shard_map/ppermute | solution.py:323
  71.1 15.7 %collective-permute-start.11 = (bf16[4,128,128]{2,1,0:T(8,128)(2,1)S(1)}, bf16[4,128,128]{2,1,0:T(8,128)(2,1)S(1)}, u32[]{:S(2)}, u32[]{:S(2)}) collective-permute-start(bf16[4,128,128]{2,1,0:T(8,128)(2,1)S(1)} %fusion.6.refs_0_), channel_id=1, source_target_pairs={{0,3},{1,4},{2,5},{3,6},{4,7},{5,0},{6,1},{7,2},{8,11},{9,12},{10,... | collective-permute-start | bytes 393224 | tf_op jit(solution)/shard_map/ppermute | solution.py:323
  74.5 12.6 %collective-permute-start.12 = (bf16[4,128,128]{2,1,0:T(8,128)(2,1)S(1)}, bf16[4,128,128]{2,1,0:T(8,128)(2,1)S(1)}, u32[]{:S(2)}, u32[]{:S(2)}) collective-permute-start(bf16[4,128,128]{2,1,0:T(8,128)(2,1)S(1)} %fusion.6.refs_0_), channel_id=1, source_target_pairs={{0,2},{1,3},{2,4},{3,5},{4,6},{5,7},{6,0},{7,1},{8,10},{9,11},{10,... | collective-permute-start | bytes 393224 | tf_op jit(solution)/shard_map/ppermute | solution.py:323
  76.3 10.8 %collective-permute-start.13 = (bf16[4,128,128]{2,1,0:T(8,128)(2,1)S(1)}, bf16[4,128,128]{2,1,0:T(8,128)(2,1)S(1)}, u32[]{:S(2)}, u32[]{:S(2)}) collective-permute-start(bf16[4,128,128]{2,1,0:T(8,128)(2,1)S(1)} %fusion.6.refs_0_), channel_id=1, source_target_pairs={{0,1},{1,2},{2,3},{3,4},{4,5},{5,6},{6,7},{7,0},{8,9},{9,10},{10,1... | collective-permute-start | bytes 393224 | tf_op jit(solution)/shard_map/ppermute | solution.py:323

commit v4 on v3

--- a/solution.py
+++ b/solution.py
@@ -38,8 +38,10 @@
     store_rows, device_count,
     cand_ref, count_ref, map_ref, query_ref,
     out_ref, holder_ref, row_ref, turned_ref, note_ref,
-    present_ref, pick_vmem, pick_smem, sem,
+    present_ref, pick_vmem, pick_smem, sem, tokens_ref, packed_ref, in_sem, out_sem,
 ):
+    load = pltpu.make_async_copy(query_ref, tokens_ref, in_sem)
+    load.start()
     slots, queries = cand_ref.shape
     table_rows, lanes = map_ref.shape
     groups = lanes // queries
@@ -105,21 +107,32 @@
     note_ref[3] = last
     tokens = query_ref.shape[1]
     extra = 2 * tokens // PLANE
+    load.wait()
     spare = []
     for seat in range(PLANE):
         query = first if seat < PLANE // 2 else middle
         start = (seat % (PLANE // 2)) * extra
-        spare.append(query_ref[query, start : start + extra, :])
+        spare.append(tokens_ref[query, start : start + extra, :])
     copy.wait()
-
-    def pack(step, carry):
-        for seat in range(PLANE):
-            device = step * PLANE + seat
-            out_ref[device, 0:tokens, :] = query_ref[pick_smem[0, device]]
-            out_ref[device, tokens : tokens + extra, :] = spare[seat]
-        return carry
-
-    lax.fori_loop(0, device_count // PLANE, pack, 0)
+    chunks = 4
+    size = device_count // chunks
+    stores = []
+    for chunk in range(chunks):
+
+        def pack(step, carry):
+            for seat in range(PLANE):
+                device = chunk * size + step * PLANE + seat
+                packed_ref[device, 0:tokens, :] = tokens_ref[pick_smem[0, device]]
+                packed_ref[device, tokens : tokens + extra, :] = spare[seat]
+            return carry
+
+        lax.fori_loop(0, size // PLANE, pack, 0)
+        here = pl.ds(chunk * size, size)
+        store = pltpu.make_async_copy(packed_ref.at[here], out_ref.at[here], out_sem.at[chunk])
+        store.start()
+        stores.append(store)
+    for store in stores:
+        store.wait()
 
 
 def prepare(candidates, cand_count, placement_map, query_tokens, store_rows, device_count):
@@ -134,13 +147,17 @@
             wide, wide, wide,
             jax.ShapeDtypeStruct((4,), jnp.int32),
         ),
-        in_specs=[vmem(), vmem(), vmem(), vmem()],
-        out_specs=(vmem(), vmem(), vmem(), vmem(), smem()),
+        in_specs=[vmem(), vmem(), vmem(), pl.BlockSpec(memory_space=pl.ANY)],
+        out_specs=(pl.BlockSpec(memory_space=pl.ANY), vmem(), vmem(), vmem(), smem()),
         scratch_shapes=[
             pltpu.VMEM((device_count, dim), F32),
             pltpu.VMEM((1, device_count), jnp.int32),
             pltpu.SMEM((1, device_count), jnp.int32),
             pltpu.SemaphoreType.DMA(()),
+            pltpu.VMEM((queries, tokens, dim), BF16),
+            pltpu.VMEM((device_count, tokens + 2 * tokens // PLANE, dim), BF16),
+            pltpu.SemaphoreType.DMA(()),
+            pltpu.SemaphoreType.DMA((4,)),
         ],
         cost_estimate=cost(10**9, 2 * 10**6),
     )(
@@ -190,7 +207,7 @@
 
 
 def score_kernel(arrived_ref, store_ref, *refs):
-    hot_refs, (out_ref,) = refs[:PLANE], refs[PLANE:]
+    hot_refs, (out_ref, best_ref) = refs[:PLANE], refs[PLANE:]
     count, height, dim = arrived_ref.shape
     _, part, length, _ = store_ref.shape
     rows = PLANE * part
@@ -200,7 +217,7 @@
     slots = 256 // extra
     wide = 256
 
-    def against(query, block, span):
+    def against(index, query, block):
         best = []
         for row in range(rows):
             similar = lax.dot_general(
@@ -208,34 +225,44 @@
                 preferred_element_type=F32,
             )
             best.append(jnp.max(similar, axis=0, keepdims=True))
-        best = jnp.concatenate(best, axis=0)
-        first = best.astype(BF16)
-        rest = best - first.astype(F32)
-        second = rest.astype(BF16)
-        third = (rest - second.astype(F32)).astype(BF16)
-        member = lax.broadcasted_iota(jnp.int32, (wide // span, wide), 1) // span
-        mine = lax.broadcasted_iota(jnp.int32, (wide // span, wide), 0)
-        picks = jnp.where(member == mine, 1.0, 0.0).astype(BF16)
-        total = [
-            lax.dot_general(
-                picks, piece, (((1,), (1,)), ((), ())), preferred_element_type=F32
-            )
-            for piece in (first, second, third)
-        ]
-        return (total[0] + total[1]) + total[2]
+        best_ref[index] = jnp.concatenate(best, axis=0)
+
+    blocks = count // slots
+    inner_blocks = slots // group
 
     def some(step, carry):
         start = pl.multiple_of(step * slots, slots)
-        for inner in range(slots // group):
+        for inner in range(inner_blocks):
             here = pl.ds(start + inner * group, group)
             query = arrived_ref[here, 0:tokens, :].reshape(wide, dim)
-            out_ref[here, 0:rows] = against(query, lambda k, j: store_ref[k, j], tokens)
-        here = pl.ds(start, slots)
-        query = arrived_ref[here, tokens:height, :].reshape(wide, dim)
-        out_ref[here, rows : 2 * rows] = against(query, lambda k, j: hot_refs[k][j], extra)
+            against(step * inner_blocks + inner, query, lambda k, j: store_ref[k, j])
+        query = arrived_ref[pl.ds(start, slots), tokens:height, :].reshape(wide, dim)
+        against(blocks * inner_blocks + step, query, lambda k, j: hot_refs[k][j])
         return carry
 
-    lax.fori_loop(0, count // slots, some, 0)
+    lax.fori_loop(0, blocks, some, 0)
+    slot = lax.broadcasted_iota(jnp.int32, (wide, count), 1)
+    token = lax.broadcasted_iota(jnp.int32, (wide, count), 0)
+
+    def sums(first_block, number, span):
+        member = lax.shift_right_logical(token, log2(span))
+        total = jnp.zeros((3 * rows, count), F32)
+        for index in range(number):
+            best = best_ref[first_block + index]
+            first = best.astype(BF16)
+            rest = best - first.astype(F32)
+            second = rest.astype(BF16)
+            third = (rest - second.astype(F32)).astype(BF16)
+            picks = jnp.where(slot == member + index * (wide // span), 1.0, 0.0).astype(BF16)
+            total = total + jnp.dot(
+                jnp.concatenate([first, second, third], axis=0), picks,
+                preferred_element_type=F32,
+            )
+        return (total[:rows] + total[rows : 2 * rows]) + total[2 * rows :]
+
+    near_sums = sums(0, blocks * inner_blocks, tokens)
+    far_sums = sums(blocks * inner_blocks, blocks, extra)
+    out_ref[...] = jnp.transpose(jnp.concatenate([near_sums, far_sums], axis=0))
 
 
 def score(arrived, store, hot_parts):
@@ -249,6 +276,7 @@
         out_shape=pltpu.VMEM((count, 2 * rows), F32),
         in_specs=[vmem()] * (2 + PLANE),
         out_specs=vmem(),
+        scratch_shapes=[pltpu.VMEM((count * height // 256, rows, 256), F32)],
         cost_estimate=cost(
             2 * count * height * rows * length * dim,
             2 * (count * height + 2 * rows * length) * dim,
@@ -312,7 +340,7 @@
         out_shape=jax.ShapeDtypeStruct((slots, queries), F32),
         in_specs=[smem(), vmem(), vmem(), vmem(), vmem()],
         out_specs=vmem(),
-    )(note, holder, row, turned, near(back))
+    )(note, near(holder), near(row), near(turned), near(back))
 
 
 def turn(value, hop, planes):

time: 140 us -> 137 us (0.979)
  Pallas kernels: 27.2 us -> 24.2 us
    pallas_call x1, Pallas kernels: 15.3 us -> 12.2 us  [score(): pl.pallas_call(score_kernel, name='score', compiler_params=pltpu.Compiler...]
  transfers between devices with their start and end apart: 15 -> 15, of which waited for: 9 -> 8; matrix products, arithmetic and copies ran while one was open for 1% -> 1% of each run, Pallas kernels for 5% -> 5%
where the time goes in v4:
time: 137 us
  starting transfers between devices  56.4 us (41%)
  waiting for transfers between devices  28.2 us (21%)
  blocking collectives  26.2 us (19%)
  Pallas kernels  24.2 us (18%)
  local copies, waits for them, and re-layouts  1.41 us (1%)
    all_to_all x1, starting transfers between devices, local(): arrived = lax.all_to_all(outgoing, 'shard', 0, 0, tiled=True)  31 us
    all_to_all x1, blocking collectives, local(): back = lax.all_to_all(visited, 'shard', 0, 0, tiled=True)  26.2 us
    ppermute x14, starting transfers between devices, turn(): return lax.ppermute(value, 'shard', pairs)  25.4 us
    ppermute x14, waiting for transfers between devices, turn(): return lax.ppermute(value, 'shard', pairs)  19 us
    pallas_call x1, Pallas kernels, score(): pl.pallas_call(score_kernel, name='score', compiler_params=pltpu.Compiler...  12.2 us
    all_to_all x1, waiting for transfers between devices, local(): arrived = lax.all_to_all(outgoing, 'shard', 0, 0, tiled=True)  9.16 us
    pallas_call x1, Pallas kernels, decode(): pl.pallas_call(decode_kernel, name='decode', out_shape=jax.ShapeDtypeStru...  6.31 us
    pallas_call x1, Pallas kernels, prepare(): pl.pallas_call(functools.partial(prepare_kernel, store_rows, device_count...  3.99 us
  transfers between devices with their start and end apart: 15, of which 8 were waited for; matrix products, arithmetic and copies ran while one was open for 1% of the time, Pallas kernels for 5%

profile of v4, /device:TPU:33, one launch (start us, length us, event | category | flops | bytes accessed | tf_op | source)
XLA Modules:
  0.0 136.8 jit_solution(3673900275092516005)
XLA Ops:
  0.0 4.0 %prepare.1 = (bf16[128,40,128]{2,1,0:T(8,128)(2,1)}, s32[6,128]{1,0:T(8,128)}, s32[6,128]{1,0:T(8,128)}, s32[6,128]{1,0:T(8,128)}, s32[4]{0:T(128)}) custom-call(s32[24,32]{1,0:T(8,128)} %bitcast.47, s32[1,32]{1,0:T(1,128)} %bitcast.48, s32[32,128]{1,0:T(8,128)} %bitcast.46, bf16[32,32,128]{2,1,0:T(8,128)(2,1)} %query_ref.1), custom_call_target="tpu_custom_call" | custom-call | flops 1000000000 | bytes 2000000 | tf_op jit(solution)/shard_map/prepare/pallas_call | solution.py:142
  4.0 31.0 %all-to-all-start = ((bf16[128,40,128]{2,1,0:T(8,128)(2,1)}), bf16[128,40,128]{2,1,0:T(8,128)(2,1)S(1)}, u32[]{:S(2)}, u32[]{:S(2)}) async-start(bf16[128,40,128]{2,1,0:T(8,128)(2,1)} %get-tuple-element.14), calls=%async_computation | async-start | bytes 2621440 | tf_op jit(solution)/shard_map/all_to_all | solution.py:367
  35.0 6.3 %decode.1.store_ref = bf16[8,4,128,128]{3,2,1,0:T(8,128)(2,1)} custom-call(s32[1]{0:T(128)} %bitcast.3.seat_ref, s32[32]{0:T(128)} %length_ref.1, f32[4]{0:T(128)} %level_ref.1, bf16[32,128,128]{2,1,0:T(8,128)(2,1)} %base_ref.1, s32[32,128,128]{2,1,0:T(8,128)} %code_ref.1), custom_call_target="tpu_custom_call" | custom-call | flops 10485760 | bytes 4194304 | tf_op jit(solution)/shard_map/decode/pallas_call | solution.py:195
  41.3 1.4 %slice_bitcast_fusion.1 = (bf16[4,128,128]{2,1,0:T(8,128)(2,1)S(1)}, bf16[4,128,128]{2,1,0:T(8,128)(2,1)S(1)}, bf16[4,128,128]{2,1,0:T(8,128)(2,1)S(1)}, bf16[4,...) fusion(bf16[8,4,128,128]{3,2,1,0:T(8,128)(2,1)} %decode.1.store_ref), kind=kLoop, calls=%fused_computation.8 | loop fusion | bytes 1835008 | tf_op jit(solution)/shard_map/squeeze | solution.py:363
  42.7 2.6 %collective-permute-start = (bf16[4,128,128]{2,1,0:T(8,128)(2,1)S(1)}, bf16[4,128,128]{2,1,0:T(8,128)(2,1)S(1)}, u32[]{:S(2)}, u32[]{:S(2)}) collective-permute-start(bf16[4,128,128]{2,1,0:T(8,128)(2,1)S(1)} %get-tuple-element.21), channel_id=1, source_target_pairs={{0,7},{1,0},{2,1},{3,2},{4,3},{5,4},{6,5},{7,6},{8,15},{9,8},{10,9... | collective-permute-start | bytes 393224 | tf_op jit(solution)/shard_map/ppermute | solution.py:351
  45.4 0.4 collective-permute-start.1
  45.7 1.0 collective-permute-start.2
  46.8 2.4 %collective-permute-start.3 = (bf16[4,128,128]{2,1,0:T(8,128)(2,1)S(1)}, bf16[4,128,128]{2,1,0:T(8,128)(2,1)S(1)}, u32[]{:S(2)}, u32[]{:S(2)}) collective-permute-start(bf16[4,128,128]{2,1,0:T(8,128)(2,1)S(1)} %get-tuple-element.18), channel_id=1, source_target_pairs={{0,4},{1,5},{2,6},{3,7},{4,0},{5,1},{6,2},{7,3},{8,12},{9,13},{10,... | collective-permute-start | bytes 393224 | tf_op jit(solution)/shard_map/ppermute | solution.py:351
  49.2 0.7 collective-permute-start.4
  49.9 0.0 collective-permute-done
  49.9 1.1 collective-permute-start.5
  51.0 3.8 %collective-permute-start.6 = (bf16[4,128,128]{2,1,0:T(8,128)(2,1)S(1)}, bf16[4,128,128]{2,1,0:T(8,128)(2,1)}, u32[]{:S(2)}, u32[]{:S(2)}) collective-permute-start(bf16[4,128,128]{2,1,0:T(8,128)(2,1)S(1)} %get-tuple-element.15), channel_id=1, source_target_pairs={{0,1},{1,2},{2,3},{3,4},{4,5},{5,6},{6,7},{7,0},{8,9},{9,10},{10,1... | collective-permute-start | bytes 393224 | tf_op jit(solution)/shard_map/ppermute | solution.py:351
  54.9 5.7 %collective-permute-done.2 = bf16[4,128,128]{2,1,0:T(8,128)(2,1)S(1)} collective-permute-done((bf16[4,128,128]{2,1,0:T(8,128)(2,1)S(1)}, bf16[4,128,128]{2,1,0:T(8,128)(2,1)S(1)}, u32[]{:S(2)}, u32[]{:S(2)}) %collective-permute-start.2) | collective-permute-done | bytes 131104 | tf_op jit(solution)/shard_map/ppermute | solution.py:351
  60.7 0.6 collective-permute-done.4
  61.2 0.3 collective-permute-done.5
  61.5 1.8 %collective-permute-done.6 = bf16[4,128,128]{2,1,0:T(8,128)(2,1)} collective-permute-done((bf16[4,128,128]{2,1,0:T(8,128)(2,1)S(1)}, bf16[4,128,128]{2,1,0:T(8,128)(2,1)}, u32[]{:S(2)}, u32[]{:S(2)}) %collective-permute-start.6) | collective-permute-done | bytes 131104 | tf_op jit(solution)/shard_map/ppermute | solution.py:351
  63.4 0.1 fusion.6.refs_0_
  63.4 0.0 copy-start.1
  63.4 4.9 %collective-permute-start.7 = (bf16[4,128,128]{2,1,0:T(8,128)(2,1)S(1)}, bf16[4,128,128]{2,1,0:T(8,128)(2,1)S(1)}, u32[]{:S(2)}, u32[]{:S(2)}) collective-permute-start(bf16[4,128,128]{2,1,0:T(8,128)(2,1)S(1)} %fusion.6.refs_0_), channel_id=1, source_target_pairs={{0,7},{1,0},{2,1},{3,2},{4,3},{5,4},{6,5},{7,6},{8,15},{9,8},{10,9... | collective-permute-start | bytes 393224 | tf_op jit(solution)/shard_map/ppermute | solution.py:351
  68.3 2.9 %collective-permute-start.8 = (bf16[4,128,128]{2,1,0:T(8,128)(2,1)S(1)}, bf16[4,128,128]{2,1,0:T(8,128)(2,1)S(1)}, u32[]{:S(2)}, u32[]{:S(2)}) collective-permute-start(bf16[4,128,128]{2,1,0:T(8,128)(2,1)S(1)} %fusion.6.refs_0_), channel_id=1, source_target_pairs={{0,6},{1,7},{2,0},{3,1},{4,2},{5,3},{6,4},{7,5},{8,14},{9,15},{10,... | collective-permute-start | bytes 393224 | tf_op jit(solution)/shard_map/ppermute | solution.py:351
  71.2 0.2 collective-permute-start.9
  71.4 0.5 collective-permute-start.10
  71.9 2.9 %collective-permute-start.11 = (bf16[4,128,128]{2,1,0:T(8,128)(2,1)S(1)}, bf16[4,128,128]{2,1,0:T(8,128)(2,1)S(1)}, u32[]{:S(2)}, u32[]{:S(2)}) collective-permute-start(bf16[4,128,128]{2,1,0:T(8,128)(2,1)S(1)} %fusion.6.refs_0_), channel_id=1, source_target_pairs={{0,3},{1,4},{2,5},{3,6},{4,7},{5,0},{6,1},{7,2},{8,11},{9,12},{10,... | collective-permute-start | bytes 393224 | tf_op jit(solution)/shard_map/ppermute | solution.py:351
  74.8 0.6 collective-permute-start.12
  75.3 1.5 %collective-permute-start.13 = (bf16[4,128,128]{2,1,0:T(8,128)(2,1)S(1)}, bf16[4,128,128]{2,1,0:T(8,128)(2,1)S(1)}, u32[]{:S(2)}, u32[]{:S(2)}) collective-permute-start(bf16[4,128,128]{2,1,0:T(8,128)(2,1)S(1)} %fusion.6.refs_0_), channel_id=1, source_target_pairs={{0,1},{1,2},{2,3},{3,4},{4,5},{5,6},{6,7},{7,0},{8,9},{9,10},{10,1... | collective-permute-start | bytes 393224 | tf_op jit(solution)/shard_map/ppermute | solution.py:351
  76.8 7.9 %collective-permute-done.9.refs_3_ = bf16[4,128,128]{2,1,0:T(8,128)(2,1)S(1)} collective-permute-done((bf16[4,128,128]{2,1,0:T(8,128)(2,1)S(1)}, bf16[4,128,128]{2,1,0:T(8,128)(2,1)S(1)}, u32[]{:S(2)}, u32[]{:S(2)}) %collective-permute-start.9) | collective-permute-done | bytes 131104 | tf_op jit(solution)/shard_map/ppermute | solution.py:351
  84.7 2.4 %collective-permute-done.11.refs_5_ = bf16[4,128,128]{2,1,0:T(8,128)(2,1)S(1)} collective-permute-done((bf16[4,128,128]{2,1,0:T(8,128)(2,1)S(1)}, bf16[4,128,128]{2,1,0:T(8,128)(2,1)S(1)}, u32[]{:S(2)}, u32[]{:S(2)}) %collective-permute-start.11) | collective-permute-done | bytes 131104 | tf_op jit(solution)/shard_map/ppermute | solution.py:351
  87.1 0.3 collective-permute-done.12.refs_6_
  87.4 9.2 %all-to-all-done.arrived_ref = bf16[128,40,128]{2,1,0:T(8,128)(2,1)S(1)} async-done(((bf16[128,40,128]{2,1,0:T(8,128)(2,1)}), bf16[128,40,128]{2,1,0:T(8,128)(2,1)S(1)}, u32[]{:S(2)}, u32[]{:S(2)}) %all-to-all-start) | async-done | bytes 1310752 | tf_op jit(solution)/shard_map/all_to_all | solution.py:367
  96.6 12.2 %score.1 = f32[128,64]{1,0:T(8,128)S(1)} custom-call(bf16[128,40,128]{2,1,0:T(8,128)(2,1)S(1)} %all-to-all-done.arrived_ref, bf16[8,4,128,128]{3,2,1,0:T(8,128)(2,1)S(1)} %copy-done, bf16[4,128,128]{2,1,0:T(8,128)(2,1)S(1)} %fusion.6.refs_0_, bf16[4,128,128]{2,1,0:T(8,128)(2,1)S(1)} %collective-permute-done.7.refs_1_, ...), custom_call_target="tpu_custom_call" | custom-call | flops 5368709120 | bytes 3407872 | tf_op jit(solution)/shard_map/score/pallas_call | solution.py:272
  108.8 26.2 %all_to_all.16 = f32[128,1,64]{2,1,0:T(1,128)S(1)} all-to-all(f32[128,1,64]{2,1,0:T(1,128)S(1)} %bitcast.42), channel_id=1, replica_groups=mesh['groups'=2,'shard'=128] {'shard'}, dimensions={0} | all-to-all | bytes 65536 | tf_op jit(solution)/shard_map/all_to_all | solution.py:374
  135.1 1.7 %finish.1 = f32[24,32]{1,0:T(8,128)} custom-call(s32[4]{0:T(128)} %get-tuple-element.10.note_ref, s32[6,128]{1,0:T(8,128)S(1)} %copy-done.1, s32[6,128]{1,0:T(8,128)S(1)} %copy-done.2, s32[6,128]{1,0:T(8,128)S(1)} %copy-done.3, f32[128,64]{1,0:T(8,128)S(1)} %bitcast.41), custom_call_target="tpu_custom_call" | custom-call | tf_op jit(solution)/shard_map/finish/pallas_call | solution.py:337
  (15 shorter events, 0.0 us)
Async XLA Ops:
  4.0 92.6 %all-to-all-start = ((bf16[128,40,128]{2,1,0:T(8,128)(2,1)}), bf16[128,40,128]{2,1,0:T(8,128)(2,1)S(1)}, u32[]{:S(2)}, u32[]{:S(2)}) async-start(bf16[128,40,128]{2,1,0:T(8,128)(2,1)} %get-tuple-element.14), calls=%async_computation | async-start | bytes 2621440 | tf_op jit(solution)/shard_map/all_to_all | solution.py:367
  41.3 13.5 %copy-start.4 = (s32[4]{0:T(128)S(1)}, s32[4]{0:T(128)}, u32[]{:S(2)}) copy-start(s32[4]{0:T(128)} %get-tuple-element.10.note_ref) | copy-start | bytes 52
  41.3 22.0 %copy-start = (bf16[8,4,128,128]{3,2,1,0:T(8,128)(2,1)S(1)}, bf16[8,4,128,128]{3,2,1,0:T(8,128)(2,1)}, u32[]{:S(2)}) copy-start(bf16[8,4,128,128]{3,2,1,0:T(8,128)(2,1)} %decode.1.store_ref) | copy-start | bytes 3145732
  42.7 7.1 %collective-permute-start = (bf16[4,128,128]{2,1,0:T(8,128)(2,1)S(1)}, bf16[4,128,128]{2,1,0:T(8,128)(2,1)S(1)}, u32[]{:S(2)}, u32[]{:S(2)}) collective-permute-start(bf16[4,128,128]{2,1,0:T(8,128)(2,1)S(1)} %get-tuple-element.21), channel_id=1, source_target_pairs={{0,7},{1,0},{2,1},{3,2},{4,3},{5,4},{6,5},{7,6},{8,15},{9,8},{10,9... | collective-permute-start | bytes 393224 | tf_op jit(solution)/shard_map/ppermute | solution.py:351
  45.4 5.6 %collective-permute-start.1 = (bf16[4,128,128]{2,1,0:T(8,128)(2,1)S(1)}, bf16[4,128,128]{2,1,0:T(8,128)(2,1)S(1)}, u32[]{:S(2)}, u32[]{:S(2)}) collective-permute-start(bf16[4,128,128]{2,1,0:T(8,128)(2,1)S(1)} %get-tuple-element.20), channel_id=1, source_target_pairs={{0,6},{1,7},{2,0},{3,1},{4,2},{5,3},{6,4},{7,5},{8,14},{9,15},{10,... | collective-permute-start | bytes 393224 | tf_op jit(solution)/shard_map/ppermute | solution.py:351
  45.7 14.9 %collective-permute-start.2 = (bf16[4,128,128]{2,1,0:T(8,128)(2,1)S(1)}, bf16[4,128,128]{2,1,0:T(8,128)(2,1)S(1)}, u32[]{:S(2)}, u32[]{:S(2)}) collective-permute-start(bf16[4,128,128]{2,1,0:T(8,128)(2,1)S(1)} %get-tuple-element.19), channel_id=1, source_target_pairs={{0,5},{1,6},{2,7},{3,0},{4,1},{5,2},{6,3},{7,4},{8,13},{9,14},{10,... | collective-permute-start | bytes 393224 | tf_op jit(solution)/shard_map/ppermute | solution.py:351
  46.8 13.9 %collective-permute-start.3 = (bf16[4,128,128]{2,1,0:T(8,128)(2,1)S(1)}, bf16[4,128,128]{2,1,0:T(8,128)(2,1)S(1)}, u32[]{:S(2)}, u32[]{:S(2)}) collective-permute-start(bf16[4,128,128]{2,1,0:T(8,128)(2,1)S(1)} %get-tuple-element.18), channel_id=1, source_target_pairs={{0,4},{1,5},{2,6},{3,7},{4,0},{5,1},{6,2},{7,3},{8,12},{9,13},{10,... | collective-permute-start | bytes 393224 | tf_op jit(solution)/shard_map/ppermute | solution.py:351
  49.2 12.1 %collective-permute-start.4 = (bf16[4,128,128]{2,1,0:T(8,128)(2,1)S(1)}, bf16[4,128,128]{2,1,0:T(8,128)(2,1)}, u32[]{:S(2)}, u32[]{:S(2)}) collective-permute-start(bf16[4,128,128]{2,1,0:T(8,128)(2,1)S(1)} %get-tuple-element.17), channel_id=1, source_target_pairs={{0,3},{1,4},{2,5},{3,6},{4,7},{5,0},{6,1},{7,2},{8,11},{9,12},{10,... | collective-permute-start | bytes 393224 | tf_op jit(solution)/shard_map/ppermute | solution.py:351
  49.9 11.7 %collective-permute-start.5 = (bf16[4,128,128]{2,1,0:T(8,128)(2,1)S(1)}, bf16[4,128,128]{2,1,0:T(8,128)(2,1)}, u32[]{:S(2)}, u32[]{:S(2)}) collective-permute-start(bf16[4,128,128]{2,1,0:T(8,128)(2,1)S(1)} %get-tuple-element.16), channel_id=1, source_target_pairs={{0,2},{1,3},{2,4},{3,5},{4,6},{5,7},{6,0},{7,1},{8,10},{9,11},{10,... | collective-permute-start | bytes 393224 | tf_op jit(solution)/shard_map/ppermute | solution.py:351
  51.0 12.3 %collective-permute-start.6 = (bf16[4,128,128]{2,1,0:T(8,128)(2,1)S(1)}, bf16[4,128,128]{2,1,0:T(8,128)(2,1)}, u32[]{:S(2)}, u32[]{:S(2)}) collective-permute-start(bf16[4,128,128]{2,1,0:T(8,128)(2,1)S(1)} %get-tuple-element.15), channel_id=1, source_target_pairs={{0,1},{1,2},{2,3},{3,4},{4,5},{5,6},{6,7},{7,0},{8,9},{9,10},{10,1... | collective-permute-start | bytes 393224 | tf_op jit(solution)/shard_map/ppermute | solution.py:351
  63.4 71.7 %copy-start.1 = (s32[6,128]{1,0:T(8,128)S(1)}, s32[6,128]{1,0:T(8,128)}, u32[]{:S(2)}) copy-start(s32[6,128]{1,0:T(8,128)} %get-tuple-element.11.holder_ref) | copy-start | bytes 9220
  63.4 71.7 %copy-start.2 = (s32[6,128]{1,0:T(8,128)S(1)}, s32[6,128]{1,0:T(8,128)}, u32[]{:S(2)}) copy-start(s32[6,128]{1,0:T(8,128)} %get-tuple-element.12.row_ref) | copy-start | bytes 9220
  63.4 71.6 %copy-start.3 = (s32[6,128]{1,0:T(8,128)S(1)}, s32[6,128]{1,0:T(8,128)}, u32[]{:S(2)}) copy-start(s32[6,128]{1,0:T(8,128)} %get-tuple-element.13.turned_ref) | copy-start | bytes 9220
  63.4 11.3 %collective-permute-start.7 = (bf16[4,128,128]{2,1,0:T(8,128)(2,1)S(1)}, bf16[4,128,128]{2,1,0:T(8,128)(2,1)S(1)}, u32[]{:S(2)}, u32[]{:S(2)}) collective-permute-start(bf16[4,128,128]{2,1,0:T(8,128)(2,1)S(1)} %fusion.6.refs_0_), channel_id=1, source_target_pairs={{0,7},{1,0},{2,1},{3,2},{4,3},{5,4},{6,5},{7,6},{8,15},{9,8},{10,9... | collective-permute-start | bytes 393224 | tf_op jit(solution)/shard_map/ppermute | solution.py:351
  68.3 7.0 %collective-permute-start.8 = (bf16[4,128,128]{2,1,0:T(8,128)(2,1)S(1)}, bf16[4,128,128]{2,1,0:T(8,128)(2,1)S(1)}, u32[]{:S(2)}, u32[]{:S(2)}) collective-permute-start(bf16[4,128,128]{2,1,0:T(8,128)(2,1)S(1)} %fusion.6.refs_0_), channel_id=1, source_target_pairs={{0,6},{1,7},{2,0},{3,1},{4,2},{5,3},{6,4},{7,5},{8,14},{9,15},{10,... | collective-permute-start | bytes 393224 | tf_op jit(solution)/shard_map/ppermute | solution.py:351
  71.2 13.5 %collective-permute-start.9 = (bf16[4,128,128]{2,1,0:T(8,128)(2,1)S(1)}, bf16[4,128,128]{2,1,0:T(8,128)(2,1)S(1)}, u32[]{:S(2)}, u32[]{:S(2)}) collective-permute-start(bf16[4,128,128]{2,1,0:T(8,128)(2,1)S(1)} %fusion.6.refs_0_), channel_id=1, source_target_pairs={{0,5},{1,6},{2,7},{3,0},{4,1},{5,2},{6,3},{7,4},{8,13},{9,14},{10,... | collective-permute-start | bytes 393224 | tf_op jit(solution)/shard_map/ppermute | solution.py:351
  71.4 13.3 %collective-permute-start.10 = (bf16[4,128,128]{2,1,0:T(8,128)(2,1)S(1)}, bf16[4,128,128]{2,1,0:T(8,128)(2,1)S(1)}, u32[]{:S(2)}, u32[]{:S(2)}) collective-permute-start(bf16[4,128,128]{2,1,0:T(8,128)(2,1)S(1)} %fusion.6.refs_0_), channel_id=1, source_target_pairs={{0,4},{1,5},{2,6},{3,7},{4,0},{5,1},{6,2},{7,3},{8,12},{9,13},{10,... | collective-permute-start | bytes 393224 | tf_op jit(solution)/shard_map/ppermute | solution.py:351
  71.9 15.2 %collective-permute-start.11 = (bf16[4,128,128]{2,1,0:T(8,128)(2,1)S(1)}, bf16[4,128,128]{2,1,0:T(8,128)(2,1)S(1)}, u32[]{:S(2)}, u32[]{:S(2)}) collective-permute-start(bf16[4,128,128]{2,1,0:T(8,128)(2,1)S(1)} %fusion.6.refs_0_), channel_id=1, source_target_pairs={{0,3},{1,4},{2,5},{3,6},{4,7},{5,0},{6,1},{7,2},{8,11},{9,12},{10,... | collective-permute-start | bytes 393224 | tf_op jit(solution)/shard_map/ppermute | solution.py:351
  74.8 12.6 %collective-permute-start.12 = (bf16[4,128,128]{2,1,0:T(8,128)(2,1)S(1)}, bf16[4,128,128]{2,1,0:T(8,128)(2,1)S(1)}, u32[]{:S(2)}, u32[]{:S(2)}) collective-permute-start(bf16[4,128,128]{2,1,0:T(8,128)(2,1)S(1)} %fusion.6.refs_0_), channel_id=1, source_target_pairs={{0,2},{1,3},{2,4},{3,5},{4,6},{5,7},{6,0},{7,1},{8,10},{9,11},{10,... | collective-permute-start | bytes 393224 | tf_op jit(solution)/shard_map/ppermute | solution.py:351
  75.3 12.1 %collective-permute-start.13 = (bf16[4,128,128]{2,1,0:T(8,128)(2,1)S(1)}, bf16[4,128,128]{2,1,0:T(8,128)(2,1)S(1)}, u32[]{:S(2)}, u32[]{:S(2)}) collective-permute-start(bf16[4,128,128]{2,1,0:T(8,128)(2,1)S(1)} %fusion.6.refs_0_), channel_id=1, source_target_pairs={{0,1},{1,2},{2,3},{3,4},{4,5},{5,6},{6,7},{7,0},{8,9},{9,10},{10,1... | collective-permute-start | bytes 393224 | tf_op jit(solution)/shard_map/ppermute | solution.py:351

commit v5 on v4

--- a/solution.py
+++ b/solution.py
@@ -37,7 +37,7 @@
 def prepare_kernel(
     store_rows, device_count,
     cand_ref, count_ref, map_ref, query_ref,
-    out_ref, holder_ref, row_ref, turned_ref, note_ref,
+    out_ref, holder_ref, row_ref, turned_ref, note_ref, busiest_ref,
     present_ref, pick_vmem, pick_smem, sem, tokens_ref, packed_ref, in_sem, out_sem,
 ):
     load = pltpu.make_async_copy(query_ref, tokens_ref, in_sem)
@@ -101,10 +101,9 @@
     pick_vmem[...] = jnp.clip(pick, 0, queries - 1)
     copy = pltpu.make_async_copy(pick_vmem, pick_smem, sem)
     copy.start()
-    note_ref[0] = busiest
-    note_ref[1] = first
-    note_ref[2] = middle
-    note_ref[3] = last
+    busiest_ref[0] = busiest
+    kind = lax.broadcasted_iota(jnp.int32, (8, device_count), 0)
+    note_ref[...] = jnp.where(kind == 0, busiest, jnp.where(kind == 1, first, middle))
     tokens = query_ref.shape[1]
     extra = 2 * tokens // PLANE
     load.wait()
@@ -138,17 +137,18 @@
 def prepare(candidates, cand_count, placement_map, query_tokens, store_rows, device_count):
     queries, slots = candidates.shape
     _, tokens, dim = query_tokens.shape
-    wide = jax.ShapeDtypeStruct((slots * queries // dim, dim), jnp.int32)
+    wide = pltpu.VMEM((slots * queries // dim, dim), jnp.int32)
     return pl.pallas_call(
         functools.partial(prepare_kernel, store_rows, device_count),
         name="prepare",
         out_shape=(
             jax.ShapeDtypeStruct((device_count, tokens + 2 * tokens // PLANE, dim), BF16),
             wide, wide, wide,
-            jax.ShapeDtypeStruct((4,), jnp.int32),
+            pltpu.VMEM((8, device_count), jnp.int32),
+            jax.ShapeDtypeStruct((1,), jnp.int32),
         ),
         in_specs=[vmem(), vmem(), vmem(), pl.BlockSpec(memory_space=pl.ANY)],
-        out_specs=(pl.BlockSpec(memory_space=pl.ANY), vmem(), vmem(), vmem(), smem()),
+        out_specs=(pl.BlockSpec(memory_space=pl.ANY), vmem(), vmem(), vmem(), vmem(), smem()),
         scratch_shapes=[
             pltpu.VMEM((device_count, dim), F32),
             pltpu.VMEM((1, device_count), jnp.int32),
@@ -290,7 +290,9 @@
     device_count, double = back_ref.shape
     rows = double // 2
     part = rows // PLANE
-    busiest = note_ref[0]
+    busiest = note_ref[0:1]
+    first_hot = note_ref[1:2]
+    second_hot = note_ref[2:3]
     back = jnp.transpose(back_ref[...])
     near, far = back[:rows], back[rows:]
     first = near.astype(BF16)
@@ -303,7 +305,7 @@
     lane = lax.broadcasted_iota(jnp.int32, (1, lanes), 1)
     query = lane & (queries - 1)
     device_lane = lax.broadcasted_iota(jnp.int32, (rows, device_count), 1)
-    plane = busiest - lax.rem(busiest, PLANE)
+    plane = busiest - (busiest & (PLANE - 1))
     sums = []
     for half in range(2):
         total = jnp.zeros((rows, 1), F32)
@@ -322,8 +324,8 @@
         mark = jnp.where(device_iota == holder, 1.0, 0.0).astype(BF16)
         three = jnp.dot(pieces, mark, preferred_element_type=F32)
         away = (three[:rows] + three[rows : 2 * rows]) + three[2 * rows :]
-        hot = (holder == busiest) & ((query == note_ref[1]) | (query == note_ref[2]))
-        extra = jnp.where(query == note_ref[1], sums[0], sums[1])
+        hot = (holder == busiest) & ((query == first_hot) | (query == second_hot))
+        extra = jnp.where(query == first_hot, sums[0], sums[1])
         found = jnp.where(hot, extra, away)
         row = jnp.where(hot, row_ref[s : s + 1], turned_ref[s : s + 1])
         value = jnp.sum(jnp.where(row_iota == row, found, 0.0), axis=0, keepdims=True)
@@ -338,9 +340,9 @@
         finish_kernel,
         name="finish",
         out_shape=jax.ShapeDtypeStruct((slots, queries), F32),
-        in_specs=[smem(), vmem(), vmem(), vmem(), vmem()],
+        in_specs=[vmem(), vmem(), vmem(), vmem(), vmem()],
         out_specs=vmem(),
-    )(note, near(holder), near(row), near(turned), near(back))
+    )(near(note), near(holder), near(row), near(turned), near(back))
 
 
 def turn(value, hop, planes):
@@ -361,11 +363,11 @@
     store_rows = passage_base.shape[0]
     store = decode(seat, passage_base, residual_codes, passage_lengths, bucket_weights)
     parts = [store[0]] + [turn(store[k], k, planes) for k in range(1, PLANE)]
-    outgoing, holder, row, turned, note = prepare(
+    outgoing, holder, row, turned, note, busiest = prepare(
         candidates, cand_count, placement_map, query_tokens, store_rows, device_count
     )
     arrived = lax.all_to_all(outgoing, "shard", 0, 0, tiled=True)
-    wanted = lax.rem(seat[0] - lax.rem(note[0], PLANE) + PLANE, PLANE)
+    wanted = lax.rem(seat[0] - lax.rem(busiest[0], PLANE) + PLANE, PLANE)
     piece = parts[0]
     for k in range(1, PLANE):
         piece = jnp.where(wanted == k, parts[k], piece)

time: 137 us -> 136 us (level)
  between operations: 0.22 us -> 2.02 us
  starting transfers between devices: 56.4 us -> 54.6 us
    ppermute x14, waiting for transfers between devices: 19 us -> 17.1 us  [turn(): return lax.ppermute(value, 'shard', pairs)]
    ppermute x14, starting transfers between devices: 25.4 us -> 23.6 us  [turn(): return lax.ppermute(value, 'shard', pairs)]
  transfers between devices with their start and end apart: 15 -> 15, of which waited for: 8 -> 8; matrix products, arithmetic and copies ran while one was open for 1% -> 2% of each run, Pallas kernels for 5% -> 5%
where the time goes in v5:
time: 136 us
  starting transfers between devices  54.6 us (40%)
  waiting for transfers between devices  27.3 us (20%)
  blocking collectives  26.3 us (19%)
  Pallas kernels  23.4 us (17%)
  between operations  2.02 us (1%)
  local copies, waits for them, and re-layouts  1.39 us (1%)
    all_to_all x1, starting transfers between devices, local(): arrived = lax.all_to_all(outgoing, 'shard', 0, 0, tiled=True)  31 us
    all_to_all x1, blocking collectives, local(): back = lax.all_to_all(visited, 'shard', 0, 0, tiled=True)  26.3 us
    ppermute x14, starting transfers between devices, turn(): return lax.ppermute(value, 'shard', pairs)  23.6 us
    ppermute x14, waiting for transfers between devices, turn(): return lax.ppermute(value, 'shard', pairs)  17.1 us
    pallas_call x1, Pallas kernels, score(): pl.pallas_call(score_kernel, name='score', compiler_params=pltpu.Compiler...  12.2 us
    all_to_all x1, waiting for transfers between devices, local(): arrived = lax.all_to_all(outgoing, 'shard', 0, 0, tiled=True)  10.2 us
    pallas_call x1, Pallas kernels, decode(): pl.pallas_call(decode_kernel, name='decode', out_shape=jax.ShapeDtypeStru...  6.32 us
    pallas_call x1, Pallas kernels, prepare(): pl.pallas_call(functools.partial(prepare_kernel, store_rows, device_count...  3.92 us
  transfers between devices with their start and end apart: 15, of which 8 were waited for; matrix products, arithmetic and copies ran while one was open for 2% of the time, Pallas kernels for 5%

profile of v5, /device:TPU:33, one launch (start us, length us, event | category | flops | bytes accessed | tf_op | source)
XLA Modules:
  0.0 136.0 jit_solution(16670153722485689309)
XLA Ops:
  0.0 3.9 %prepare.1 = (bf16[128,40,128]{2,1,0:T(8,128)(2,1)}, s32[6,128]{1,0:T(8,128)S(1)}, s32[6,128]{1,0:T(8,128)S(1)}, s32[6,128]{1,0:T(8,128)S(1)}, s32[8,128]{1,0:T(8,128)S(1)}, /*index=5*/s32[1]{0:T(128)}) custom-call(s32[24,32]{1,0:T(8,128)} %bitcast.43, s32[1,32]{1,0:T(1,128)} %bitcast.44, s32[32,128]{1,0:T(8,128)} %bitcast.42, bf16[32,32,128]{2,1,0:T(8,128)(2,1)} %query_ref.1), custom_call_target="tpu_custom_call" | custom-call | flops 1000000000 | bytes 2000000 | tf_op jit(solution)/shard_map/prepare/pallas_call | solution.py:141
  3.9 31.0 %all-to-all-start = ((bf16[128,40,128]{2,1,0:T(8,128)(2,1)}), bf16[128,40,128]{2,1,0:T(8,128)(2,1)S(1)}, u32[]{:S(2)}, u32[]{:S(2)}) async-start(bf16[128,40,128]{2,1,0:T(8,128)(2,1)} %get-tuple-element.15), calls=%async_computation | async-start | bytes 2621440 | tf_op jit(solution)/shard_map/all_to_all | solution.py:369
  35.0 6.3 %decode.1.store_ref = bf16[8,4,128,128]{3,2,1,0:T(8,128)(2,1)} custom-call(s32[1]{0:T(128)} %bitcast.3.seat_ref, s32[32]{0:T(128)} %length_ref.1, f32[4]{0:T(128)} %level_ref.1, bf16[32,128,128]{2,1,0:T(8,128)(2,1)} %base_ref.1, s32[32,128,128]{2,1,0:T(8,128)} %code_ref.1), custom_call_target="tpu_custom_call" | custom-call | flops 10485760 | bytes 4194304 | tf_op jit(solution)/shard_map/decode/pallas_call | solution.py:195
  41.3 1.4 %slice_bitcast_fusion.1 = (bf16[4,128,128]{2,1,0:T(8,128)(2,1)S(1)}, bf16[4,128,128]{2,1,0:T(8,128)(2,1)S(1)}, bf16[4,128,128]{2,1,0:T(8,128)(2,1)S(1)}, bf16[4,...) fusion(bf16[8,4,128,128]{3,2,1,0:T(8,128)(2,1)} %decode.1.store_ref), kind=kLoop, calls=%fused_computation.8 | loop fusion | bytes 1835008 | tf_op jit(solution)/shard_map/squeeze | solution.py:365
  42.7 2.6 %collective-permute-start = (bf16[4,128,128]{2,1,0:T(8,128)(2,1)S(1)}, bf16[4,128,128]{2,1,0:T(8,128)(2,1)S(1)}, u32[]{:S(2)}, u32[]{:S(2)}) collective-permute-start(bf16[4,128,128]{2,1,0:T(8,128)(2,1)S(1)} %get-tuple-element.23), channel_id=1, source_target_pairs={{0,7},{1,0},{2,1},{3,2},{4,3},{5,4},{6,5},{7,6},{8,15},{9,8},{10,9... | collective-permute-start | bytes 393224 | tf_op jit(solution)/shard_map/ppermute | solution.py:353
  45.3 0.4 collective-permute-start.1
  45.7 1.0 collective-permute-start.2
  46.7 2.4 %collective-permute-start.3 = (bf16[4,128,128]{2,1,0:T(8,128)(2,1)S(1)}, bf16[4,128,128]{2,1,0:T(8,128)(2,1)S(1)}, u32[]{:S(2)}, u32[]{:S(2)}) collective-permute-start(bf16[4,128,128]{2,1,0:T(8,128)(2,1)S(1)} %get-tuple-element.20), channel_id=1, source_target_pairs={{0,4},{1,5},{2,6},{3,7},{4,0},{5,1},{6,2},{7,3},{8,12},{9,13},{10,... | collective-permute-start | bytes 393224 | tf_op jit(solution)/shard_map/ppermute | solution.py:353
  49.1 0.7 collective-permute-start.4
  49.8 0.0 collective-permute-done
  49.8 1.1 collective-permute-start.5
  50.9 0.0 collective-permute-done.1
  50.9 3.8 %collective-permute-start.6 = (bf16[4,128,128]{2,1,0:T(8,128)(2,1)S(1)}, bf16[4,128,128]{2,1,0:T(8,128)(2,1)}, u32[]{:S(2)}, u32[]{:S(2)}) collective-permute-start(bf16[4,128,128]{2,1,0:T(8,128)(2,1)S(1)} %get-tuple-element.17), channel_id=1, source_target_pairs={{0,1},{1,2},{2,3},{3,4},{4,5},{5,6},{6,7},{7,0},{8,9},{9,10},{10,1... | collective-permute-start | bytes 393224 | tf_op jit(solution)/shard_map/ppermute | solution.py:353
  56.7 3.9 %collective-permute-done.2 = bf16[4,128,128]{2,1,0:T(8,128)(2,1)S(1)} collective-permute-done((bf16[4,128,128]{2,1,0:T(8,128)(2,1)S(1)}, bf16[4,128,128]{2,1,0:T(8,128)(2,1)S(1)}, u32[]{:S(2)}, u32[]{:S(2)}) %collective-permute-start.2) | collective-permute-done | bytes 131104 | tf_op jit(solution)/shard_map/ppermute | solution.py:353
  60.6 0.6 collective-permute-done.4
  61.2 0.3 collective-permute-done.5
  61.5 1.8 %collective-permute-done.6 = bf16[4,128,128]{2,1,0:T(8,128)(2,1)} collective-permute-done((bf16[4,128,128]{2,1,0:T(8,128)(2,1)S(1)}, bf16[4,128,128]{2,1,0:T(8,128)(2,1)}, u32[]{:S(2)}, u32[]{:S(2)}) %collective-permute-start.6) | collective-permute-done | bytes 131104 | tf_op jit(solution)/shard_map/ppermute | solution.py:353
  63.3 1.0 fusion.6.refs_0_
  64.2 3.1 %collective-permute-start.7 = (bf16[4,128,128]{2,1,0:T(8,128)(2,1)S(1)}, bf16[4,128,128]{2,1,0:T(8,128)(2,1)S(1)}, u32[]{:S(2)}, u32[]{:S(2)}) collective-permute-start(bf16[4,128,128]{2,1,0:T(8,128)(2,1)S(1)} %fusion.6.refs_0_), channel_id=1, source_target_pairs={{0,7},{1,0},{2,1},{3,2},{4,3},{5,4},{6,5},{7,6},{8,15},{9,8},{10,9... | collective-permute-start | bytes 393224 | tf_op jit(solution)/shard_map/ppermute | solution.py:353
  67.3 2.9 %collective-permute-start.8 = (bf16[4,128,128]{2,1,0:T(8,128)(2,1)S(1)}, bf16[4,128,128]{2,1,0:T(8,128)(2,1)S(1)}, u32[]{:S(2)}, u32[]{:S(2)}) collective-permute-start(bf16[4,128,128]{2,1,0:T(8,128)(2,1)S(1)} %fusion.6.refs_0_), channel_id=1, source_target_pairs={{0,6},{1,7},{2,0},{3,1},{4,2},{5,3},{6,4},{7,5},{8,14},{9,15},{10,... | collective-permute-start | bytes 393224 | tf_op jit(solution)/shard_map/ppermute | solution.py:353
  70.2 0.2 collective-permute-start.9
  70.4 0.5 collective-permute-start.10
  70.9 2.9 %collective-permute-start.11 = (bf16[4,128,128]{2,1,0:T(8,128)(2,1)S(1)}, bf16[4,128,128]{2,1,0:T(8,128)(2,1)S(1)}, u32[]{:S(2)}, u32[]{:S(2)}) collective-permute-start(bf16[4,128,128]{2,1,0:T(8,128)(2,1)S(1)} %fusion.6.refs_0_), channel_id=1, source_target_pairs={{0,3},{1,4},{2,5},{3,6},{4,7},{5,0},{6,1},{7,2},{8,11},{9,12},{10,... | collective-permute-start | bytes 393224 | tf_op jit(solution)/shard_map/ppermute | solution.py:353
  73.8 0.6 collective-permute-start.12
  74.3 1.5 %collective-permute-start.13 = (bf16[4,128,128]{2,1,0:T(8,128)(2,1)S(1)}, bf16[4,128,128]{2,1,0:T(8,128)(2,1)S(1)}, u32[]{:S(2)}, u32[]{:S(2)}) collective-permute-start(bf16[4,128,128]{2,1,0:T(8,128)(2,1)S(1)} %fusion.6.refs_0_), channel_id=1, source_target_pairs={{0,1},{1,2},{2,3},{3,4},{4,5},{5,6},{6,7},{7,0},{8,9},{9,10},{10,1... | collective-permute-start | bytes 393224 | tf_op jit(solution)/shard_map/ppermute | solution.py:353
  75.8 8.3 %collective-permute-done.9.refs_3_ = bf16[4,128,128]{2,1,0:T(8,128)(2,1)S(1)} collective-permute-done((bf16[4,128,128]{2,1,0:T(8,128)(2,1)S(1)}, bf16[4,128,128]{2,1,0:T(8,128)(2,1)S(1)}, u32[]{:S(2)}, u32[]{:S(2)}) %collective-permute-start.9) | collective-permute-done | bytes 131104 | tf_op jit(solution)/shard_map/ppermute | solution.py:353
  84.1 1.9 %collective-permute-done.11.refs_5_ = bf16[4,128,128]{2,1,0:T(8,128)(2,1)S(1)} collective-permute-done((bf16[4,128,128]{2,1,0:T(8,128)(2,1)S(1)}, bf16[4,128,128]{2,1,0:T(8,128)(2,1)S(1)}, u32[]{:S(2)}, u32[]{:S(2)}) %collective-permute-start.11) | collective-permute-done | bytes 131104 | tf_op jit(solution)/shard_map/ppermute | solution.py:353
  86.0 0.3 collective-permute-done.12.refs_6_
  86.3 10.2 %all-to-all-done.arrived_ref = bf16[128,40,128]{2,1,0:T(8,128)(2,1)S(1)} async-done(((bf16[128,40,128]{2,1,0:T(8,128)(2,1)}), bf16[128,40,128]{2,1,0:T(8,128)(2,1)S(1)}, u32[]{:S(2)}, u32[]{:S(2)}) %all-to-all-start) | async-done | bytes 1310752 | tf_op jit(solution)/shard_map/all_to_all | solution.py:369
  96.5 12.2 %score.1 = f32[128,64]{1,0:T(8,128)S(1)} custom-call(bf16[128,40,128]{2,1,0:T(8,128)(2,1)S(1)} %all-to-all-done.arrived_ref, bf16[8,4,128,128]{3,2,1,0:T(8,128)(2,1)S(1)} %copy-done, bf16[4,128,128]{2,1,0:T(8,128)(2,1)S(1)} %fusion.6.refs_0_, bf16[4,128,128]{2,1,0:T(8,128)(2,1)S(1)} %collective-permute-done.7.refs_1_, ...), custom_call_target="tpu_custom_call" | custom-call | flops 5368709120 | bytes 3407872 | tf_op jit(solution)/shard_map/score/pallas_call | solution.py:272
  108.7 26.3 %all_to_all.16 = f32[128,1,64]{2,1,0:T(1,128)S(1)} all-to-all(f32[128,1,64]{2,1,0:T(1,128)S(1)} %bitcast.41), channel_id=1, replica_groups=mesh['groups'=2,'shard'=128] {'shard'}, dimensions={0} | all-to-all | bytes 65536 | tf_op jit(solution)/shard_map/all_to_all | solution.py:376
  135.0 1.0 finish.1
  (7 shorter events, 0.0 us)
Async XLA Ops:
  3.9 92.6 %all-to-all-start = ((bf16[128,40,128]{2,1,0:T(8,128)(2,1)}), bf16[128,40,128]{2,1,0:T(8,128)(2,1)S(1)}, u32[]{:S(2)}, u32[]{:S(2)}) async-start(bf16[128,40,128]{2,1,0:T(8,128)(2,1)} %get-tuple-element.15), calls=%async_computation | async-start | bytes 2621440 | tf_op jit(solution)/shard_map/all_to_all | solution.py:369
  41.3 22.0 %copy-start = (bf16[8,4,128,128]{3,2,1,0:T(8,128)(2,1)S(1)}, bf16[8,4,128,128]{3,2,1,0:T(8,128)(2,1)}, u32[]{:S(2)}) copy-start(bf16[8,4,128,128]{3,2,1,0:T(8,128)(2,1)} %decode.1.store_ref) | copy-start | bytes 3145732
  42.7 7.1 %collective-permute-start = (bf16[4,128,128]{2,1,0:T(8,128)(2,1)S(1)}, bf16[4,128,128]{2,1,0:T(8,128)(2,1)S(1)}, u32[]{:S(2)}, u32[]{:S(2)}) collective-permute-start(bf16[4,128,128]{2,1,0:T(8,128)(2,1)S(1)} %get-tuple-element.23), channel_id=1, source_target_pairs={{0,7},{1,0},{2,1},{3,2},{4,3},{5,4},{6,5},{7,6},{8,15},{9,8},{10,9... | collective-permute-start | bytes 393224 | tf_op jit(solution)/shard_map/ppermute | solution.py:353
  45.3 5.6 %collective-permute-start.1 = (bf16[4,128,128]{2,1,0:T(8,128)(2,1)S(1)}, bf16[4,128,128]{2,1,0:T(8,128)(2,1)S(1)}, u32[]{:S(2)}, u32[]{:S(2)}) collective-permute-start(bf16[4,128,128]{2,1,0:T(8,128)(2,1)S(1)} %get-tuple-element.22), channel_id=1, source_target_pairs={{0,6},{1,7},{2,0},{3,1},{4,2},{5,3},{6,4},{7,5},{8,14},{9,15},{10,... | collective-permute-start | bytes 393224 | tf_op jit(solution)/shard_map/ppermute | solution.py:353
  45.7 14.9 %collective-permute-start.2 = (bf16[4,128,128]{2,1,0:T(8,128)(2,1)S(1)}, bf16[4,128,128]{2,1,0:T(8,128)(2,1)S(1)}, u32[]{:S(2)}, u32[]{:S(2)}) collective-permute-start(bf16[4,128,128]{2,1,0:T(8,128)(2,1)S(1)} %get-tuple-element.21), channel_id=1, source_target_pairs={{0,5},{1,6},{2,7},{3,0},{4,1},{5,2},{6,3},{7,4},{8,13},{9,14},{10,... | collective-permute-start | bytes 393224 | tf_op jit(solution)/shard_map/ppermute | solution.py:353
  46.7 13.9 %collective-permute-start.3 = (bf16[4,128,128]{2,1,0:T(8,128)(2,1)S(1)}, bf16[4,128,128]{2,1,0:T(8,128)(2,1)S(1)}, u32[]{:S(2)}, u32[]{:S(2)}) collective-permute-start(bf16[4,128,128]{2,1,0:T(8,128)(2,1)S(1)} %get-tuple-element.20), channel_id=1, source_target_pairs={{0,4},{1,5},{2,6},{3,7},{4,0},{5,1},{6,2},{7,3},{8,12},{9,13},{10,... | collective-permute-start | bytes 393224 | tf_op jit(solution)/shard_map/ppermute | solution.py:353
  49.1 12.1 %collective-permute-start.4 = (bf16[4,128,128]{2,1,0:T(8,128)(2,1)S(1)}, bf16[4,128,128]{2,1,0:T(8,128)(2,1)}, u32[]{:S(2)}, u32[]{:S(2)}) collective-permute-start(bf16[4,128,128]{2,1,0:T(8,128)(2,1)S(1)} %get-tuple-element.19), channel_id=1, source_target_pairs={{0,3},{1,4},{2,5},{3,6},{4,7},{5,0},{6,1},{7,2},{8,11},{9,12},{10,... | collective-permute-start | bytes 393224 | tf_op jit(solution)/shard_map/ppermute | solution.py:353
  49.8 11.7 %collective-permute-start.5 = (bf16[4,128,128]{2,1,0:T(8,128)(2,1)S(1)}, bf16[4,128,128]{2,1,0:T(8,128)(2,1)}, u32[]{:S(2)}, u32[]{:S(2)}) collective-permute-start(bf16[4,128,128]{2,1,0:T(8,128)(2,1)S(1)} %get-tuple-element.18), channel_id=1, source_target_pairs={{0,2},{1,3},{2,4},{3,5},{4,6},{5,7},{6,0},{7,1},{8,10},{9,11},{10,... | collective-permute-start | bytes 393224 | tf_op jit(solution)/shard_map/ppermute | solution.py:353
  50.9 12.3 %collective-permute-start.6 = (bf16[4,128,128]{2,1,0:T(8,128)(2,1)S(1)}, bf16[4,128,128]{2,1,0:T(8,128)(2,1)}, u32[]{:S(2)}, u32[]{:S(2)}) collective-permute-start(bf16[4,128,128]{2,1,0:T(8,128)(2,1)S(1)} %get-tuple-element.17), channel_id=1, source_target_pairs={{0,1},{1,2},{2,3},{3,4},{4,5},{5,6},{6,7},{7,0},{8,9},{9,10},{10,1... | collective-permute-start | bytes 393224 | tf_op jit(solution)/shard_map/ppermute | solution.py:353
  64.2 9.5 %collective-permute-start.7 = (bf16[4,128,128]{2,1,0:T(8,128)(2,1)S(1)}, bf16[4,128,128]{2,1,0:T(8,128)(2,1)S(1)}, u32[]{:S(2)}, u32[]{:S(2)}) collective-permute-start(bf16[4,128,128]{2,1,0:T(8,128)(2,1)S(1)} %fusion.6.refs_0_), channel_id=1, source_target_pairs={{0,7},{1,0},{2,1},{3,2},{4,3},{5,4},{6,5},{7,6},{8,15},{9,8},{10,9... | collective-permute-start | bytes 393224 | tf_op jit(solution)/shard_map/ppermute | solution.py:353
  67.3 7.0 %collective-permute-start.8 = (bf16[4,128,128]{2,1,0:T(8,128)(2,1)S(1)}, bf16[4,128,128]{2,1,0:T(8,128)(2,1)S(1)}, u32[]{:S(2)}, u32[]{:S(2)}) collective-permute-start(bf16[4,128,128]{2,1,0:T(8,128)(2,1)S(1)} %fusion.6.refs_0_), channel_id=1, source_target_pairs={{0,6},{1,7},{2,0},{3,1},{4,2},{5,3},{6,4},{7,5},{8,14},{9,15},{10,... | collective-permute-start | bytes 393224 | tf_op jit(solution)/shard_map/ppermute | solution.py:353
  70.2 13.9 %collective-permute-start.9 = (bf16[4,128,128]{2,1,0:T(8,128)(2,1)S(1)}, bf16[4,128,128]{2,1,0:T(8,128)(2,1)S(1)}, u32[]{:S(2)}, u32[]{:S(2)}) collective-permute-start(bf16[4,128,128]{2,1,0:T(8,128)(2,1)S(1)} %fusion.6.refs_0_), channel_id=1, source_target_pairs={{0,5},{1,6},{2,7},{3,0},{4,1},{5,2},{6,3},{7,4},{8,13},{9,14},{10,... | collective-permute-start | bytes 393224 | tf_op jit(solution)/shard_map/ppermute | solution.py:353
  70.4 13.7 %collective-permute-start.10 = (bf16[4,128,128]{2,1,0:T(8,128)(2,1)S(1)}, bf16[4,128,128]{2,1,0:T(8,128)(2,1)S(1)}, u32[]{:S(2)}, u32[]{:S(2)}) collective-permute-start(bf16[4,128,128]{2,1,0:T(8,128)(2,1)S(1)} %fusion.6.refs_0_), channel_id=1, source_target_pairs={{0,4},{1,5},{2,6},{3,7},{4,0},{5,1},{6,2},{7,3},{8,12},{9,13},{10,... | collective-permute-start | bytes 393224 | tf_op jit(solution)/shard_map/ppermute | solution.py:353
  70.9 15.1 %collective-permute-start.11 = (bf16[4,128,128]{2,1,0:T(8,128)(2,1)S(1)}, bf16[4,128,128]{2,1,0:T(8,128)(2,1)S(1)}, u32[]{:S(2)}, u32[]{:S(2)}) collective-permute-start(bf16[4,128,128]{2,1,0:T(8,128)(2,1)S(1)} %fusion.6.refs_0_), channel_id=1, source_target_pairs={{0,3},{1,4},{2,5},{3,6},{4,7},{5,0},{6,1},{7,2},{8,11},{9,12},{10,... | collective-permute-start | bytes 393224 | tf_op jit(solution)/shard_map/ppermute | solution.py:353
  73.8 12.5 %collective-permute-start.12 = (bf16[4,128,128]{2,1,0:T(8,128)(2,1)S(1)}, bf16[4,128,128]{2,1,0:T(8,128)(2,1)S(1)}, u32[]{:S(2)}, u32[]{:S(2)}) collective-permute-start(bf16[4,128,128]{2,1,0:T(8,128)(2,1)S(1)} %fusion.6.refs_0_), channel_id=1, source_target_pairs={{0,2},{1,3},{2,4},{3,5},{4,6},{5,7},{6,0},{7,1},{8,10},{9,11},{10,... | collective-permute-start | bytes 393224 | tf_op jit(solution)/shard_map/ppermute | solution.py:353
  74.3 12.0 %collective-permute-start.13 = (bf16[4,128,128]{2,1,0:T(8,128)(2,1)S(1)}, bf16[4,128,128]{2,1,0:T(8,128)(2,1)S(1)}, u32[]{:S(2)}, u32[]{:S(2)}) collective-permute-start(bf16[4,128,128]{2,1,0:T(8,128)(2,1)S(1)} %fusion.6.refs_0_), channel_id=1, source_target_pairs={{0,1},{1,2},{2,3},{3,4},{4,5},{5,6},{6,7},{7,0},{8,9},{9,10},{10,1... | collective-permute-start | bytes 393224 | tf_op jit(solution)/shard_map/ppermute | solution.py:353

commit v6 on v5

--- a/solution.py
+++ b/solution.py
@@ -89,6 +89,9 @@
         weigh.astype(F32).astype(BF16), present.astype(BF16),
         (((1,), (1,)), ((), ())), preferred_element_type=F32,
     )
+    pick_vmem[...] = jnp.clip(sums[0:1].astype(jnp.int32), 0, queries - 1)
+    copy = pltpu.make_async_copy(pick_vmem, pick_smem, sem)
+    copy.start()
     device = lax.broadcasted_iota(jnp.int32, (1, device_count), 1)
     busiest = jnp.max(jnp.where(sums[1:2] > 1.5, device.astype(F32), 0.0)).astype(jnp.int32)
     theirs = present_ref[pl.ds(busiest, 1), :]
@@ -97,10 +100,6 @@
     first = queries - 1 - jnp.max(theirs * (queries - 1 - lane_f)).astype(jnp.int32)
     middle = jnp.sum(theirs * lane_f).astype(jnp.int32) - first - last
     middle = jnp.clip(middle, 0, queries - 1)
-    pick = jnp.where(device == busiest, last, sums[0:1].astype(jnp.int32))
-    pick_vmem[...] = jnp.clip(pick, 0, queries - 1)
-    copy = pltpu.make_async_copy(pick_vmem, pick_smem, sem)
-    copy.start()
     busiest_ref[0] = busiest
     kind = lax.broadcasted_iota(jnp.int32, (8, device_count), 0)
     note_ref[...] = jnp.where(kind == 0, busiest, jnp.where(kind == 1, first, middle))
@@ -112,8 +111,16 @@
         query = first if seat < PLANE // 2 else middle
         start = (seat % (PLANE // 2)) * extra
         spare.append(tokens_ref[query, start : start + extra, :])
+
+    def pack_extra(step, carry):
+        for seat in range(PLANE):
+            packed_ref[step * PLANE + seat, tokens : tokens + extra, :] = spare[seat]
+        return carry
+
+    lax.fori_loop(0, device_count // PLANE, pack_extra, 0)
     copy.wait()
-    chunks = 4
+    pick_smem[0, busiest] = jnp.clip(last, 0, queries - 1)
+    chunks = 8
     size = device_count // chunks
     stores = []
     for chunk in range(chunks):
@@ -122,7 +129,6 @@
             for seat in range(PLANE):
                 device = chunk * size + step * PLANE + seat
                 packed_ref[device, 0:tokens, :] = tokens_ref[pick_smem[0, device]]
-                packed_ref[device, tokens : tokens + extra, :] = spare[seat]
             return carry
 
         lax.fori_loop(0, size // PLANE, pack, 0)
@@ -157,7 +163,7 @@
             pltpu.VMEM((queries, tokens, dim), BF16),
             pltpu.VMEM((device_count, tokens + 2 * tokens // PLANE, dim), BF16),
             pltpu.SemaphoreType.DMA(()),
-            pltpu.SemaphoreType.DMA((4,)),
+            pltpu.SemaphoreType.DMA((8,)),
         ],
         cost_estimate=cost(10**9, 2 * 10**6),
     )(

time: 136 us -> 136 us (level)
  no operation moved by 1% of the time
where the time goes in v6:
time: 136 us
  starting transfers between devices  54.6 us (40%)
  waiting for transfers between devices  27.3 us (20%)
  blocking collectives  26.3 us (19%)
  Pallas kernels  23.2 us (17%)
  between operations  2.02 us (1%)
  local copies, waits for them, and re-layouts  1.39 us (1%)
    all_to_all x1, starting transfers between devices, local(): arrived = lax.all_to_all(outgoing, 'shard', 0, 0, tiled=True)  31 us
    all_to_all x1, blocking collectives, local(): back = lax.all_to_all(visited, 'shard', 0, 0, tiled=True)  26.3 us
    ppermute x14, starting transfers between devices, turn(): return lax.ppermute(value, 'shard', pairs)  23.6 us
    ppermute x14, waiting for transfers between devices, turn(): return lax.ppermute(value, 'shard', pairs)  17.1 us
    pallas_call x1, Pallas kernels, score(): pl.pallas_call(score_kernel, name='score', compiler_params=pltpu.Compiler...  12.2 us
    all_to_all x1, waiting for transfers between devices, local(): arrived = lax.all_to_all(outgoing, 'shard', 0, 0, tiled=True)  10.2 us
    pallas_call x1, Pallas kernels, decode(): pl.pallas_call(decode_kernel, name='decode', out_shape=jax.ShapeDtypeStru...  6.32 us
    pallas_call x1, Pallas kernels, prepare(): pl.pallas_call(functools.partial(prepare_kernel, store_rows, device_count...  3.69 us
  transfers between devices with their start and end apart: 15, of which 8 were waited for; matrix products, arithmetic and copies ran while one was open for 2% of the time, Pallas kernels for 5%

profile of v6, /device:TPU:33, one launch (start us, length us, event | category | flops | bytes accessed | tf_op | source)
XLA Modules:
  0.0 135.7 jit_solution(17906402760325296638)
XLA Ops:
  0.0 3.7 %prepare.1 = (bf16[128,40,128]{2,1,0:T(8,128)(2,1)}, s32[6,128]{1,0:T(8,128)S(1)}, s32[6,128]{1,0:T(8,128)S(1)}, s32[6,128]{1,0:T(8,128)S(1)}, s32[8,128]{1,0:T(8,128)S(1)}, /*index=5*/s32[1]{0:T(128)}) custom-call(s32[24,32]{1,0:T(8,128)} %bitcast.43, s32[1,32]{1,0:T(1,128)} %bitcast.44, s32[32,128]{1,0:T(8,128)} %bitcast.42, bf16[32,32,128]{2,1,0:T(8,128)(2,1)} %query_ref.1), custom_call_target="tpu_custom_call" | custom-call | flops 1000000000 | bytes 2000000 | tf_op jit(solution)/shard_map/prepare/pallas_call | solution.py:147
  3.7 31.0 %all-to-all-start = ((bf16[128,40,128]{2,1,0:T(8,128)(2,1)}), bf16[128,40,128]{2,1,0:T(8,128)(2,1)S(1)}, u32[]{:S(2)}, u32[]{:S(2)}) async-start(bf16[128,40,128]{2,1,0:T(8,128)(2,1)} %get-tuple-element.15), calls=%async_computation | async-start | bytes 2621440 | tf_op jit(solution)/shard_map/all_to_all | solution.py:375
  34.7 6.3 %decode.1.store_ref = bf16[8,4,128,128]{3,2,1,0:T(8,128)(2,1)} custom-call(s32[1]{0:T(128)} %bitcast.3.seat_ref, s32[32]{0:T(128)} %length_ref.1, f32[4]{0:T(128)} %level_ref.1, bf16[32,128,128]{2,1,0:T(8,128)(2,1)} %base_ref.1, s32[32,128,128]{2,1,0:T(8,128)} %code_ref.1), custom_call_target="tpu_custom_call" | custom-call | flops 10485760 | bytes 4194304 | tf_op jit(solution)/shard_map/decode/pallas_call | solution.py:201
  41.0 1.4 %slice_bitcast_fusion.1 = (bf16[4,128,128]{2,1,0:T(8,128)(2,1)S(1)}, bf16[4,128,128]{2,1,0:T(8,128)(2,1)S(1)}, bf16[4,128,128]{2,1,0:T(8,128)(2,1)S(1)}, bf16[4,...) fusion(bf16[8,4,128,128]{3,2,1,0:T(8,128)(2,1)} %decode.1.store_ref), kind=kLoop, calls=%fused_computation.8 | loop fusion | bytes 1835008 | tf_op jit(solution)/shard_map/squeeze | solution.py:371
  42.4 2.6 %collective-permute-start = (bf16[4,128,128]{2,1,0:T(8,128)(2,1)S(1)}, bf16[4,128,128]{2,1,0:T(8,128)(2,1)S(1)}, u32[]{:S(2)}, u32[]{:S(2)}) collective-permute-start(bf16[4,128,128]{2,1,0:T(8,128)(2,1)S(1)} %get-tuple-element.23), channel_id=1, source_target_pairs={{0,7},{1,0},{2,1},{3,2},{4,3},{5,4},{6,5},{7,6},{8,15},{9,8},{10,9... | collective-permute-start | bytes 393224 | tf_op jit(solution)/shard_map/ppermute | solution.py:359
  45.1 0.4 collective-permute-start.1
  45.4 1.0 collective-permute-start.2
  46.5 2.4 %collective-permute-start.3 = (bf16[4,128,128]{2,1,0:T(8,128)(2,1)S(1)}, bf16[4,128,128]{2,1,0:T(8,128)(2,1)S(1)}, u32[]{:S(2)}, u32[]{:S(2)}) collective-permute-start(bf16[4,128,128]{2,1,0:T(8,128)(2,1)S(1)} %get-tuple-element.20), channel_id=1, source_target_pairs={{0,4},{1,5},{2,6},{3,7},{4,0},{5,1},{6,2},{7,3},{8,12},{9,13},{10,... | collective-permute-start | bytes 393224 | tf_op jit(solution)/shard_map/ppermute | solution.py:359
  48.9 0.7 collective-permute-start.4
  49.6 0.0 collective-permute-done
  49.6 1.1 collective-permute-start.5
  50.7 0.0 collective-permute-done.1
  50.7 3.8 %collective-permute-start.6 = (bf16[4,128,128]{2,1,0:T(8,128)(2,1)S(1)}, bf16[4,128,128]{2,1,0:T(8,128)(2,1)}, u32[]{:S(2)}, u32[]{:S(2)}) collective-permute-start(bf16[4,128,128]{2,1,0:T(8,128)(2,1)S(1)} %get-tuple-element.17), channel_id=1, source_target_pairs={{0,1},{1,2},{2,3},{3,4},{4,5},{5,6},{6,7},{7,0},{8,9},{9,10},{10,1... | collective-permute-start | bytes 393224 | tf_op jit(solution)/shard_map/ppermute | solution.py:359
  56.5 3.9 %collective-permute-done.2 = bf16[4,128,128]{2,1,0:T(8,128)(2,1)S(1)} collective-permute-done((bf16[4,128,128]{2,1,0:T(8,128)(2,1)S(1)}, bf16[4,128,128]{2,1,0:T(8,128)(2,1)S(1)}, u32[]{:S(2)}, u32[]{:S(2)}) %collective-permute-start.2) | collective-permute-done | bytes 131104 | tf_op jit(solution)/shard_map/ppermute | solution.py:359
  60.4 0.6 collective-permute-done.4
  60.9 0.3 collective-permute-done.5
  61.2 1.8 %collective-permute-done.6 = bf16[4,128,128]{2,1,0:T(8,128)(2,1)} collective-permute-done((bf16[4,128,128]{2,1,0:T(8,128)(2,1)S(1)}, bf16[4,128,128]{2,1,0:T(8,128)(2,1)}, u32[]{:S(2)}, u32[]{:S(2)}) %collective-permute-start.6) | collective-permute-done | bytes 131104 | tf_op jit(solution)/shard_map/ppermute | solution.py:359
  63.1 1.0 fusion.6.refs_0_
  64.0 4.0 %collective-permute-start.7 = (bf16[4,128,128]{2,1,0:T(8,128)(2,1)S(1)}, bf16[4,128,128]{2,1,0:T(8,128)(2,1)S(1)}, u32[]{:S(2)}, u32[]{:S(2)}) collective-permute-start(bf16[4,128,128]{2,1,0:T(8,128)(2,1)S(1)} %fusion.6.refs_0_), channel_id=1, source_target_pairs={{0,7},{1,0},{2,1},{3,2},{4,3},{5,4},{6,5},{7,6},{8,15},{9,8},{10,9... | collective-permute-start | bytes 393224 | tf_op jit(solution)/shard_map/ppermute | solution.py:359
  68.0 2.0 %collective-permute-start.8 = (bf16[4,128,128]{2,1,0:T(8,128)(2,1)S(1)}, bf16[4,128,128]{2,1,0:T(8,128)(2,1)S(1)}, u32[]{:S(2)}, u32[]{:S(2)}) collective-permute-start(bf16[4,128,128]{2,1,0:T(8,128)(2,1)S(1)} %fusion.6.refs_0_), channel_id=1, source_target_pairs={{0,6},{1,7},{2,0},{3,1},{4,2},{5,3},{6,4},{7,5},{8,14},{9,15},{10,... | collective-permute-start | bytes 393224 | tf_op jit(solution)/shard_map/ppermute | solution.py:359
  70.0 0.2 collective-permute-start.9
  70.2 1.4 %collective-permute-start.10 = (bf16[4,128,128]{2,1,0:T(8,128)(2,1)S(1)}, bf16[4,128,128]{2,1,0:T(8,128)(2,1)S(1)}, u32[]{:S(2)}, u32[]{:S(2)}) collective-permute-start(bf16[4,128,128]{2,1,0:T(8,128)(2,1)S(1)} %fusion.6.refs_0_), channel_id=1, source_target_pairs={{0,4},{1,5},{2,6},{3,7},{4,0},{5,1},{6,2},{7,3},{8,12},{9,13},{10,... | collective-permute-start | bytes 393224 | tf_op jit(solution)/shard_map/ppermute | solution.py:359
  71.6 2.0 %collective-permute-start.11 = (bf16[4,128,128]{2,1,0:T(8,128)(2,1)S(1)}, bf16[4,128,128]{2,1,0:T(8,128)(2,1)S(1)}, u32[]{:S(2)}, u32[]{:S(2)}) collective-permute-start(bf16[4,128,128]{2,1,0:T(8,128)(2,1)S(1)} %fusion.6.refs_0_), channel_id=1, source_target_pairs={{0,3},{1,4},{2,5},{3,6},{4,7},{5,0},{6,1},{7,2},{8,11},{9,12},{10,... | collective-permute-start | bytes 393224 | tf_op jit(solution)/shard_map/ppermute | solution.py:359
  73.6 0.6 collective-permute-start.12
  74.1 1.5 %collective-permute-start.13 = (bf16[4,128,128]{2,1,0:T(8,128)(2,1)S(1)}, bf16[4,128,128]{2,1,0:T(8,128)(2,1)S(1)}, u32[]{:S(2)}, u32[]{:S(2)}) collective-permute-start(bf16[4,128,128]{2,1,0:T(8,128)(2,1)S(1)} %fusion.6.refs_0_), channel_id=1, source_target_pairs={{0,1},{1,2},{2,3},{3,4},{4,5},{5,6},{6,7},{7,0},{8,9},{9,10},{10,1... | collective-permute-start | bytes 393224 | tf_op jit(solution)/shard_map/ppermute | solution.py:359
  75.6 8.4 %collective-permute-done.9.refs_3_ = bf16[4,128,128]{2,1,0:T(8,128)(2,1)S(1)} collective-permute-done((bf16[4,128,128]{2,1,0:T(8,128)(2,1)S(1)}, bf16[4,128,128]{2,1,0:T(8,128)(2,1)S(1)}, u32[]{:S(2)}, u32[]{:S(2)}) %collective-permute-start.9) | collective-permute-done | bytes 131104 | tf_op jit(solution)/shard_map/ppermute | solution.py:359
  84.0 1.8 %collective-permute-done.11.refs_5_ = bf16[4,128,128]{2,1,0:T(8,128)(2,1)S(1)} collective-permute-done((bf16[4,128,128]{2,1,0:T(8,128)(2,1)S(1)}, bf16[4,128,128]{2,1,0:T(8,128)(2,1)S(1)}, u32[]{:S(2)}, u32[]{:S(2)}) %collective-permute-start.11) | collective-permute-done | bytes 131104 | tf_op jit(solution)/shard_map/ppermute | solution.py:359
  85.8 0.3 collective-permute-done.12.refs_6_
  86.1 10.2 %all-to-all-done.arrived_ref = bf16[128,40,128]{2,1,0:T(8,128)(2,1)S(1)} async-done(((bf16[128,40,128]{2,1,0:T(8,128)(2,1)}), bf16[128,40,128]{2,1,0:T(8,128)(2,1)S(1)}, u32[]{:S(2)}, u32[]{:S(2)}) %all-to-all-start) | async-done | bytes 1310752 | tf_op jit(solution)/shard_map/all_to_all | solution.py:375
  96.3 12.2 %score.1 = f32[128,64]{1,0:T(8,128)S(1)} custom-call(bf16[128,40,128]{2,1,0:T(8,128)(2,1)S(1)} %all-to-all-done.arrived_ref, bf16[8,4,128,128]{3,2,1,0:T(8,128)(2,1)S(1)} %copy-done, bf16[4,128,128]{2,1,0:T(8,128)(2,1)S(1)} %fusion.6.refs_0_, bf16[4,128,128]{2,1,0:T(8,128)(2,1)S(1)} %collective-permute-done.7.refs_1_, ...), custom_call_target="tpu_custom_call" | custom-call | flops 5368709120 | bytes 3407872 | tf_op jit(solution)/shard_map/score/pallas_call | solution.py:278
  108.5 26.3 %all_to_all.16 = f32[128,1,64]{2,1,0:T(1,128)S(1)} all-to-all(f32[128,1,64]{2,1,0:T(1,128)S(1)} %bitcast.41), channel_id=1, replica_groups=mesh['groups'=2,'shard'=128] {'shard'}, dimensions={0} | all-to-all | bytes 65536 | tf_op jit(solution)/shard_map/all_to_all | solution.py:382
  134.7 1.0 finish.1
  (7 shorter events, 0.0 us)
Async XLA Ops:
  3.7 92.6 %all-to-all-start = ((bf16[128,40,128]{2,1,0:T(8,128)(2,1)}), bf16[128,40,128]{2,1,0:T(8,128)(2,1)S(1)}, u32[]{:S(2)}, u32[]{:S(2)}) async-start(bf16[128,40,128]{2,1,0:T(8,128)(2,1)} %get-tuple-element.15), calls=%async_computation | async-start | bytes 2621440 | tf_op jit(solution)/shard_map/all_to_all | solution.py:375
  41.0 22.0 %copy-start = (bf16[8,4,128,128]{3,2,1,0:T(8,128)(2,1)S(1)}, bf16[8,4,128,128]{3,2,1,0:T(8,128)(2,1)}, u32[]{:S(2)}) copy-start(bf16[8,4,128,128]{3,2,1,0:T(8,128)(2,1)} %decode.1.store_ref) | copy-start | bytes 3145732
  42.4 7.1 %collective-permute-start = (bf16[4,128,128]{2,1,0:T(8,128)(2,1)S(1)}, bf16[4,128,128]{2,1,0:T(8,128)(2,1)S(1)}, u32[]{:S(2)}, u32[]{:S(2)}) collective-permute-start(bf16[4,128,128]{2,1,0:T(8,128)(2,1)S(1)} %get-tuple-element.23), channel_id=1, source_target_pairs={{0,7},{1,0},{2,1},{3,2},{4,3},{5,4},{6,5},{7,6},{8,15},{9,8},{10,9... | collective-permute-start | bytes 393224 | tf_op jit(solution)/shard_map/ppermute | solution.py:359
  45.1 5.6 %collective-permute-start.1 = (bf16[4,128,128]{2,1,0:T(8,128)(2,1)S(1)}, bf16[4,128,128]{2,1,0:T(8,128)(2,1)S(1)}, u32[]{:S(2)}, u32[]{:S(2)}) collective-permute-start(bf16[4,128,128]{2,1,0:T(8,128)(2,1)S(1)} %get-tuple-element.22), channel_id=1, source_target_pairs={{0,6},{1,7},{2,0},{3,1},{4,2},{5,3},{6,4},{7,5},{8,14},{9,15},{10,... | collective-permute-start | bytes 393224 | tf_op jit(solution)/shard_map/ppermute | solution.py:359
  45.4 14.9 %collective-permute-start.2 = (bf16[4,128,128]{2,1,0:T(8,128)(2,1)S(1)}, bf16[4,128,128]{2,1,0:T(8,128)(2,1)S(1)}, u32[]{:S(2)}, u32[]{:S(2)}) collective-permute-start(bf16[4,128,128]{2,1,0:T(8,128)(2,1)S(1)} %get-tuple-element.21), channel_id=1, source_target_pairs={{0,5},{1,6},{2,7},{3,0},{4,1},{5,2},{6,3},{7,4},{8,13},{9,14},{10,... | collective-permute-start | bytes 393224 | tf_op jit(solution)/shard_map/ppermute | solution.py:359
  46.5 13.9 %collective-permute-start.3 = (bf16[4,128,128]{2,1,0:T(8,128)(2,1)S(1)}, bf16[4,128,128]{2,1,0:T(8,128)(2,1)S(1)}, u32[]{:S(2)}, u32[]{:S(2)}) collective-permute-start(bf16[4,128,128]{2,1,0:T(8,128)(2,1)S(1)} %get-tuple-element.20), channel_id=1, source_target_pairs={{0,4},{1,5},{2,6},{3,7},{4,0},{5,1},{6,2},{7,3},{8,12},{9,13},{10,... | collective-permute-start | bytes 393224 | tf_op jit(solution)/shard_map/ppermute | solution.py:359
  48.9 12.1 %collective-permute-start.4 = (bf16[4,128,128]{2,1,0:T(8,128)(2,1)S(1)}, bf16[4,128,128]{2,1,0:T(8,128)(2,1)}, u32[]{:S(2)}, u32[]{:S(2)}) collective-permute-start(bf16[4,128,128]{2,1,0:T(8,128)(2,1)S(1)} %get-tuple-element.19), channel_id=1, source_target_pairs={{0,3},{1,4},{2,5},{3,6},{4,7},{5,0},{6,1},{7,2},{8,11},{9,12},{10,... | collective-permute-start | bytes 393224 | tf_op jit(solution)/shard_map/ppermute | solution.py:359
  49.6 11.7 %collective-permute-start.5 = (bf16[4,128,128]{2,1,0:T(8,128)(2,1)S(1)}, bf16[4,128,128]{2,1,0:T(8,128)(2,1)}, u32[]{:S(2)}, u32[]{:S(2)}) collective-permute-start(bf16[4,128,128]{2,1,0:T(8,128)(2,1)S(1)} %get-tuple-element.18), channel_id=1, source_target_pairs={{0,2},{1,3},{2,4},{3,5},{4,6},{5,7},{6,0},{7,1},{8,10},{9,11},{10,... | collective-permute-start | bytes 393224 | tf_op jit(solution)/shard_map/ppermute | solution.py:359
  50.7 12.3 %collective-permute-start.6 = (bf16[4,128,128]{2,1,0:T(8,128)(2,1)S(1)}, bf16[4,128,128]{2,1,0:T(8,128)(2,1)}, u32[]{:S(2)}, u32[]{:S(2)}) collective-permute-start(bf16[4,128,128]{2,1,0:T(8,128)(2,1)S(1)} %get-tuple-element.17), channel_id=1, source_target_pairs={{0,1},{1,2},{2,3},{3,4},{4,5},{5,6},{6,7},{7,0},{8,9},{9,10},{10,1... | collective-permute-start | bytes 393224 | tf_op jit(solution)/shard_map/ppermute | solution.py:359
  64.0 9.5 %collective-permute-start.7 = (bf16[4,128,128]{2,1,0:T(8,128)(2,1)S(1)}, bf16[4,128,128]{2,1,0:T(8,128)(2,1)S(1)}, u32[]{:S(2)}, u32[]{:S(2)}) collective-permute-start(bf16[4,128,128]{2,1,0:T(8,128)(2,1)S(1)} %fusion.6.refs_0_), channel_id=1, source_target_pairs={{0,7},{1,0},{2,1},{3,2},{4,3},{5,4},{6,5},{7,6},{8,15},{9,8},{10,9... | collective-permute-start | bytes 393224 | tf_op jit(solution)/shard_map/ppermute | solution.py:359
  68.0 6.1 %collective-permute-start.8 = (bf16[4,128,128]{2,1,0:T(8,128)(2,1)S(1)}, bf16[4,128,128]{2,1,0:T(8,128)(2,1)S(1)}, u32[]{:S(2)}, u32[]{:S(2)}) collective-permute-start(bf16[4,128,128]{2,1,0:T(8,128)(2,1)S(1)} %fusion.6.refs_0_), channel_id=1, source_target_pairs={{0,6},{1,7},{2,0},{3,1},{4,2},{5,3},{6,4},{7,5},{8,14},{9,15},{10,... | collective-permute-start | bytes 393224 | tf_op jit(solution)/shard_map/ppermute | solution.py:359
  70.0 14.0 %collective-permute-start.9 = (bf16[4,128,128]{2,1,0:T(8,128)(2,1)S(1)}, bf16[4,128,128]{2,1,0:T(8,128)(2,1)S(1)}, u32[]{:S(2)}, u32[]{:S(2)}) collective-permute-start(bf16[4,128,128]{2,1,0:T(8,128)(2,1)S(1)} %fusion.6.refs_0_), channel_id=1, source_target_pairs={{0,5},{1,6},{2,7},{3,0},{4,1},{5,2},{6,3},{7,4},{8,13},{9,14},{10,... | collective-permute-start | bytes 393224 | tf_op jit(solution)/shard_map/ppermute | solution.py:359
  70.2 13.8 %collective-permute-start.10 = (bf16[4,128,128]{2,1,0:T(8,128)(2,1)S(1)}, bf16[4,128,128]{2,1,0:T(8,128)(2,1)S(1)}, u32[]{:S(2)}, u32[]{:S(2)}) collective-permute-start(bf16[4,128,128]{2,1,0:T(8,128)(2,1)S(1)} %fusion.6.refs_0_), channel_id=1, source_target_pairs={{0,4},{1,5},{2,6},{3,7},{4,0},{5,1},{6,2},{7,3},{8,12},{9,13},{10,... | collective-permute-start | bytes 393224 | tf_op jit(solution)/shard_map/ppermute | solution.py:359
  71.6 14.3 %collective-permute-start.11 = (bf16[4,128,128]{2,1,0:T(8,128)(2,1)S(1)}, bf16[4,128,128]{2,1,0:T(8,128)(2,1)S(1)}, u32[]{:S(2)}, u32[]{:S(2)}) collective-permute-start(bf16[4,128,128]{2,1,0:T(8,128)(2,1)S(1)} %fusion.6.refs_0_), channel_id=1, source_target_pairs={{0,3},{1,4},{2,5},{3,6},{4,7},{5,0},{6,1},{7,2},{8,11},{9,12},{10,... | collective-permute-start | bytes 393224 | tf_op jit(solution)/shard_map/ppermute | solution.py:359
  73.6 12.5 %collective-permute-start.12 = (bf16[4,128,128]{2,1,0:T(8,128)(2,1)S(1)}, bf16[4,128,128]{2,1,0:T(8,128)(2,1)S(1)}, u32[]{:S(2)}, u32[]{:S(2)}) collective-permute-start(bf16[4,128,128]{2,1,0:T(8,128)(2,1)S(1)} %fusion.6.refs_0_), channel_id=1, source_target_pairs={{0,2},{1,3},{2,4},{3,5},{4,6},{5,7},{6,0},{7,1},{8,10},{9,11},{10,... | collective-permute-start | bytes 393224 | tf_op jit(solution)/shard_map/ppermute | solution.py:359
  74.1 12.0 %collective-permute-start.13 = (bf16[4,128,128]{2,1,0:T(8,128)(2,1)S(1)}, bf16[4,128,128]{2,1,0:T(8,128)(2,1)S(1)}, u32[]{:S(2)}, u32[]{:S(2)}) collective-permute-start(bf16[4,128,128]{2,1,0:T(8,128)(2,1)S(1)} %fusion.6.refs_0_), channel_id=1, source_target_pairs={{0,1},{1,2},{2,3},{3,4},{4,5},{5,6},{6,7},{7,0},{8,9},{9,10},{10,1... | collective-permute-start | bytes 393224 | tf_op jit(solution)/shard_map/ppermute | solution.py:359
